TPU v7x, 32 devices: a whole 2x2x4 slice. The times are simulated.
32 devices in a mesh: seq: 8 (over y, x, core), head: 4 (over z).
Axes of the slice: x: 2, y: 2, z: 4, core: 2. Of those that a mesh axis runs over, the one named last changes fastest.
Arguments:
- lat_query: bfloat16 [1024, 73728], P('seq', 'head'), may hold values from -6 to 6
- lat_keys: bfloat16 [1024, 576], P('seq'), may hold values from -6 to 6
- normalizer: float32 [1024, 128], P('seq'), may hold values from 3 to 7
- lookback: int32 [1024], P('seq'), may hold values from 1 to 1024
- index_query: bfloat16 [1024, 8192], P(('seq', 'head')), may hold values from -20 to 20
- index_keys: bfloat16 [1024, 128], P('seq'), may hold values from -6 to 6
- index_weight: float32 [1024, 64], P(('seq', 'head')), may hold values from 0.25 to 2
Outputs:
- grad_query: float32 [1024, 8192], P(('seq', 'head'))
- grad_weight: float32 [1024, 64], P(('seq', 'head'))
- grad_key: float32 [1024, 128], P(('seq', 'head'))
All inputs are finite; a program needn't handle non-finite values.
Results may differ from a plain program's by a relative error of at most 0.0029.
Values may be sent and summed in bfloat16 or wider, within the bound.
No kernel may reach another device: no remote copies, remote signals or barrier semaphores. Data moves between devices by JAX's collectives and lax.ppermute only.
A program may use at most 64 MiB of HBM per device.

v0:
```python
import functools
import math

import jax
import jax.numpy as jnp
from jax import lax
from jax.experimental import pallas as pl
from jax.experimental.pallas import tpu as pltpu
from jax.sharding import PartitionSpec as P


KDIM = 576
LANES = 128
WIDE = 2 * LANES
PAD = LANES - KDIM % LANES
LOG2E = 1.0 / math.log(2.0)
HBM = pl.BlockSpec(memory_space=pltpu.HBM)
VMEM = pl.BlockSpec(memory_space=pltpu.VMEM)


def shape_of(dims, kind):
    return jax.ShapeDtypeStruct(dims, kind)


def call(body, out_shape, args, specs=None, scratch=(), flops=0, limit=20):
    return pl.pallas_call(
        body,
        out_shape=out_shape,
        in_specs=specs or [VMEM] * len(args),
        out_specs=jax.tree.map(lambda _: VMEM, out_shape),
        scratch_shapes=list(scratch),
        compiler_params=pltpu.CompilerParams(vmem_limit_bytes=limit << 20),
        cost_estimate=pl.CostEstimate(flops=flops, bytes_accessed=0, transcendentals=0),
    )(*args)


def lanes_of(place):
    return slice(place * LANES, (place + 1) * LANES)


def spread_kernel(factor, query_hbm, norm_hbm, weight_hbm, look_hbm, *refs):
    query_ref, off_ref, scale_ref, low_ref, norm, weight, look, tall, sems = refs
    pairs = ((norm_hbm, norm), (weight_hbm, weight), (look_hbm, look), (query_hbm, query_ref))
    copies = [pltpu.make_async_copy(*pair, sems.at[place]) for place, pair in enumerate(pairs)]
    for copy in copies:
        copy.start()
    heads, local_rows, _ = off_ref.shape
    rows = low_ref.shape[0]
    me = lax.axis_index("head")
    copies[0].wait()
    width = norm.shape[1]
    offsets = pltpu.roll(norm[...] * LOG2E, lax.rem(width - me * heads, width), 1)
    for head in range(heads):
        off_ref[head] = jnp.broadcast_to(offsets[:, head : head + 1], (local_rows, LANES))
    copies[1].wait()
    weights = weight[...] * factor
    for head in range(scale_ref.shape[0]):
        scale_ref[head] = jnp.broadcast_to(weights[:, head : head + 1], (rows, LANES))
    copies[2].wait()
    tall[...] = jnp.transpose(
        jnp.broadcast_to(look[...].astype(jnp.float32), (LANES, local_rows))
    )
    low_ref[...] = tall[pl.ds(me * rows, rows), :]
    copies[3].wait()


def spread(lat_query, normalizer, weight, lookback, heads, factor):
    rows, index_heads = weight.shape
    local_rows = normalizer.shape[0]
    look = lookback.reshape(1, local_rows)
    out = (
        shape_of(lat_query.shape, lat_query.dtype),
        shape_of((heads, local_rows, LANES), jnp.float32),
        shape_of((index_heads, rows, LANES), jnp.float32),
        shape_of((rows, LANES), jnp.float32),
    )
    scratch = [pltpu.VMEM(value.shape, value.dtype) for value in (normalizer, weight, look)]
    scratch += [pltpu.VMEM((local_rows, LANES), jnp.float32), pltpu.SemaphoreType.DMA((4,))]
    return call(
        functools.partial(spread_kernel, factor),
        out,
        tuple(pltpu.with_memory_space_constraint(value, pltpu.HBM) for value in (lat_query, normalizer, weight, look)),
        specs=[HBM] * 4,
        scratch=scratch,
        flops=1_500_000_000,
    )


def mass_kernel(slots, carried, places, query_ref, off_ref, *refs):
    blocks, refs = refs[:slots], refs[slots:]
    prior, refs = refs[:carried], refs[carried:]
    outs, (keys, acc) = refs[:-2], refs[-2:]
    tiles, local_rows, wide = acc.shape
    heads = off_ref.shape[0]
    group = min(16, heads)
    depth = KDIM + PAD
    per_tile = wide // LANES
    for tile in range(tiles):
        keys[tile, :PAD] = jnp.zeros((PAD, wide), keys.dtype)
        keys[tile, PAD + KDIM :] = jnp.zeros((PAD, wide), keys.dtype)
        for part in range(per_tile):
            keys[tile, PAD : PAD + KDIM, lanes_of(part)] = blocks[tile * per_tile + part][:KDIM]
    acc[...] = jnp.zeros_like(acc)
    scale = KDIM ** (-0.5) * LOG2E

    @pl.loop(0, heads // group)
    def _(step):
        @pl.loop(0, tiles)
        def _(tile):
            total = acc[tile]
            for odd in range(2):
                picked = []
                for head in range(odd, group, 2):
                    begin = step * (group * KDIM) + (head * KDIM - (PAD if odd else 0))
                    picked.append(query_ref[:, pl.ds(pl.multiple_of(begin, LANES), depth)])
                first = 0 if odd else PAD
                scores = jnp.dot(
                    jnp.concatenate(picked, axis=0),
                    keys[tile, first : first + depth],
                    preferred_element_type=jnp.float32,
                )
                for place, head in enumerate(range(odd, group, 2)):
                    offset = jnp.concatenate([off_ref[step * group + head]] * per_tile, axis=1)
                    part = scores[place * local_rows : (place + 1) * local_rows]
                    total = total + jnp.exp2(part * scale - offset)
            acc[tile] = total

    if not places:
        outs[0][...] = acc[...]
        return
    own, sends = outs[0], outs[1:]
    rows = own.shape[0]
    size = len(sends) + 1
    me = lax.axis_index("head")
    sources = [(ref, tile) for ref in (*prior, acc) for tile in range(ref.shape[0])]
    pieces = [(ref, tile, part) for ref, tile in sources for part in range(per_tile)]
    for place, (ref, tile, part) in zip(places, pieces):
        lanes = lanes_of(part)
        own[:, lanes_of(place)] = ref[tile, pl.ds(me * rows, rows), lanes]
        for hop, send in enumerate(sends):
            there = lax.rem(me + hop + 1, size)
            send[:, lanes_of(place)] = ref[tile, pl.ds(there * rows, rows), lanes].astype(send.dtype)


def attention_mass(query, offsets, blocks, prior, places, rows, peers):
    local_rows = query.shape[0]
    heads = offsets.shape[0]
    slots = len(blocks)
    tiles = slots * LANES // WIDE
    if places:
        columns = len(places) * LANES
        out = (shape_of((rows, columns), jnp.float32),)
        out += (shape_of((rows, columns), jnp.bfloat16),) * (peers - 1)
    else:
        out = shape_of((tiles, local_rows, WIDE), jnp.float32)
    return call(
        functools.partial(mass_kernel, slots, len(prior), places),
        out,
        (query, offsets, *blocks, *prior),
        scratch=[
            pltpu.VMEM((tiles, KDIM + 2 * PAD, WIDE), jnp.bfloat16),
            pltpu.VMEM((tiles, local_rows, WIDE), jnp.float32),
        ],
        flops=2 * local_rows * heads * KDIM * slots * LANES,
    )


def stack_heads(value, heads, dims):
    parts = [value[:, head * dims : (head + 1) * dims] for head in range(heads)]
    if value.shape[0] % 16 == 0:
        return jnp.concatenate(parts, axis=0)
    parts = [part.astype(jnp.float32) for part in parts]
    return jnp.concatenate(parts, axis=0).astype(value.dtype)


def score_kernel(order, query_ref, scale_ref, low_ref, *refs):
    slots = len(order)
    blocks = refs[:slots]
    active_ref, predicted_ref, keys, score = refs[slots:]
    index_heads, rows, seq_total = active_ref.shape
    dims = keys.shape[1]
    group = min(8, index_heads)
    score[...] = jnp.zeros_like(score)
    for place in range(slots):
        keys[lanes_of(place)] = blocks[place][KDIM:]

    @pl.loop(0, index_heads // group)
    def _(step):
        begin = pl.multiple_of(step * (group * dims), LANES)
        stacked = stack_heads(query_ref[:, pl.ds(begin, group * dims)], group, dims)
        for begin in range(0, seq_total, WIDE):
            inner = lax.dot_general(
                stacked,
                keys[begin : begin + WIDE],
                (((1,), (1,)), ((), ())),
                preferred_element_type=jnp.float32,
            )
            total = score[:, begin : begin + WIDE]
            for head in range(group):
                active = jnp.maximum(inner[head * rows : (head + 1) * rows], 0.0)
                active_ref[step * group + head, :, begin : begin + WIDE] = active
                total = total + active * jnp.concatenate([scale_ref[step * group + head]] * 2, axis=1)
            score[:, begin : begin + WIDE] = total

    seq = lax.axis_index("seq")
    query_pos = (
        seq * lax.axis_size("head") + lax.axis_index("head")
    ) * rows + lax.broadcasted_iota(jnp.int32, (rows, LANES), 0)
    low = query_pos - low_ref[...].astype(jnp.int32)
    lane = lax.broadcasted_iota(jnp.int32, (rows, LANES), 1)
    seen = []
    for slot in order:
        key_pos = jnp.bitwise_xor(seq, slot) * LANES + lane
        seen.append((key_pos <= query_pos) & (key_pos >= low))
    parts = [score[:, lanes_of(place)] for place in range(slots)]
    parts = [jnp.where(see, part, -jnp.inf) for see, part in zip(seen, parts)]
    top = jnp.max(functools.reduce(jnp.maximum, parts), axis=1, keepdims=True)
    parts = [jnp.exp(part - top) for part in parts]
    mass = jnp.sum(functools.reduce(jnp.add, parts), axis=1, keepdims=True)
    for place in range(slots):
        predicted_ref[:, lanes_of(place)] = jnp.where(seen[place], parts[place] / mass, -1.0)


def index_scores(index_query, scales, lows, blocks, order, dims):
    rows = index_query.shape[0]
    index_heads = scales.shape[0]
    seq_total = len(order) * LANES
    return call(
        functools.partial(score_kernel, order),
        (
            shape_of((index_heads, rows, seq_total), jnp.float32),
            shape_of((rows, seq_total), jnp.float32),
            shape_of((seq_total, dims), jnp.bfloat16),
        ),
        (index_query, scales, lows, *blocks),
        scratch=[pltpu.VMEM((rows, seq_total), jnp.float32)],
        flops=6 * rows * index_heads * seq_total * dims,
    )


def gap_of(shares, predicted):
    mine, *others = shares
    mass = mine[...]
    for other in others:
        mass = mass + other[...].astype(jnp.float32)
    seen = predicted >= 0.0
    mass = jnp.where(seen, mass, 0.0)
    target = mass / jnp.sum(mass, axis=1, keepdims=True)
    return jnp.where(seen, predicted - target, 0.0)


def key_kernel(peers, half, *refs):
    shares, refs = refs[:peers], refs[peers:]
    if peers:
        predicted_ref, active_ref, scale_ref, query_ref, gap_ref, slopes_ref, out_ref, tall = refs
        gap_ref[...] = gap_of(shares, predicted_ref[...])
    else:
        gap_ref, active_ref, scale_ref, query_ref, slopes_ref, out_ref, tall = refs
    index_heads, rows, _ = active_ref.shape
    dims, columns = tall.shape
    lanes = slice(half * columns, (half + 1) * columns)
    group = min(8, index_heads)
    tall[...] = jnp.zeros_like(tall)

    @pl.loop(0, index_heads // group)
    def _(step):
        gap = gap_ref[:, lanes]
        slopes = []
        for head in range(group):
            place = step * group + head
            scaled = gap * jnp.concatenate([scale_ref[place]] * (columns // LANES), axis=1)
            slope = jnp.where(active_ref[place, :, lanes] > 0.0, scaled, 0.0)
            slopes.append(slope if rows % 16 else slope.astype(jnp.bfloat16))
        slopes = jnp.concatenate(slopes, axis=0).astype(jnp.bfloat16)
        block = pl.ds(pl.multiple_of(step * (group * rows), group * rows), group * rows)
        slopes_ref[block, :] = slopes
        begin = pl.multiple_of(step * (group * dims), LANES)
        stacked = stack_heads(query_ref[:, pl.ds(begin, group * dims)], group, dims)
        tall[...] += lax.dot_general(
            stacked, slopes, (((0,), (0,)), ((), ())), preferred_element_type=jnp.float32
        )

    for place in range(columns // LANES):
        out_ref[lanes_of(place)] = jnp.transpose(tall[:, lanes_of(place)])


def key_terms(shares, gap, predicted, active, scales, index_query, dims, half):
    index_heads, rows, seq_total = active.shape
    columns = seq_total // 2
    out = (
        shape_of((index_heads * rows, columns), jnp.bfloat16),
        shape_of((columns, dims), jnp.float32),
    )
    if shares:
        out = (shape_of((rows, seq_total), jnp.float32), *out)
        args = (*shares, predicted)
    else:
        args = (gap,)
    return call(
        functools.partial(key_kernel, len(shares), half),
        out,
        (*args, active, scales, index_query),
        scratch=[pltpu.VMEM((dims, columns), jnp.float32)],
        flops=4 * rows * index_heads * seq_total * dims,
    )


def query_kernel(factor, gap_ref, even_ref, odd_ref, active_ref, keys_ref, grad_query_ref, grad_weight_ref, sums):
    index_heads, rows, seq_total = active_ref.shape
    dims = keys_ref.shape[1]
    group = min(8, index_heads)
    lane = lax.broadcasted_iota(jnp.int32, (rows, LANES), 1)
    sums[...] = jnp.zeros_like(sums)

    @pl.loop(0, index_heads // group)
    def _(step):
        gap = gap_ref[...]
        total = sums[...]
        for head in range(group):
            product = active_ref[step * group + head] * gap
            partial = functools.reduce(
                jnp.add, [product[:, lanes_of(place)] for place in range(seq_total // LANES)]
            )
            partial = jnp.sum(partial, axis=1, keepdims=True)
            total = jnp.where(lane == step * group + head, partial, total)
        sums[...] = total
        block = pl.ds(pl.multiple_of(step * (group * rows), group * rows), group * rows)
        slopes = jnp.concatenate([even_ref[block, :], odd_ref[block, :]], axis=1)
        grad = jnp.dot(slopes, keys_ref[...], preferred_element_type=jnp.float32)
        for head in range(group):
            begin = pl.multiple_of((step * group + head) * dims, dims)
            grad_query_ref[:, pl.ds(begin, dims)] = grad[head * rows : (head + 1) * rows]

    grad_weight_ref[...] = sums[:, :index_heads] * factor


def query_grads(gap, even, odd, active, keys, factor):
    index_heads, rows, seq_total = active.shape
    dims = keys.shape[1]
    return call(
        functools.partial(query_kernel, factor),
        (
            shape_of((rows, index_heads * dims), jnp.float32),
            shape_of((rows, index_heads), jnp.float32),
        ),
        (gap, even, odd, active, keys),
        scratch=[pltpu.VMEM((rows, LANES), jnp.float32)],
        flops=6 * rows * index_heads * seq_total * dims,
    )


def fold_kernel(keep_ref, come_ref, own_ref, *sends):
    total = keep_ref[...] + come_ref[...]
    rows = own_ref.shape[0]
    own_ref[...] = total[:rows]
    for hop, send in enumerate(sends):
        send[...] = total[(hop + 1) * rows : (hop + 2) * rows].astype(send.dtype)


def fold(keep, come, block):
    count = keep.shape[0] // block
    piece = (block, keep.shape[1])
    out = (shape_of(piece, jnp.float32),) + (shape_of(piece, jnp.bfloat16),) * (count - 1)
    return call(fold_kernel, out, (keep, come), flops=10_000_000)


def per_device(lat_query, lat_keys, normalizer, lookback, index_query, index_keys, index_weight):
    seq_count = lax.axis_size("seq")
    peers = lax.axis_size("head")
    heads = lat_query.shape[1] // KDIM
    rows, _ = index_weight.shape
    dims = index_keys.shape[1]
    factor = dims ** (-0.5)

    def swap(value, bits):
        return lax.ppermute(value, "seq", [(place, place ^ bits) for place in range(seq_count)])

    def pass_on(values):
        out = []
        for hop, value in enumerate(values):
            to = [(place, (place + hop + 1) % peers) for place in range(peers)]
            out.append(lax.ppermute(value, "head", to))
        return out

    mine = jnp.concatenate([lat_keys.T, index_keys], axis=0)
    blocks = {0: mine}
    for bits in range(2, seq_count, 2):
        blocks[bits] = swap(mine, bits)
    for bits in range(0, seq_count, 2):
        blocks[bits + 1] = swap(blocks[bits], 1)
    phases = [[0, 1], [2, 4], [3, 5], list(range(6, seq_count))]
    order = [*range(0, seq_count, 2), *range(1, seq_count, 2)]

    query, offsets, scales, lows = spread(
        lat_query, normalizer, index_weight, lookback, heads, factor
    )
    prior = []
    for phase in phases:
        last = phase is phases[-1]
        mass = attention_mass(
            query,
            offsets,
            [blocks[slot] for slot in phase],
            prior if last else [],
            [order.index(slot) for slots in phases for slot in slots] if last else [],
            rows,
            peers,
        )
        prior.append(mass)
    own, *sends = mass
    shares = [own, *pass_on(sends)]
    active, predicted, keys = index_scores(
        index_query, scales, lows, [blocks[slot] for slot in order], order, dims
    )
    terms = functools.partial(
        key_terms, active=active, scales=scales, index_query=index_query, dims=dims
    )
    gap, odd, give = terms(shares, None, predicted, half=1)
    come = swap(give, 1)
    even, keep = terms([], gap, None, half=0)
    own, *sends = fold(keep, come, LANES)
    others = [swap(send, 2 * (hop + 1)) for hop, send in enumerate(sends)]
    grad_query, grad_weight = query_grads(gap, even, odd, active, keys, factor)
    own, *sends = gather_terms(own, others, rows, peers)
    others = pass_on(sends)
    grad_key = functools.reduce(jnp.add, others, own)
    return grad_query, grad_weight, grad_key


def gather_kernel(peers, own_ref, *refs):
    others, (mine_ref, *sends), total = refs[: len(refs) - peers - 1], refs[-peers - 1 : -1], refs[-1]
    value = own_ref[...]
    for other in others:
        value = value + other[...].astype(jnp.float32)
    total[...] = value
    rows = mine_ref.shape[0]
    me = lax.axis_index("head")
    mine_ref[...] = total[pl.ds(me * rows, rows), :]
    for hop, send in enumerate(sends):
        send[...] = total[pl.ds(lax.rem(me + hop + 1, peers) * rows, rows), :]


def gather_terms(own, others, rows, peers):
    piece = shape_of((rows, own.shape[1]), jnp.float32)
    return call(
        functools.partial(gather_kernel, peers),
        (piece,) * peers,
        (own, *others),
        scratch=[pltpu.VMEM(own.shape, jnp.float32)],
        flops=10_000_000,
    )


def solution(mesh):
    return jax.shard_map(
        per_device,
        mesh=mesh,
        in_specs=(
            P("seq", "head"),
            P("seq", None),
            P("seq", None),
            P("seq"),
            P(("seq", "head"), None),
            P("seq", None),
            P(("seq", "head"), None),
        ),
        out_specs=(P(("seq", "head"), None), P(("seq", "head"), None), P(("seq", "head"), None)),
        check_vma=False,
    )
```

profile of v0, /device:TPU:0, one launch (start us, length us, event | category | flops | bytes accessed | tf_op | source)
XLA Modules:
  0.0 52.8 jit_solution(9894239059655561684)
XLA Ops:
  0.6 0.9 %pad_maximum_fusion.refs_0_ = bf16[704,128]{1,0:T(8,128)(2,1)S(1)} fusion(bf16[128,128]{1,0:T(8,128)(2,1)} %param.12, bf16[576,128]{1,0:T(8,128)(2,1)} %bitcast.2), kind=kLoop, calls=%fused_computation | loop fusion | flops 360448 | bytes 360448 | tf_op jit(solution)/shard_map/concatenate | solution.py:385
  1.6 3.1 %collective-permute-start.4 = (bf16[704,128]{1,0:T(8,128)(2,1)S(1)}, bf16[704,128]{1,0:T(8,128)(2,1)S(1)}, u32[]{:S(2)}, u32[]{:S(2)}) collective-permute-start(bf16[704,128]{1,0:T(8,128)(2,1)S(1)} %pad_maximum_fusion.refs_0_), channel_id=1, source_target_pairs={{0,16},{4,20},{8,24},{12,28},{16,0},{20,4},{24,8},{28,12},{1,17},{... | collective-permute-start | bytes 540680 | tf_op jit(solution)/shard_map/ppermute | solution.py:376
  4.6 1.5 %collective-permute-start.3 = (bf16[704,128]{1,0:T(8,128)(2,1)S(1)}, bf16[704,128]{1,0:T(8,128)(2,1)S(1)}, u32[]{:S(2)}, u32[]{:S(2)}) collective-permute-start(bf16[704,128]{1,0:T(8,128)(2,1)S(1)} %pad_maximum_fusion.refs_0_), channel_id=1, source_target_pairs={{0,8},{4,12},{8,0},{12,4},{16,24},{20,28},{24,16},{28,20},{1,9},{5... | collective-permute-start | bytes 540680 | tf_op jit(solution)/shard_map/ppermute | solution.py:376
  6.1 0.0 collective-permute-start
  6.2 0.0 collective-permute-start.2
  6.2 2.4 %shard_map.94 = (bf16[128,18432]{1,0:T(8,128)(2,1)S(1)}, f32[32,128,128]{2,1,0:T(8,128)S(1)}, f32[64,32,128]{2,1,0:T(8,128)S(1)}, f32[32,128]{1,0:T(8,128)S(1)}) custom-call(bf16[128,18432]{1,0:T(8,128)(2,1)} %query_hbm.1, f32[128,128]{1,0:T(8,128)} %norm_hbm.1, f32[32,64]{1,0:T(8,128)} %weight_hbm.1, s32[1,128]{1,0:T(1,128)} %bitcast.3), custom_call_target="tpu_custom_call" | custom-call | flops 1500000000 | tf_op jit(solution)/shard_map/pallas_call | solution.py:26
  8.6 0.6 %collective-permute-done.4.refs_1_.refs_2_ = bf16[704,128]{1,0:T(8,128)(2,1)S(1)} collective-permute-done((bf16[704,128]{1,0:T(8,128)(2,1)S(1)}, bf16[704,128]{1,0:T(8,128)(2,1)S(1)}, u32[]{:S(2)}, u32[]{:S(2)}) %collective-permute-start.4) | collective-permute-done | bytes 180256 | tf_op jit(solution)/shard_map/ppermute | solution.py:376
  9.2 0.0 collective-permute-start.6
  9.2 2.8 %collective-permute-done.3.refs_0_.refs_1_ = bf16[704,128]{1,0:T(8,128)(2,1)S(1)} collective-permute-done((bf16[704,128]{1,0:T(8,128)(2,1)S(1)}, bf16[704,128]{1,0:T(8,128)(2,1)S(1)}, u32[]{:S(2)}, u32[]{:S(2)}) %collective-permute-start.3) | collective-permute-done | bytes 180256 | tf_op jit(solution)/shard_map/ppermute | solution.py:376
  12.1 0.0 collective-permute-start.5
  12.1 2.2 %collective-permute-done.refs_0_.refs_3_ = bf16[704,128]{1,0:T(8,128)(2,1)S(1)} collective-permute-done((bf16[704,128]{1,0:T(8,128)(2,1)S(1)}, bf16[704,128]{1,0:T(8,128)(2,1)S(1)}, u32[]{:S(2)}, u32[]{:S(2)}) %collective-permute-start) | collective-permute-done | bytes 180256 | tf_op jit(solution)/shard_map/ppermute | solution.py:376
  14.3 0.0 collective-permute-start.1
  14.3 2.1 %shard_map.96.refs_3_ = f32[1,128,256]{2,1,0:T(8,128)S(1)} custom-call(bf16[128,18432]{1,0:T(8,128)(2,1)S(1)} %get-tuple-element.29.query_ref, f32[32,128,128]{2,1,0:T(8,128)S(1)} %get-tuple-element.30.off_ref, bf16[704,128]{1,0:T(8,128)(2,1)S(1)} %collective-permute-done.3.refs_0_.refs_1_, bf16[704,128]{1,0:T(8,128)(2,1)S(1)} %collective-permute-done.4.refs_1_.refs_2_), custom_call_target="tpu_custom_call" | custom-call | flops 1207959552 | tf_op jit(solution)/shard_map/pallas_call | solution.py:26
  16.4 0.0 collective-permute-done.2.refs_1_.refs_4_
  16.5 2.1 %shard_map.95.refs_2_ = f32[1,128,256]{2,1,0:T(8,128)S(1)} custom-call(bf16[128,18432]{1,0:T(8,128)(2,1)S(1)} %get-tuple-element.29.query_ref, f32[32,128,128]{2,1,0:T(8,128)S(1)} %get-tuple-element.30.off_ref, bf16[704,128]{1,0:T(8,128)(2,1)S(1)} %pad_maximum_fusion.refs_0_, bf16[704,128]{1,0:T(8,128)(2,1)S(1)} %collective-permute-done.2.refs_1_.refs_4_), custom_call_target="tpu_custom_call" | custom-call | flops 1207959552 | tf_op jit(solution)/shard_map/pallas_call | solution.py:26
  18.6 0.0 collective-permute-done.6.refs_1_.refs_6_
  18.6 0.0 collective-permute-done.5.refs_0_.refs_5_
  18.6 2.1 %shard_map.97.refs_4_ = f32[1,128,256]{2,1,0:T(8,128)S(1)} custom-call(bf16[128,18432]{1,0:T(8,128)(2,1)S(1)} %get-tuple-element.29.query_ref, f32[32,128,128]{2,1,0:T(8,128)S(1)} %get-tuple-element.30.off_ref, bf16[704,128]{1,0:T(8,128)(2,1)S(1)} %collective-permute-done.5.refs_0_.refs_5_, bf16[704,128]{1,0:T(8,128)(2,1)S(1)} %collective-permute-done.6.refs_1_.refs_6_), custom_call_target="tpu_custom_call" | custom-call | flops 1207959552 | tf_op jit(solution)/shard_map/pallas_call | solution.py:26
  20.7 0.0 copy-start
  20.8 0.0 collective-permute-done.1.refs_1_.refs_7_
  20.8 2.2 %shard_map.98 = (f32[32,1024]{1,0:T(8,128)S(1)}, bf16[32,1024]{1,0:T(8,128)(2,1)S(1)}, bf16[32,1024]{1,0:T(8,128)(2,1)S(1)}, bf16[32,1024]{1,0:T(8,128)(2,1)S(1)}) custom-call(bf16[128,18432]{1,0:T(8,128)(2,1)S(1)} %get-tuple-element.29.query_ref, f32[32,128,128]{2,1,0:T(8,128)S(1)} %get-tuple-element.30.off_ref, ...), custom_call_target="tpu_custom_call" | custom-call | flops 1207959552 | tf_op jit(solution)/shard_map/pallas_call | solution.py:26
  22.9 1.8 %collective-permute-start.7 = (bf16[32,1024]{1,0:T(8,128)(2,1)S(1)}, bf16[32,1024]{1,0:T(8,128)(2,1)S(1)}, u32[]{:S(2)}, u32[]{:S(2)}) collective-permute-start(bf16[32,1024]{1,0:T(8,128)(2,1)S(1)} %get-tuple-element.32), channel_id=1, source_target_pairs={{0,1},{1,2},{2,3},{3,0},{4,5},{5,6},{6,7},{7,4},{8,9},{9,10},{10,1... | collective-permute-start | bytes 196616 | tf_op jit(solution)/shard_map/ppermute | solution.py:382
  24.7 2.6 %collective-permute-start.8 = (bf16[32,1024]{1,0:T(8,128)(2,1)S(1)}, bf16[32,1024]{1,0:T(8,128)(2,1)S(1)}, u32[]{:S(2)}, u32[]{:S(2)}) collective-permute-start(bf16[32,1024]{1,0:T(8,128)(2,1)S(1)} %get-tuple-element.33), channel_id=1, source_target_pairs={{0,2},{1,3},{2,0},{3,1},{4,6},{5,7},{6,4},{7,5},{8,10},{9,11},{10,... | collective-permute-start | bytes 196616 | tf_op jit(solution)/shard_map/ppermute | solution.py:382
  27.3 1.4 %collective-permute-start.9 = (bf16[32,1024]{1,0:T(8,128)(2,1)S(1)}, bf16[32,1024]{1,0:T(8,128)(2,1)S(1)}, u32[]{:S(2)}, u32[]{:S(2)}) collective-permute-start(bf16[32,1024]{1,0:T(8,128)(2,1)S(1)} %get-tuple-element.34), channel_id=1, source_target_pairs={{0,3},{1,0},{2,1},{3,2},{4,7},{5,4},{6,5},{7,6},{8,11},{9,8},{10,9... | collective-permute-start | bytes 196616 | tf_op jit(solution)/shard_map/ppermute | solution.py:382
  28.7 0.0 copy-done
  28.7 2.7 %shard_map.99 = (f32[64,32,1024]{2,1,0:T(8,128)S(1)}, f32[32,1024]{1,0:T(8,128)S(1)}, bf16[1024,128]{1,0:T(8,128)(2,1)S(1)}) custom-call(bf16[32,8192]{1,0:T(8,128)(2,1)S(1)} %copy-done, f32[64,32,128]{2,1,0:T(8,128)S(1)} %get-tuple-element.35.scale_ref.refs_6_.refs_2_, f32[32,128]{1,0:T(8,128)S(1)} %get-tuple-element.36.low_ref, ...), custom_call_target="tpu_custom_call" | custom-call | flops 1610612736 | tf_op jit(solution)/shard_map/pallas_call | solution.py:26
  31.3 0.0 collective-permute-done.7.refs_1_
  31.3 1.1 %collective-permute-done.8.refs_2_ = bf16[32,1024]{1,0:T(8,128)(2,1)S(1)} collective-permute-done((bf16[32,1024]{1,0:T(8,128)(2,1)S(1)}, bf16[32,1024]{1,0:T(8,128)(2,1)S(1)}, u32[]{:S(2)}, u32[]{:S(2)}) %collective-permute-start.8) | collective-permute-done | bytes 65568 | tf_op jit(solution)/shard_map/ppermute | solution.py:382
  32.4 0.2 collective-permute-done.9.refs_3_
  32.6 2.1 %shard_map.100 = (f32[32,1024]{1,0:T(8,128)S(1)}, bf16[2048,512]{1,0:T(8,128)(2,1)S(1)}, f32[512,128]{1,0:T(8,128)S(1)}) custom-call(f32[32,1024]{1,0:T(8,128)S(1)} %get-tuple-element.31.refs_0_, bf16[32,1024]{1,0:T(8,128)(2,1)S(1)} %collective-permute-done.7.refs_1_, bf16[32,1024]{1,0:T(8,128)(2,1)S(1)} %collective-permute-done.8.refs_2_, ...), custom_call_target="tpu_custom_call" | custom-call | flops 1073741824 | tf_op jit(solution)/shard_map/pallas_call | solution.py:26
  34.8 0.1 collective-permute-start.10
  34.8 2.0 %shard_map.101 = (bf16[2048,512]{1,0:T(8,128)(2,1)S(1)}, f32[512,128]{1,0:T(8,128)S(1)}) custom-call(f32[32,1024]{1,0:T(8,128)S(1)} %get-tuple-element.39.refs_0_.gap_ref, f32[64,32,1024]{2,1,0:T(8,128)S(1)} %get-tuple-element.38.refs_5_.refs_1_.active_ref, f32[64,32,128]{2,1,0:T(8,128)S(1)} %get-tuple-element.35.scale_ref.refs_6_.refs_2_, ...), custom_call_target="tpu_custom_call" | custom-call | flops 1073741824 | tf_op jit(solution)/shard_map/pallas_call | solution.py:26
  36.8 0.0 collective-permute-done.10.come_ref
  36.9 1.6 %collective-permute-start.11 = (bf16[128,128]{1,0:T(8,128)(2,1)S(1)}, bf16[128,128]{1,0:T(8,128)(2,1)S(1)}, u32[]{:S(2)}, u32[]{:S(2)}) collective-permute-start(bf16[128,128]{1,0:T(8,128)(2,1)S(1)} %get-tuple-element.48), channel_id=1, source_target_pairs={{0,8},{4,12},{8,0},{12,4},{16,24},{20,28},{24,16},{28,20},{1,9},{5... | collective-permute-start | bytes 98312 | tf_op jit(solution)/shard_map/ppermute | solution.py:376
  38.4 1.5 %collective-permute-start.12 = (bf16[128,128]{1,0:T(8,128)(2,1)S(1)}, bf16[128,128]{1,0:T(8,128)(2,1)S(1)}, u32[]{:S(2)}, u32[]{:S(2)}) collective-permute-start(bf16[128,128]{1,0:T(8,128)(2,1)S(1)} %get-tuple-element.49), channel_id=1, source_target_pairs={{0,16},{4,20},{8,24},{12,28},{16,0},{20,4},{24,8},{28,12},{1,17},{... | collective-permute-start | bytes 98312 | tf_op jit(solution)/shard_map/ppermute | solution.py:376
  40.0 0.5 collective-permute-start.13
  40.4 0.4 collective-permute-done.11.refs_0_
  40.9 1.5 %collective-permute-done.12.refs_1_ = bf16[128,128]{1,0:T(8,128)(2,1)S(1)} collective-permute-done((bf16[128,128]{1,0:T(8,128)(2,1)S(1)}, bf16[128,128]{1,0:T(8,128)(2,1)S(1)}, u32[]{:S(2)}, u32[]{:S(2)}) %collective-permute-start.12) | collective-permute-done | bytes 32800 | tf_op jit(solution)/shard_map/ppermute | solution.py:376
  42.4 2.4 %collective-permute-done.13.refs_2_ = bf16[128,128]{1,0:T(8,128)(2,1)S(1)} collective-permute-done((bf16[128,128]{1,0:T(8,128)(2,1)S(1)}, bf16[128,128]{1,0:T(8,128)(2,1)S(1)}, u32[]{:S(2)}, u32[]{:S(2)}) %collective-permute-start.13) | collective-permute-done | bytes 32800 | tf_op jit(solution)/shard_map/ppermute | solution.py:376
  44.8 1.7 %collective-permute-start.14 = (f32[32,128]{1,0:T(8,128)S(1)}, f32[32,128]{1,0:T(8,128)S(1)}, u32[]{:S(2)}, u32[]{:S(2)}) collective-permute-start(f32[32,128]{1,0:T(8,128)S(1)} %get-tuple-element.52), channel_id=1, source_target_pairs={{0,1},{1,2},{2,3},{3,0},{4,5},{5,6},{6,7},{7,4},{8,9},{9,10},{10,1... | collective-permute-start | bytes 49160 | tf_op jit(solution)/shard_map/ppermute | solution.py:382
  46.5 1.6 %collective-permute-start.15 = (f32[32,128]{1,0:T(8,128)S(1)}, f32[32,128]{1,0:T(8,128)S(1)}, u32[]{:S(2)}, u32[]{:S(2)}) collective-permute-start(f32[32,128]{1,0:T(8,128)S(1)} %get-tuple-element.53), channel_id=1, source_target_pairs={{0,2},{1,3},{2,0},{3,1},{4,6},{5,7},{6,4},{7,5},{8,10},{9,11},{10,... | collective-permute-start | bytes 49160 | tf_op jit(solution)/shard_map/ppermute | solution.py:382
  48.1 0.8 %collective-permute-start.16 = (f32[32,128]{1,0:T(8,128)S(1)}, f32[32,128]{1,0:T(8,128)S(1)}, u32[]{:S(2)}, u32[]{:S(2)}) collective-permute-start(f32[32,128]{1,0:T(8,128)S(1)} %get-tuple-element.54), channel_id=1, source_target_pairs={{0,3},{1,0},{2,1},{3,2},{4,7},{5,4},{6,5},{7,6},{8,11},{9,8},{10,9... | collective-permute-start | bytes 49160 | tf_op jit(solution)/shard_map/ppermute | solution.py:382
  49.0 3.3 %shard_map.102 = (f32[32,8192]{1,0:T(8,128)}, f32[32,64]{1,0:T(8,128)}) custom-call(f32[32,1024]{1,0:T(8,128)S(1)} %get-tuple-element.39.refs_0_.gap_ref, bf16[2048,512]{1,0:T(8,128)(2,1)S(1)} %get-tuple-element.40.even_ref, bf16[2048,512]{1,0:T(8,128)(2,1)S(1)} %get-tuple-element.41.odd_ref, ...), custom_call_target="tpu_custom_call" | custom-call | flops 1610612736 | tf_op jit(solution)/shard_map/pallas_call | solution.py:26
  52.2 0.0 collective-permute-done.14
  52.2 0.0 collective-permute-done.15
  52.2 0.0 collective-permute-done.16
  52.2 0.6 %add_add_fusion = f32[32,128]{1,0:T(8,128)} fusion(f32[32,128]{1,0:T(8,128)S(1)} %collective-permute-done.16, f32[32,128]{1,0:T(8,128)S(1)} %collective-permute-done.15, f32[32,128]{1,0:T(8,128)S(1)} %get-tuple-element.51, f32[32,128]{1,0:T(8,128)S(1)} %collective-permute-done.14), kind=kLoop, calls=%fused_computation.1 | loop fusion | flops 12288 | bytes 81920 | tf_op jit(solution)/shard_map/add | solution.py:426
  (2 shorter events, 0.1 us)
Async XLA Ops:
  1.6 7.6 %collective-permute-start.4 = (bf16[704,128]{1,0:T(8,128)(2,1)S(1)}, bf16[704,128]{1,0:T(8,128)(2,1)S(1)}, u32[]{:S(2)}, u32[]{:S(2)}) collective-permute-start(bf16[704,128]{1,0:T(8,128)(2,1)S(1)} %pad_maximum_fusion.refs_0_), channel_id=1, source_target_pairs={{0,16},{4,20},{8,24},{12,28},{16,0},{20,4},{24,8},{28,12},{1,17},{... | collective-permute-start | bytes 540680 | tf_op jit(solution)/shard_map/ppermute | solution.py:376
  4.6 7.4 %collective-permute-start.3 = (bf16[704,128]{1,0:T(8,128)(2,1)S(1)}, bf16[704,128]{1,0:T(8,128)(2,1)S(1)}, u32[]{:S(2)}, u32[]{:S(2)}) collective-permute-start(bf16[704,128]{1,0:T(8,128)(2,1)S(1)} %pad_maximum_fusion.refs_0_), channel_id=1, source_target_pairs={{0,8},{4,12},{8,0},{12,4},{16,24},{20,28},{24,16},{28,20},{1,9},{5... | collective-permute-start | bytes 540680 | tf_op jit(solution)/shard_map/ppermute | solution.py:376
  6.1 8.2 %collective-permute-start = (bf16[704,128]{1,0:T(8,128)(2,1)S(1)}, bf16[704,128]{1,0:T(8,128)(2,1)S(1)}, u32[]{:S(2)}, u32[]{:S(2)}) collective-permute-start(bf16[704,128]{1,0:T(8,128)(2,1)S(1)} %pad_maximum_fusion.refs_0_), channel_id=1, source_target_pairs={{0,24},{4,28},{8,16},{12,20},{16,8},{20,12},{24,0},{28,4},{1,25},{... | collective-permute-start | bytes 540680 | tf_op jit(solution)/shard_map/ppermute | solution.py:376
  6.2 10.3 %collective-permute-start.2 = (bf16[704,128]{1,0:T(8,128)(2,1)S(1)}, bf16[704,128]{1,0:T(8,128)(2,1)S(1)}, u32[]{:S(2)}, u32[]{:S(2)}) collective-permute-start(bf16[704,128]{1,0:T(8,128)(2,1)S(1)} %pad_maximum_fusion.refs_0_), channel_id=1, source_target_pairs={{0,4},{4,0},{8,12},{12,8},{16,20},{20,16},{24,28},{28,24},{1,5},{5... | collective-permute-start | bytes 540680 | tf_op jit(solution)/shard_map/ppermute | solution.py:376
  9.2 9.4 %collective-permute-start.6 = (bf16[704,128]{1,0:T(8,128)(2,1)S(1)}, bf16[704,128]{1,0:T(8,128)(2,1)S(1)}, u32[]{:S(2)}, u32[]{:S(2)}) collective-permute-start(bf16[704,128]{1,0:T(8,128)(2,1)S(1)} %collective-permute-done.4.refs_1_.refs_2_), channel_id=1, source_target_pairs={{0,4},{4,0},{8,12},{12,8},{16,20},{20,16},{24,28},{28,24},{1,5},{5... | collective-permute-start | bytes 540680 | tf_op jit(solution)/shard_map/ppermute | solution.py:376
  12.1 6.5 %collective-permute-start.5 = (bf16[704,128]{1,0:T(8,128)(2,1)S(1)}, bf16[704,128]{1,0:T(8,128)(2,1)S(1)}, u32[]{:S(2)}, u32[]{:S(2)}) collective-permute-start(bf16[704,128]{1,0:T(8,128)(2,1)S(1)} %collective-permute-done.3.refs_0_.refs_1_), channel_id=1, source_target_pairs={{0,4},{4,0},{8,12},{12,8},{16,20},{20,16},{24,28},{28,24},{1,5},{5... | collective-permute-start | bytes 540680 | tf_op jit(solution)/shard_map/ppermute | solution.py:376
  14.3 6.5 %collective-permute-start.1 = (bf16[704,128]{1,0:T(8,128)(2,1)S(1)}, bf16[704,128]{1,0:T(8,128)(2,1)S(1)}, u32[]{:S(2)}, u32[]{:S(2)}) collective-permute-start(bf16[704,128]{1,0:T(8,128)(2,1)S(1)} %collective-permute-done.refs_0_.refs_3_), channel_id=1, source_target_pairs={{0,4},{4,0},{8,12},{12,8},{16,20},{20,16},{24,28},{28,24},{1,5},{5... | collective-permute-start | bytes 540680 | tf_op jit(solution)/shard_map/ppermute | solution.py:376
  20.7 7.9 %copy-start = (bf16[32,8192]{1,0:T(8,128)(2,1)S(1)}, bf16[32,8192]{1,0:T(8,128)(2,1)}, u32[]{:S(2)}) copy-start(bf16[32,8192]{1,0:T(8,128)(2,1)} %refs_3_.1) | copy-start | bytes 1572868
  22.9 8.4 %collective-permute-start.7 = (bf16[32,1024]{1,0:T(8,128)(2,1)S(1)}, bf16[32,1024]{1,0:T(8,128)(2,1)S(1)}, u32[]{:S(2)}, u32[]{:S(2)}) collective-permute-start(bf16[32,1024]{1,0:T(8,128)(2,1)S(1)} %get-tuple-element.32), channel_id=1, source_target_pairs={{0,1},{1,2},{2,3},{3,0},{4,5},{5,6},{6,7},{7,4},{8,9},{9,10},{10,1... | collective-permute-start | bytes 196616 | tf_op jit(solution)/shard_map/ppermute | solution.py:382
  24.7 7.7 %collective-permute-start.8 = (bf16[32,1024]{1,0:T(8,128)(2,1)S(1)}, bf16[32,1024]{1,0:T(8,128)(2,1)S(1)}, u32[]{:S(2)}, u32[]{:S(2)}) collective-permute-start(bf16[32,1024]{1,0:T(8,128)(2,1)S(1)} %get-tuple-element.33), channel_id=1, source_target_pairs={{0,2},{1,3},{2,0},{3,1},{4,6},{5,7},{6,4},{7,5},{8,10},{9,11},{10,... | collective-permute-start | bytes 196616 | tf_op jit(solution)/shard_map/ppermute | solution.py:382
  27.3 5.3 %collective-permute-start.9 = (bf16[32,1024]{1,0:T(8,128)(2,1)S(1)}, bf16[32,1024]{1,0:T(8,128)(2,1)S(1)}, u32[]{:S(2)}, u32[]{:S(2)}) collective-permute-start(bf16[32,1024]{1,0:T(8,128)(2,1)S(1)} %get-tuple-element.34), channel_id=1, source_target_pairs={{0,3},{1,0},{2,1},{3,2},{4,7},{5,4},{6,5},{7,6},{8,11},{9,8},{10,9... | collective-permute-start | bytes 196616 | tf_op jit(solution)/shard_map/ppermute | solution.py:382
  34.8 2.1 %collective-permute-start.10 = (f32[512,128]{1,0:T(8,128)S(1)}, f32[512,128]{1,0:T(8,128)S(1)}, u32[]{:S(2)}, u32[]{:S(2)}) collective-permute-start(f32[512,128]{1,0:T(8,128)S(1)} %get-tuple-element.46), channel_id=1, source_target_pairs={{0,4},{4,0},{8,12},{12,8},{16,20},{20,16},{24,28},{28,24},{1,5},{5... | collective-permute-start | bytes 786440 | tf_op jit(solution)/shard_map/ppermute | solution.py:376
  36.9 4.0 %collective-permute-start.11 = (bf16[128,128]{1,0:T(8,128)(2,1)S(1)}, bf16[128,128]{1,0:T(8,128)(2,1)S(1)}, u32[]{:S(2)}, u32[]{:S(2)}) collective-permute-start(bf16[128,128]{1,0:T(8,128)(2,1)S(1)} %get-tuple-element.48), channel_id=1, source_target_pairs={{0,8},{4,12},{8,0},{12,4},{16,24},{20,28},{24,16},{28,20},{1,9},{5... | collective-permute-start | bytes 98312 | tf_op jit(solution)/shard_map/ppermute | solution.py:376
  38.4 3.9 %collective-permute-start.12 = (bf16[128,128]{1,0:T(8,128)(2,1)S(1)}, bf16[128,128]{1,0:T(8,128)(2,1)S(1)}, u32[]{:S(2)}, u32[]{:S(2)}) collective-permute-start(bf16[128,128]{1,0:T(8,128)(2,1)S(1)} %get-tuple-element.49), channel_id=1, source_target_pairs={{0,16},{4,20},{8,24},{12,28},{16,0},{20,4},{24,8},{28,12},{1,17},{... | collective-permute-start | bytes 98312 | tf_op jit(solution)/shard_map/ppermute | solution.py:376
  40.0 4.8 %collective-permute-start.13 = (bf16[128,128]{1,0:T(8,128)(2,1)S(1)}, bf16[128,128]{1,0:T(8,128)(2,1)S(1)}, u32[]{:S(2)}, u32[]{:S(2)}) collective-permute-start(bf16[128,128]{1,0:T(8,128)(2,1)S(1)} %get-tuple-element.50), channel_id=1, source_target_pairs={{0,24},{4,28},{8,16},{12,20},{16,8},{20,12},{24,0},{28,4},{1,25},{... | collective-permute-start | bytes 98312 | tf_op jit(solution)/shard_map/ppermute | solution.py:376
  44.8 7.4 %collective-permute-start.14 = (f32[32,128]{1,0:T(8,128)S(1)}, f32[32,128]{1,0:T(8,128)S(1)}, u32[]{:S(2)}, u32[]{:S(2)}) collective-permute-start(f32[32,128]{1,0:T(8,128)S(1)} %get-tuple-element.52), channel_id=1, source_target_pairs={{0,1},{1,2},{2,3},{3,0},{4,5},{5,6},{6,7},{7,4},{8,9},{9,10},{10,1... | collective-permute-start | bytes 49160 | tf_op jit(solution)/shard_map/ppermute | solution.py:382
  46.5 5.7 %collective-permute-start.15 = (f32[32,128]{1,0:T(8,128)S(1)}, f32[32,128]{1,0:T(8,128)S(1)}, u32[]{:S(2)}, u32[]{:S(2)}) collective-permute-start(f32[32,128]{1,0:T(8,128)S(1)} %get-tuple-element.53), channel_id=1, source_target_pairs={{0,2},{1,3},{2,0},{3,1},{4,6},{5,7},{6,4},{7,5},{8,10},{9,11},{10,... | collective-permute-start | bytes 49160 | tf_op jit(solution)/shard_map/ppermute | solution.py:382
  48.1 4.1 %collective-permute-start.16 = (f32[32,128]{1,0:T(8,128)S(1)}, f32[32,128]{1,0:T(8,128)S(1)}, u32[]{:S(2)}, u32[]{:S(2)}) collective-permute-start(f32[32,128]{1,0:T(8,128)S(1)} %get-tuple-element.54), channel_id=1, source_target_pairs={{0,3},{1,0},{2,1},{3,2},{4,7},{5,4},{6,5},{7,6},{8,11},{9,8},{10,9... | collective-permute-start | bytes 49160 | tf_op jit(solution)/shard_map/ppermute | solution.py:382
where the time goes:
time: 53 us; the launch traced here: 52.8 us
  Pallas kernels  21.1 us (40%)
  starting transfers between devices  18.1 us (34%)
  waiting for transfers between devices  11.3 us (21%)
  other arithmetic  1.56 us (3%)
  between operations  0.78 us (1%)
    pallas_call x11, Pallas kernels, call(): pl.pallas_call(body, out_shape=out_shape, in_specs=specs or [VMEM] * len(...  21.1 us
    ppermute x11, waiting for transfers between devices, swap(): lax.ppermute(value, 'seq', [(place, place ^ bits) for place in range(seq_...  9.99 us
    ppermute x6, starting transfers between devices, pass_on(): out.append(lax.ppermute(value, 'head', to))  9.88 us
    ppermute x11, starting transfers between devices, swap(): lax.ppermute(value, 'seq', [(place, place ^ bits) for place in range(seq_...  8.26 us
    ppermute x6, waiting for transfers between devices, pass_on(): out.append(lax.ppermute(value, 'head', to))  1.32 us
  transfers between devices with their start and end apart: 17, of which 8 were waited for; matrix products, arithmetic and copies ran while one was open for 0% of the time, Pallas kernels for 32%

commit v1 on v0

--- a/solution.py
+++ b/solution.py
@@ -130,7 +130,6 @@
         return
     own, sends = outs[0], outs[1:]
     rows = own.shape[0]
-    size = len(sends) + 1
     me = lax.axis_index("head")
     sources = [(ref, tile) for ref in (*prior, acc) for tile in range(ref.shape[0])]
     pieces = [(ref, tile, part) for ref, tile in sources for part in range(per_tile)]
@@ -138,7 +137,7 @@
         lanes = lanes_of(part)
         own[:, lanes_of(place)] = ref[tile, pl.ds(me * rows, rows), lanes]
         for hop, send in enumerate(sends):
-            there = lax.rem(me + hop + 1, size)
+            there = jnp.bitwise_xor(me, hop + 1)
             send[:, lanes_of(place)] = ref[tile, pl.ds(there * rows, rows), lanes].astype(send.dtype)
 
 
@@ -173,22 +172,24 @@
     return jnp.concatenate(parts, axis=0).astype(value.dtype)
 
 
-def score_kernel(order, query_ref, scale_ref, low_ref, *refs):
-    slots = len(order)
-    blocks = refs[:slots]
-    active_ref, predicted_ref, keys, score = refs[slots:]
-    index_heads, rows, seq_total = active_ref.shape
+def score_kernel(slots, query_ref, scale_ref, *refs):
+    blocks, (active_ref, score, keys) = refs[:slots], refs[slots:]
+    score_blocks(blocks, query_ref, scale_ref, active_ref, score, keys)
+
+
+def score_blocks(blocks, query_ref, scale_ref, active_ref, score, keys):
+    index_heads, rows, columns = active_ref.shape
     dims = keys.shape[1]
     group = min(8, index_heads)
     score[...] = jnp.zeros_like(score)
-    for place in range(slots):
-        keys[lanes_of(place)] = blocks[place][KDIM:]
+    for place, block in enumerate(blocks):
+        keys[lanes_of(place)] = block[KDIM:]
 
     @pl.loop(0, index_heads // group)
     def _(step):
         begin = pl.multiple_of(step * (group * dims), LANES)
         stacked = stack_heads(query_ref[:, pl.ds(begin, group * dims)], group, dims)
-        for begin in range(0, seq_total, WIDE):
+        for begin in range(0, columns, WIDE):
             inner = lax.dot_general(
                 stacked,
                 keys[begin : begin + WIDE],
@@ -202,39 +203,84 @@
                 total = total + active * jnp.concatenate([scale_ref[step * group + head]] * 2, axis=1)
             score[:, begin : begin + WIDE] = total
 
+
+def predict_kernel(order, slots, query_ref, scale_ref, low_ref, first_ref, first_keys_ref, *refs):
+    blocks, refs = refs[:slots], refs[slots:]
+    active_ref, predicted_ref, keys_ref, score, keys = refs
+    score_blocks(blocks, query_ref, scale_ref, active_ref, score, keys)
+    rows = score.shape[0]
+    halves = halved((first_ref, score), 1)
+    for half in range(2):
+        begin = half * (len(order) // 2) * LANES
+        for ref in (first_keys_ref, keys):
+            part = ref.shape[0] // 2
+            keys_ref[begin : begin + part] = ref[half * part : (half + 1) * part]
+            begin += part
+
     seq = lax.axis_index("seq")
     query_pos = (
         seq * lax.axis_size("head") + lax.axis_index("head")
     ) * rows + lax.broadcasted_iota(jnp.int32, (rows, LANES), 0)
     low = query_pos - low_ref[...].astype(jnp.int32)
     lane = lax.broadcasted_iota(jnp.int32, (rows, LANES), 1)
-    seen = []
-    for slot in order:
+    scores = jnp.concatenate(halves, axis=1)
+    parts, seen = [], []
+    for place, slot in enumerate(order):
         key_pos = jnp.bitwise_xor(seq, slot) * LANES + lane
         seen.append((key_pos <= query_pos) & (key_pos >= low))
-    parts = [score[:, lanes_of(place)] for place in range(slots)]
-    parts = [jnp.where(see, part, -jnp.inf) for see, part in zip(seen, parts)]
+        parts.append(jnp.where(seen[-1], scores[:, lanes_of(place)], -jnp.inf))
     top = jnp.max(functools.reduce(jnp.maximum, parts), axis=1, keepdims=True)
     parts = [jnp.exp(part - top) for part in parts]
     mass = jnp.sum(functools.reduce(jnp.add, parts), axis=1, keepdims=True)
-    for place in range(slots):
+    for place in range(len(order)):
         predicted_ref[:, lanes_of(place)] = jnp.where(seen[place], parts[place] / mass, -1.0)
 
 
-def index_scores(index_query, scales, lows, blocks, order, dims):
+def halved(refs, axis, *index):
+    out = []
+    for half in range(2):
+        parts = []
+        for ref in refs:
+            part = ref.shape[-1] // 2
+            parts.append(ref[(*index, slice(None), slice(half * part, (half + 1) * part))])
+        out.append(jnp.concatenate(parts, axis=axis))
+    return out
+
+
+def index_scores(index_query, scales, blocks, dims):
     rows = index_query.shape[0]
     index_heads = scales.shape[0]
+    columns = len(blocks) * LANES
+    return call(
+        functools.partial(score_kernel, len(blocks)),
+        (
+            shape_of((index_heads, rows, columns), jnp.float32),
+            shape_of((rows, columns), jnp.float32),
+            shape_of((columns, dims), jnp.bfloat16),
+        ),
+        (index_query, scales, *blocks),
+        flops=6 * rows * index_heads * columns * dims,
+    )
+
+
+def predictions(index_query, scales, lows, scores, keys, blocks, order, dims):
+    rows = index_query.shape[0]
+    index_heads = scales.shape[0]
+    columns = len(blocks) * LANES
     seq_total = len(order) * LANES
     return call(
-        functools.partial(score_kernel, order),
+        functools.partial(predict_kernel, order, len(blocks)),
         (
-            shape_of((index_heads, rows, seq_total), jnp.float32),
+            shape_of((index_heads, rows, columns), jnp.float32),
             shape_of((rows, seq_total), jnp.float32),
             shape_of((seq_total, dims), jnp.bfloat16),
         ),
-        (index_query, scales, lows, *blocks),
-        scratch=[pltpu.VMEM((rows, seq_total), jnp.float32)],
-        flops=6 * rows * index_heads * seq_total * dims,
+        (index_query, scales, lows, scores, keys, *blocks),
+        scratch=[
+            pltpu.VMEM((rows, columns), jnp.float32),
+            pltpu.VMEM((columns, dims), jnp.bfloat16),
+        ],
+        flops=8 * rows * index_heads * columns * dims,
     )
 
 
@@ -252,11 +298,11 @@
 def key_kernel(peers, half, *refs):
     shares, refs = refs[:peers], refs[peers:]
     if peers:
-        predicted_ref, active_ref, scale_ref, query_ref, gap_ref, slopes_ref, out_ref, tall = refs
+        predicted_ref, *actives, scale_ref, query_ref, gap_ref, slopes_ref, out_ref, tall = refs
         gap_ref[...] = gap_of(shares, predicted_ref[...])
     else:
-        gap_ref, active_ref, scale_ref, query_ref, slopes_ref, out_ref, tall = refs
-    index_heads, rows, _ = active_ref.shape
+        gap_ref, *actives, scale_ref, query_ref, slopes_ref, out_ref, tall = refs
+    index_heads, rows, _ = actives[0].shape
     dims, columns = tall.shape
     lanes = slice(half * columns, (half + 1) * columns)
     group = min(8, index_heads)
@@ -269,7 +315,7 @@
         for head in range(group):
             place = step * group + head
             scaled = gap * jnp.concatenate([scale_ref[place]] * (columns // LANES), axis=1)
-            slope = jnp.where(active_ref[place, :, lanes] > 0.0, scaled, 0.0)
+            slope = jnp.where(halved(actives, 1, place)[half] > 0.0, scaled, 0.0)
             slopes.append(slope if rows % 16 else slope.astype(jnp.bfloat16))
         slopes = jnp.concatenate(slopes, axis=0).astype(jnp.bfloat16)
         block = pl.ds(pl.multiple_of(step * (group * rows), group * rows), group * rows)
@@ -284,8 +330,9 @@
         out_ref[lanes_of(place)] = jnp.transpose(tall[:, lanes_of(place)])
 
 
-def key_terms(shares, gap, predicted, active, scales, index_query, dims, half):
-    index_heads, rows, seq_total = active.shape
+def key_terms(shares, gap, predicted, actives, scales, index_query, dims, half):
+    index_heads, rows, _ = actives[0].shape
+    seq_total = sum(active.shape[2] for active in actives)
     columns = seq_total // 2
     out = (
         shape_of((index_heads * rows, columns), jnp.bfloat16),
@@ -299,31 +346,20 @@
     return call(
         functools.partial(key_kernel, len(shares), half),
         out,
-        (*args, active, scales, index_query),
+        (*args, *actives, scales, index_query),
         scratch=[pltpu.VMEM((dims, columns), jnp.float32)],
         flops=4 * rows * index_heads * seq_total * dims,
     )
 
 
-def query_kernel(factor, gap_ref, even_ref, odd_ref, active_ref, keys_ref, grad_query_ref, grad_weight_ref, sums):
-    index_heads, rows, seq_total = active_ref.shape
+def query_kernel(even_ref, odd_ref, keys_ref, grad_query_ref):
+    rows = grad_query_ref.shape[0]
     dims = keys_ref.shape[1]
+    index_heads = grad_query_ref.shape[1] // dims
     group = min(8, index_heads)
-    lane = lax.broadcasted_iota(jnp.int32, (rows, LANES), 1)
-    sums[...] = jnp.zeros_like(sums)
 
     @pl.loop(0, index_heads // group)
     def _(step):
-        gap = gap_ref[...]
-        total = sums[...]
-        for head in range(group):
-            product = active_ref[step * group + head] * gap
-            partial = functools.reduce(
-                jnp.add, [product[:, lanes_of(place)] for place in range(seq_total // LANES)]
-            )
-            partial = jnp.sum(partial, axis=1, keepdims=True)
-            total = jnp.where(lane == step * group + head, partial, total)
-        sums[...] = total
         block = pl.ds(pl.multiple_of(step * (group * rows), group * rows), group * rows)
         slopes = jnp.concatenate([even_ref[block, :], odd_ref[block, :]], axis=1)
         grad = jnp.dot(slopes, keys_ref[...], preferred_element_type=jnp.float32)
@@ -331,21 +367,48 @@
             begin = pl.multiple_of((step * group + head) * dims, dims)
             grad_query_ref[:, pl.ds(begin, dims)] = grad[head * rows : (head + 1) * rows]
 
+
+def query_grads(even, odd, keys, rows):
+    return call(
+        query_kernel,
+        shape_of((rows, even.shape[0] // rows * keys.shape[1]), jnp.float32),
+        (even, odd, keys),
+        flops=4 * even.shape[0] * keys.shape[0] * keys.shape[1],
+    )
+
+
+def weight_kernel(factor, gap_ref, *refs):
+    *actives, grad_weight_ref, sums = refs
+    index_heads, rows, _ = actives[0].shape
+    group = min(8, index_heads)
+    lane = lax.broadcasted_iota(jnp.int32, (rows, LANES), 1)
+    sums[...] = jnp.zeros_like(sums)
+
+    @pl.loop(0, index_heads // group)
+    def _(step):
+        gap = gap_ref[...]
+        total = sums[...]
+        for head in range(group):
+            place = step * group + head
+            product = jnp.concatenate(halved(actives, 1, place), axis=1) * gap
+            partial = functools.reduce(
+                jnp.add, [product[:, lanes_of(slot)] for slot in range(gap.shape[1] // LANES)]
+            )
+            partial = jnp.sum(partial, axis=1, keepdims=True)
+            total = jnp.where(lane == place, partial, total)
+        sums[...] = total
+
     grad_weight_ref[...] = sums[:, :index_heads] * factor
 
 
-def query_grads(gap, even, odd, active, keys, factor):
-    index_heads, rows, seq_total = active.shape
-    dims = keys.shape[1]
-    return call(
-        functools.partial(query_kernel, factor),
-        (
-            shape_of((rows, index_heads * dims), jnp.float32),
-            shape_of((rows, index_heads), jnp.float32),
-        ),
-        (gap, even, odd, active, keys),
+def weight_grads(gap, actives, factor):
+    index_heads, rows, _ = actives[0].shape
+    return call(
+        functools.partial(weight_kernel, factor),
+        shape_of((rows, index_heads), jnp.float32),
+        (gap, *actives),
         scratch=[pltpu.VMEM((rows, LANES), jnp.float32)],
-        flops=6 * rows * index_heads * seq_total * dims,
+        flops=512 * rows * index_heads * gap.shape[1],
     )
 
 
@@ -378,7 +441,7 @@
     def pass_on(values):
         out = []
         for hop, value in enumerate(values):
-            to = [(place, (place + hop + 1) % peers) for place in range(peers)]
+            to = [(place, place ^ (hop + 1)) for place in range(peers)]
             out.append(lax.ppermute(value, "head", to))
         return out
 
@@ -409,18 +472,22 @@
         prior.append(mass)
     own, *sends = mass
     shares = [own, *pass_on(sends)]
-    active, predicted, keys = index_scores(
-        index_query, scales, lows, [blocks[slot] for slot in order], order, dims
+    early = sorted((slot for phase in phases[:-1] for slot in phase), key=order.index)
+    late = sorted(phases[-1], key=order.index)
+    first, scores, keys = index_scores(index_query, scales, [blocks[slot] for slot in early], dims)
+    second, predicted, keys = predictions(
+        index_query, scales, lows, scores, keys, [blocks[slot] for slot in late], order, dims
     )
     terms = functools.partial(
-        key_terms, active=active, scales=scales, index_query=index_query, dims=dims
+        key_terms, actives=(first, second), scales=scales, index_query=index_query, dims=dims
     )
     gap, odd, give = terms(shares, None, predicted, half=1)
     come = swap(give, 1)
     even, keep = terms([], gap, None, half=0)
     own, *sends = fold(keep, come, LANES)
     others = [swap(send, 2 * (hop + 1)) for hop, send in enumerate(sends)]
-    grad_query, grad_weight = query_grads(gap, even, odd, active, keys, factor)
+    grad_query = query_grads(even, odd, keys, rows)
+    grad_weight = weight_grads(gap, (first, second), factor)
     own, *sends = gather_terms(own, others, rows, peers)
     others = pass_on(sends)
     grad_key = functools.reduce(jnp.add, others, own)
@@ -437,7 +504,7 @@
     me = lax.axis_index("head")
     mine_ref[...] = total[pl.ds(me * rows, rows), :]
     for hop, send in enumerate(sends):
-        send[...] = total[pl.ds(lax.rem(me + hop + 1, peers) * rows, rows), :]
+        send[...] = total[pl.ds(jnp.bitwise_xor(me, hop + 1) * rows, rows), :]
 
 
 def gather_terms(own, others, rows, peers):

time: 53 us -> 53.8 us (1.015)
  Pallas kernels: 21.1 us -> 24.2 us
  waiting for transfers between devices: 11.3 us -> 9.4 us
    pallas_call x11 -> x13, Pallas kernels: 21.1 us -> 24.2 us  [call(): pl.pallas_call(body, out_shape=out_shape, in_specs=specs or [VMEM] * len(...]
    ppermute x11, waiting for transfers between devices: 9.99 us -> 7.45 us  [swap(): lax.ppermute(value, 'seq', [(place, place ^ bits) for place in range(seq_...]
    ppermute x6, starting transfers between devices: 9.88 us -> 8.9 us  [pass_on(): out.append(lax.ppermute(value, 'head', to))]
    ppermute x6, waiting for transfers between devices: 1.32 us -> 1.95 us  [pass_on(): out.append(lax.ppermute(value, 'head', to))]
  transfers between devices with their start and end apart: 17 -> 17, of which waited for: 8 -> 6; matrix products, arithmetic and copies ran while one was open for 0% -> 0% of each run, Pallas kernels for 32% -> 37%
where the time goes in v1:
time: 53.8 us; the launch traced here: 53.6 us
  Pallas kernels  24.2 us (45%)
  starting transfers between devices  17.7 us (33%)
  waiting for transfers between devices  9.4 us (17%)
  other arithmetic  1.56 us (3%)
  between operations  0.79 us (1%)
    pallas_call x13, Pallas kernels, call(): pl.pallas_call(body, out_shape=out_shape, in_specs=specs or [VMEM] * len(...  24.2 us
    ppermute x6, starting transfers between devices, pass_on(): out.append(lax.ppermute(value, 'head', to))  8.9 us
    ppermute x11, starting transfers between devices, swap(): lax.ppermute(value, 'seq', [(place, place ^ bits) for place in range(seq_...  8.77 us
    ppermute x11, waiting for transfers between devices, swap(): lax.ppermute(value, 'seq', [(place, place ^ bits) for place in range(seq_...  7.45 us
    ppermute x6, waiting for transfers between devices, pass_on(): out.append(lax.ppermute(value, 'head', to))  1.95 us
  transfers between devices with their start and end apart: 17, of which 6 were waited for; matrix products, arithmetic and copies ran while one was open for 0% of the time, Pallas kernels for 37%

profile of v1, /device:TPU:0, one launch (start us, length us, event | category | flops | bytes accessed | tf_op | source)
XLA Modules:
  0.0 53.6 jit_solution(9061985656308066139)
XLA Ops:
  0.6 0.9 %pad_maximum_fusion.refs_0_ = bf16[704,128]{1,0:T(8,128)(2,1)S(1)} fusion(bf16[128,128]{1,0:T(8,128)(2,1)} %param.12, bf16[576,128]{1,0:T(8,128)(2,1)} %bitcast.2), kind=kLoop, calls=%fused_computation | loop fusion | flops 360448 | bytes 360448 | tf_op jit(solution)/shard_map/concatenate | solution.py:448
  1.6 4.0 %collective-permute-start = (bf16[704,128]{1,0:T(8,128)(2,1)S(1)}, bf16[704,128]{1,0:T(8,128)(2,1)S(1)}, u32[]{:S(2)}, u32[]{:S(2)}) collective-permute-start(bf16[704,128]{1,0:T(8,128)(2,1)S(1)} %pad_maximum_fusion.refs_0_), channel_id=1, source_target_pairs={{0,24},{4,28},{8,16},{12,20},{16,8},{20,12},{24,0},{28,4},{1,25},{... | collective-permute-start | bytes 540680 | tf_op jit(solution)/shard_map/ppermute | solution.py:439
  5.6 0.5 collective-permute-start.3
  6.1 0.1 collective-permute-start.4
  6.2 0.0 collective-permute-start.2
  6.2 2.4 %shard_map.94 = (bf16[128,18432]{1,0:T(8,128)(2,1)S(1)}, f32[32,128,128]{2,1,0:T(8,128)S(1)}, f32[64,32,128]{2,1,0:T(8,128)S(1)}, f32[32,128]{1,0:T(8,128)S(1)}) custom-call(bf16[128,18432]{1,0:T(8,128)(2,1)} %query_hbm.1, f32[128,128]{1,0:T(8,128)} %norm_hbm.1, f32[32,64]{1,0:T(8,128)} %weight_hbm.1, s32[1,128]{1,0:T(1,128)} %bitcast.3), custom_call_target="tpu_custom_call" | custom-call | flops 1500000000 | tf_op jit(solution)/shard_map/pallas_call | solution.py:26
  8.7 2.3 %collective-permute-done.refs_0_ = bf16[704,128]{1,0:T(8,128)(2,1)S(1)} collective-permute-done((bf16[704,128]{1,0:T(8,128)(2,1)S(1)}, bf16[704,128]{1,0:T(8,128)(2,1)S(1)}, u32[]{:S(2)}, u32[]{:S(2)}) %collective-permute-start) | collective-permute-done | bytes 180256 | tf_op jit(solution)/shard_map/ppermute | solution.py:439
  11.0 0.0 collective-permute-start.1
  11.0 3.3 %collective-permute-done.3.refs_0_.refs_1_ = bf16[704,128]{1,0:T(8,128)(2,1)S(1)} collective-permute-done((bf16[704,128]{1,0:T(8,128)(2,1)S(1)}, bf16[704,128]{1,0:T(8,128)(2,1)S(1)}, u32[]{:S(2)}, u32[]{:S(2)}) %collective-permute-start.3) | collective-permute-done | bytes 180256 | tf_op jit(solution)/shard_map/ppermute | solution.py:439
  14.3 0.0 collective-permute-start.5
  14.3 0.0 collective-permute-done.4.refs_1_.refs_2_
  14.3 0.5 collective-permute-start.6
  14.8 2.1 %shard_map.96.refs_3_ = f32[1,128,256]{2,1,0:T(8,128)S(1)} custom-call(bf16[128,18432]{1,0:T(8,128)(2,1)S(1)} %get-tuple-element.30.query_ref, f32[32,128,128]{2,1,0:T(8,128)S(1)} %get-tuple-element.31.off_ref, bf16[704,128]{1,0:T(8,128)(2,1)S(1)} %collective-permute-done.3.refs_0_.refs_1_, bf16[704,128]{1,0:T(8,128)(2,1)S(1)} %collective-permute-done.4.refs_1_.refs_2_), custom_call_target="tpu_custom_call" | custom-call | flops 1207959552 | tf_op jit(solution)/shard_map/pallas_call | solution.py:26
  16.9 0.0 collective-permute-done.2.refs_1_.refs_3_
  16.9 2.1 %shard_map.95.refs_2_ = f32[1,128,256]{2,1,0:T(8,128)S(1)} custom-call(bf16[128,18432]{1,0:T(8,128)(2,1)S(1)} %get-tuple-element.30.query_ref, f32[32,128,128]{2,1,0:T(8,128)S(1)} %get-tuple-element.31.off_ref, bf16[704,128]{1,0:T(8,128)(2,1)S(1)} %pad_maximum_fusion.refs_0_, bf16[704,128]{1,0:T(8,128)(2,1)S(1)} %collective-permute-done.2.refs_1_.refs_3_), custom_call_target="tpu_custom_call" | custom-call | flops 1207959552 | tf_op jit(solution)/shard_map/pallas_call | solution.py:26
  19.1 0.0 collective-permute-done.5.refs_0_.refs_4_
  19.1 0.0 collective-permute-done.6.refs_1_.refs_5_
  19.1 2.1 %shard_map.97.refs_4_ = f32[1,128,256]{2,1,0:T(8,128)S(1)} custom-call(bf16[128,18432]{1,0:T(8,128)(2,1)S(1)} %get-tuple-element.30.query_ref, f32[32,128,128]{2,1,0:T(8,128)S(1)} %get-tuple-element.31.off_ref, bf16[704,128]{1,0:T(8,128)(2,1)S(1)} %collective-permute-done.5.refs_0_.refs_4_, bf16[704,128]{1,0:T(8,128)(2,1)S(1)} %collective-permute-done.6.refs_1_.refs_5_), custom_call_target="tpu_custom_call" | custom-call | flops 1207959552 | tf_op jit(solution)/shard_map/pallas_call | solution.py:26
  21.2 0.0 copy-start
  21.2 0.0 collective-permute-done.1.refs_1_
  21.2 2.2 %shard_map.98 = (f32[32,1024]{1,0:T(8,128)S(1)}, bf16[32,1024]{1,0:T(8,128)(2,1)S(1)}, bf16[32,1024]{1,0:T(8,128)(2,1)S(1)}, bf16[32,1024]{1,0:T(8,128)(2,1)S(1)}) custom-call(bf16[128,18432]{1,0:T(8,128)(2,1)S(1)} %get-tuple-element.30.query_ref, f32[32,128,128]{2,1,0:T(8,128)S(1)} %get-tuple-element.31.off_ref, ...), custom_call_target="tpu_custom_call" | custom-call | flops 1207959552 | tf_op jit(solution)/shard_map/pallas_call | solution.py:26
  23.4 1.6 %collective-permute-start.7 = (bf16[32,1024]{1,0:T(8,128)(2,1)S(1)}, bf16[32,1024]{1,0:T(8,128)(2,1)S(1)}, u32[]{:S(2)}, u32[]{:S(2)}) collective-permute-start(bf16[32,1024]{1,0:T(8,128)(2,1)S(1)} %get-tuple-element.33), channel_id=1, source_target_pairs={{0,1},{1,0},{2,3},{3,2},{4,5},{5,4},{6,7},{7,6},{8,9},{9,8},{10,11... | collective-permute-start | bytes 196616 | tf_op jit(solution)/shard_map/ppermute | solution.py:445
  25.1 2.6 %collective-permute-start.8 = (bf16[32,1024]{1,0:T(8,128)(2,1)S(1)}, bf16[32,1024]{1,0:T(8,128)(2,1)S(1)}, u32[]{:S(2)}, u32[]{:S(2)}) collective-permute-start(bf16[32,1024]{1,0:T(8,128)(2,1)S(1)} %get-tuple-element.34), channel_id=1, source_target_pairs={{0,2},{1,3},{2,0},{3,1},{4,6},{5,7},{6,4},{7,5},{8,10},{9,11},{10,... | collective-permute-start | bytes 196616 | tf_op jit(solution)/shard_map/ppermute | solution.py:445
  27.6 0.2 collective-permute-start.9
  27.9 0.0 copy-done
  27.9 2.2 %shard_map.99 = (f32[64,32,768]{2,1,0:T(8,128)S(1)}, f32[32,768]{1,0:T(8,128)S(1)}, bf16[768,128]{1,0:T(8,128)(2,1)S(1)}) custom-call(bf16[32,8192]{1,0:T(8,128)(2,1)S(1)} %copy-done, f32[64,32,128]{2,1,0:T(8,128)S(1)} %get-tuple-element.36.scale_ref.refs_7_.refs_3_, bf16[704,128]{1,0:T(8,128)(2,1)S(1)} %pad_maximum_fusion.refs_0_, ...), custom_call_target="tpu_custom_call" | custom-call | flops 1207959552 | tf_op jit(solution)/shard_map/pallas_call | solution.py:26
  30.1 1.8 %shard_map.100 = (f32[64,32,256]{2,1,0:T(8,128)S(1)}, f32[32,1024]{1,0:T(8,128)S(1)}, bf16[1024,128]{1,0:T(8,128)(2,1)S(1)}) custom-call(bf16[32,8192]{1,0:T(8,128)(2,1)S(1)} %copy-done, f32[64,32,128]{2,1,0:T(8,128)S(1)} %get-tuple-element.36.scale_ref.refs_7_.refs_3_, f32[32,128]{1,0:T(8,128)S(1)} %get-tuple-element.37.low_ref, ...), custom_call_target="tpu_custom_call" | custom-call | flops 536870912 | tf_op jit(solution)/shard_map/pallas_call | solution.py:26
  31.9 0.0 collective-permute-done.7.refs_1_
  31.9 0.6 %collective-permute-done.8.refs_2_ = bf16[32,1024]{1,0:T(8,128)(2,1)S(1)} collective-permute-done((bf16[32,1024]{1,0:T(8,128)(2,1)S(1)}, bf16[32,1024]{1,0:T(8,128)(2,1)S(1)}, u32[]{:S(2)}, u32[]{:S(2)}) %collective-permute-start.8) | collective-permute-done | bytes 65568 | tf_op jit(solution)/shard_map/ppermute | solution.py:445
  32.5 1.3 %collective-permute-done.9.refs_3_ = bf16[32,1024]{1,0:T(8,128)(2,1)S(1)} collective-permute-done((bf16[32,1024]{1,0:T(8,128)(2,1)S(1)}, bf16[32,1024]{1,0:T(8,128)(2,1)S(1)}, u32[]{:S(2)}, u32[]{:S(2)}) %collective-permute-start.9) | collective-permute-done | bytes 65568 | tf_op jit(solution)/shard_map/ppermute | solution.py:445
  33.8 2.1 %shard_map.101 = (f32[32,1024]{1,0:T(8,128)S(1)}, bf16[2048,512]{1,0:T(8,128)(2,1)S(1)}, f32[512,128]{1,0:T(8,128)S(1)}) custom-call(f32[32,1024]{1,0:T(8,128)S(1)} %get-tuple-element.32.refs_0_, bf16[32,1024]{1,0:T(8,128)(2,1)S(1)} %collective-permute-done.7.refs_1_, bf16[32,1024]{1,0:T(8,128)(2,1)S(1)} %collective-permute-done.8.refs_2_, ...), custom_call_target="tpu_custom_call" | custom-call | flops 1073741824 | tf_op jit(solution)/shard_map/pallas_call | solution.py:26
  35.9 0.1 collective-permute-start.10
  36.0 2.0 %shard_map.102 = (bf16[2048,512]{1,0:T(8,128)(2,1)S(1)}, f32[512,128]{1,0:T(8,128)S(1)}) custom-call(f32[32,1024]{1,0:T(8,128)S(1)} %get-tuple-element.43.refs_0_.gap_ref, f32[64,32,768]{2,1,0:T(8,128)S(1)} %get-tuple-element.41.refs_5_.refs_1_.refs_0_, f32[64,32,256]{2,1,0:T(8,128)S(1)} %get-tuple-element.42.refs_6_.refs_2_.refs_1_, ...), custom_call_target="tpu_custom_call" | custom-call | flops 1073741824 | tf_op jit(solution)/shard_map/pallas_call | solution.py:26
  38.0 0.0 collective-permute-done.10.come_ref
  38.0 1.6 %collective-permute-start.11 = (bf16[128,128]{1,0:T(8,128)(2,1)S(1)}, bf16[128,128]{1,0:T(8,128)(2,1)S(1)}, u32[]{:S(2)}, u32[]{:S(2)}) collective-permute-start(bf16[128,128]{1,0:T(8,128)(2,1)S(1)} %get-tuple-element.50), channel_id=1, source_target_pairs={{0,8},{4,12},{8,0},{12,4},{16,24},{20,28},{24,16},{28,20},{1,9},{5... | collective-permute-start | bytes 98312 | tf_op jit(solution)/shard_map/ppermute | solution.py:439
  39.6 0.8 %collective-permute-start.12 = (bf16[128,128]{1,0:T(8,128)(2,1)S(1)}, bf16[128,128]{1,0:T(8,128)(2,1)S(1)}, u32[]{:S(2)}, u32[]{:S(2)}) collective-permute-start(bf16[128,128]{1,0:T(8,128)(2,1)S(1)} %get-tuple-element.51), channel_id=1, source_target_pairs={{0,16},{4,20},{8,24},{12,28},{16,0},{20,4},{24,8},{28,12},{1,17},{... | collective-permute-start | bytes 98312 | tf_op jit(solution)/shard_map/ppermute | solution.py:439
  40.4 1.2 %collective-permute-start.13 = (bf16[128,128]{1,0:T(8,128)(2,1)S(1)}, bf16[128,128]{1,0:T(8,128)(2,1)S(1)}, u32[]{:S(2)}, u32[]{:S(2)}) collective-permute-start(bf16[128,128]{1,0:T(8,128)(2,1)S(1)} %get-tuple-element.52), channel_id=1, source_target_pairs={{0,24},{4,28},{8,16},{12,20},{16,8},{20,12},{24,0},{28,4},{1,25},{... | collective-permute-start | bytes 98312 | tf_op jit(solution)/shard_map/ppermute | solution.py:439
  41.6 1.8 %shard_map.104 = f32[32,64]{1,0:T(8,128)} custom-call(f32[32,1024]{1,0:T(8,128)S(1)} %get-tuple-element.43.refs_0_.gap_ref, f32[64,32,768]{2,1,0:T(8,128)S(1)} %get-tuple-element.41.refs_5_.refs_1_.refs_0_, f32[64,32,256]{2,1,0:T(8,128)S(1)} %get-tuple-element.42.refs_6_.refs_2_.refs_1_), custom_call_target="tpu_custom_call" | custom-call | flops 1073741824 | tf_op jit(solution)/shard_map/pallas_call | solution.py:26
  43.4 0.0 collective-permute-done.11.refs_0_
  43.4 0.1 collective-permute-done.12.refs_1_
  43.5 1.7 %collective-permute-done.13.refs_2_ = bf16[128,128]{1,0:T(8,128)(2,1)S(1)} collective-permute-done((bf16[128,128]{1,0:T(8,128)(2,1)S(1)}, bf16[128,128]{1,0:T(8,128)(2,1)S(1)}, u32[]{:S(2)}, u32[]{:S(2)}) %collective-permute-start.13) | collective-permute-done | bytes 32800 | tf_op jit(solution)/shard_map/ppermute | solution.py:439
  45.3 2.5 %collective-permute-start.16 = (f32[32,128]{1,0:T(8,128)S(1)}, f32[32,128]{1,0:T(8,128)S(1)}, u32[]{:S(2)}, u32[]{:S(2)}) collective-permute-start(f32[32,128]{1,0:T(8,128)S(1)} %get-tuple-element.56), channel_id=1, source_target_pairs={{0,3},{1,2},{2,1},{3,0},{4,7},{5,6},{6,5},{7,4},{8,11},{9,10},{10,... | collective-permute-start | bytes 49160 | tf_op jit(solution)/shard_map/ppermute | solution.py:445
  47.8 0.3 collective-permute-start.15
  48.1 1.6 %collective-permute-start.14 = (f32[32,128]{1,0:T(8,128)S(1)}, f32[32,128]{1,0:T(8,128)S(1)}, u32[]{:S(2)}, u32[]{:S(2)}) collective-permute-start(f32[32,128]{1,0:T(8,128)S(1)} %get-tuple-element.54), channel_id=1, source_target_pairs={{0,1},{1,0},{2,3},{3,2},{4,5},{5,4},{6,7},{7,6},{8,9},{9,8},{10,11... | collective-permute-start | bytes 49160 | tf_op jit(solution)/shard_map/ppermute | solution.py:445
  49.7 3.3 %shard_map.103 = f32[32,8192]{1,0:T(8,128)} custom-call(bf16[2048,512]{1,0:T(8,128)(2,1)S(1)} %get-tuple-element.44.even_ref, bf16[2048,512]{1,0:T(8,128)(2,1)S(1)} %get-tuple-element.45.odd_ref, bf16[1024,128]{1,0:T(8,128)(2,1)S(1)} %get-tuple-element.46.keys_ref), custom_call_target="tpu_custom_call" | custom-call | flops 1073741824 | tf_op jit(solution)/shard_map/pallas_call | solution.py:26
  53.0 0.0 collective-permute-done.16
  53.0 0.0 collective-permute-done.15
  53.0 0.0 collective-permute-done.14
  53.0 0.6 %add_add_fusion = f32[32,128]{1,0:T(8,128)} fusion(f32[32,128]{1,0:T(8,128)S(1)} %collective-permute-done.16, f32[32,128]{1,0:T(8,128)S(1)} %collective-permute-done.15, f32[32,128]{1,0:T(8,128)S(1)} %get-tuple-element.53, f32[32,128]{1,0:T(8,128)S(1)} %collective-permute-done.14), kind=kLoop, calls=%fused_computation.1 | loop fusion | flops 12288 | bytes 81920 | tf_op jit(solution)/shard_map/add | solution.py:493
  (2 shorter events, 0.1 us)
Async XLA Ops:
  1.6 9.4 %collective-permute-start = (bf16[704,128]{1,0:T(8,128)(2,1)S(1)}, bf16[704,128]{1,0:T(8,128)(2,1)S(1)}, u32[]{:S(2)}, u32[]{:S(2)}) collective-permute-start(bf16[704,128]{1,0:T(8,128)(2,1)S(1)} %pad_maximum_fusion.refs_0_), channel_id=1, source_target_pairs={{0,24},{4,28},{8,16},{12,20},{16,8},{20,12},{24,0},{28,4},{1,25},{... | collective-permute-start | bytes 540680 | tf_op jit(solution)/shard_map/ppermute | solution.py:439
  5.6 8.7 %collective-permute-start.3 = (bf16[704,128]{1,0:T(8,128)(2,1)S(1)}, bf16[704,128]{1,0:T(8,128)(2,1)S(1)}, u32[]{:S(2)}, u32[]{:S(2)}) collective-permute-start(bf16[704,128]{1,0:T(8,128)(2,1)S(1)} %pad_maximum_fusion.refs_0_), channel_id=1, source_target_pairs={{0,8},{4,12},{8,0},{12,4},{16,24},{20,28},{24,16},{28,20},{1,9},{5... | collective-permute-start | bytes 540680 | tf_op jit(solution)/shard_map/ppermute | solution.py:439
  6.1 8.2 %collective-permute-start.4 = (bf16[704,128]{1,0:T(8,128)(2,1)S(1)}, bf16[704,128]{1,0:T(8,128)(2,1)S(1)}, u32[]{:S(2)}, u32[]{:S(2)}) collective-permute-start(bf16[704,128]{1,0:T(8,128)(2,1)S(1)} %pad_maximum_fusion.refs_0_), channel_id=1, source_target_pairs={{0,16},{4,20},{8,24},{12,28},{16,0},{20,4},{24,8},{28,12},{1,17},{... | collective-permute-start | bytes 540680 | tf_op jit(solution)/shard_map/ppermute | solution.py:439
  6.2 10.7 %collective-permute-start.2 = (bf16[704,128]{1,0:T(8,128)(2,1)S(1)}, bf16[704,128]{1,0:T(8,128)(2,1)S(1)}, u32[]{:S(2)}, u32[]{:S(2)}) collective-permute-start(bf16[704,128]{1,0:T(8,128)(2,1)S(1)} %pad_maximum_fusion.refs_0_), channel_id=1, source_target_pairs={{0,4},{4,0},{8,12},{12,8},{16,20},{20,16},{24,28},{28,24},{1,5},{5... | collective-permute-start | bytes 540680 | tf_op jit(solution)/shard_map/ppermute | solution.py:439
  11.0 10.3 %collective-permute-start.1 = (bf16[704,128]{1,0:T(8,128)(2,1)S(1)}, bf16[704,128]{1,0:T(8,128)(2,1)S(1)}, u32[]{:S(2)}, u32[]{:S(2)}) collective-permute-start(bf16[704,128]{1,0:T(8,128)(2,1)S(1)} %collective-permute-done.refs_0_), channel_id=1, source_target_pairs={{0,4},{4,0},{8,12},{12,8},{16,20},{20,16},{24,28},{28,24},{1,5},{5... | collective-permute-start | bytes 540680 | tf_op jit(solution)/shard_map/ppermute | solution.py:439
  14.3 4.8 %collective-permute-start.5 = (bf16[704,128]{1,0:T(8,128)(2,1)S(1)}, bf16[704,128]{1,0:T(8,128)(2,1)S(1)}, u32[]{:S(2)}, u32[]{:S(2)}) collective-permute-start(bf16[704,128]{1,0:T(8,128)(2,1)S(1)} %collective-permute-done.3.refs_0_.refs_1_), channel_id=1, source_target_pairs={{0,4},{4,0},{8,12},{12,8},{16,20},{20,16},{24,28},{28,24},{1,5},{5... | collective-permute-start | bytes 540680 | tf_op jit(solution)/shard_map/ppermute | solution.py:439
  14.3 4.8 %collective-permute-start.6 = (bf16[704,128]{1,0:T(8,128)(2,1)S(1)}, bf16[704,128]{1,0:T(8,128)(2,1)S(1)}, u32[]{:S(2)}, u32[]{:S(2)}) collective-permute-start(bf16[704,128]{1,0:T(8,128)(2,1)S(1)} %collective-permute-done.4.refs_1_.refs_2_), channel_id=1, source_target_pairs={{0,4},{4,0},{8,12},{12,8},{16,20},{20,16},{24,28},{28,24},{1,5},{5... | collective-permute-start | bytes 540680 | tf_op jit(solution)/shard_map/ppermute | solution.py:439
  21.2 6.7 %copy-start = (bf16[32,8192]{1,0:T(8,128)(2,1)S(1)}, bf16[32,8192]{1,0:T(8,128)(2,1)}, u32[]{:S(2)}) copy-start(bf16[32,8192]{1,0:T(8,128)(2,1)} %refs_4_.1) | copy-start | bytes 1572868
  23.4 8.4 %collective-permute-start.7 = (bf16[32,1024]{1,0:T(8,128)(2,1)S(1)}, bf16[32,1024]{1,0:T(8,128)(2,1)S(1)}, u32[]{:S(2)}, u32[]{:S(2)}) collective-permute-start(bf16[32,1024]{1,0:T(8,128)(2,1)S(1)} %get-tuple-element.33), channel_id=1, source_target_pairs={{0,1},{1,0},{2,3},{3,2},{4,5},{5,4},{6,7},{7,6},{8,9},{9,8},{10,11... | collective-permute-start | bytes 196616 | tf_op jit(solution)/shard_map/ppermute | solution.py:445
  25.1 7.5 %collective-permute-start.8 = (bf16[32,1024]{1,0:T(8,128)(2,1)S(1)}, bf16[32,1024]{1,0:T(8,128)(2,1)S(1)}, u32[]{:S(2)}, u32[]{:S(2)}) collective-permute-start(bf16[32,1024]{1,0:T(8,128)(2,1)S(1)} %get-tuple-element.34), channel_id=1, source_target_pairs={{0,2},{1,3},{2,0},{3,1},{4,6},{5,7},{6,4},{7,5},{8,10},{9,11},{10,... | collective-permute-start | bytes 196616 | tf_op jit(solution)/shard_map/ppermute | solution.py:445
  27.6 6.2 %collective-permute-start.9 = (bf16[32,1024]{1,0:T(8,128)(2,1)S(1)}, bf16[32,1024]{1,0:T(8,128)(2,1)S(1)}, u32[]{:S(2)}, u32[]{:S(2)}) collective-permute-start(bf16[32,1024]{1,0:T(8,128)(2,1)S(1)} %get-tuple-element.35), channel_id=1, source_target_pairs={{0,3},{1,2},{2,1},{3,0},{4,7},{5,6},{6,5},{7,4},{8,11},{9,10},{10,... | collective-permute-start | bytes 196616 | tf_op jit(solution)/shard_map/ppermute | solution.py:445
  35.9 2.1 %collective-permute-start.10 = (f32[512,128]{1,0:T(8,128)S(1)}, f32[512,128]{1,0:T(8,128)S(1)}, u32[]{:S(2)}, u32[]{:S(2)}) collective-permute-start(f32[512,128]{1,0:T(8,128)S(1)} %get-tuple-element.48), channel_id=1, source_target_pairs={{0,4},{4,0},{8,12},{12,8},{16,20},{20,16},{24,28},{28,24},{1,5},{5... | collective-permute-start | bytes 786440 | tf_op jit(solution)/shard_map/ppermute | solution.py:439
  38.0 5.4 %collective-permute-start.11 = (bf16[128,128]{1,0:T(8,128)(2,1)S(1)}, bf16[128,128]{1,0:T(8,128)(2,1)S(1)}, u32[]{:S(2)}, u32[]{:S(2)}) collective-permute-start(bf16[128,128]{1,0:T(8,128)(2,1)S(1)} %get-tuple-element.50), channel_id=1, source_target_pairs={{0,8},{4,12},{8,0},{12,4},{16,24},{20,28},{24,16},{28,20},{1,9},{5... | collective-permute-start | bytes 98312 | tf_op jit(solution)/shard_map/ppermute | solution.py:439
  39.6 3.9 %collective-permute-start.12 = (bf16[128,128]{1,0:T(8,128)(2,1)S(1)}, bf16[128,128]{1,0:T(8,128)(2,1)S(1)}, u32[]{:S(2)}, u32[]{:S(2)}) collective-permute-start(bf16[128,128]{1,0:T(8,128)(2,1)S(1)} %get-tuple-element.51), channel_id=1, source_target_pairs={{0,16},{4,20},{8,24},{12,28},{16,0},{20,4},{24,8},{28,12},{1,17},{... | collective-permute-start | bytes 98312 | tf_op jit(solution)/shard_map/ppermute | solution.py:439
  40.4 4.8 %collective-permute-start.13 = (bf16[128,128]{1,0:T(8,128)(2,1)S(1)}, bf16[128,128]{1,0:T(8,128)(2,1)S(1)}, u32[]{:S(2)}, u32[]{:S(2)}) collective-permute-start(bf16[128,128]{1,0:T(8,128)(2,1)S(1)} %get-tuple-element.52), channel_id=1, source_target_pairs={{0,24},{4,28},{8,16},{12,20},{16,8},{20,12},{24,0},{28,4},{1,25},{... | collective-permute-start | bytes 98312 | tf_op jit(solution)/shard_map/ppermute | solution.py:439
  45.3 7.7 %collective-permute-start.16 = (f32[32,128]{1,0:T(8,128)S(1)}, f32[32,128]{1,0:T(8,128)S(1)}, u32[]{:S(2)}, u32[]{:S(2)}) collective-permute-start(f32[32,128]{1,0:T(8,128)S(1)} %get-tuple-element.56), channel_id=1, source_target_pairs={{0,3},{1,2},{2,1},{3,0},{4,7},{5,6},{6,5},{7,4},{8,11},{9,10},{10,... | collective-permute-start | bytes 49160 | tf_op jit(solution)/shard_map/ppermute | solution.py:445
  47.8 5.2 %collective-permute-start.15 = (f32[32,128]{1,0:T(8,128)S(1)}, f32[32,128]{1,0:T(8,128)S(1)}, u32[]{:S(2)}, u32[]{:S(2)}) collective-permute-start(f32[32,128]{1,0:T(8,128)S(1)} %get-tuple-element.55), channel_id=1, source_target_pairs={{0,2},{1,3},{2,0},{3,1},{4,6},{5,7},{6,4},{7,5},{8,10},{9,11},{10,... | collective-permute-start | bytes 49160 | tf_op jit(solution)/shard_map/ppermute | solution.py:445
  48.1 4.9 %collective-permute-start.14 = (f32[32,128]{1,0:T(8,128)S(1)}, f32[32,128]{1,0:T(8,128)S(1)}, u32[]{:S(2)}, u32[]{:S(2)}) collective-permute-start(f32[32,128]{1,0:T(8,128)S(1)} %get-tuple-element.54), channel_id=1, source_target_pairs={{0,1},{1,0},{2,3},{3,2},{4,5},{5,4},{6,7},{7,6},{8,9},{9,8},{10,11... | collective-permute-start | bytes 49160 | tf_op jit(solution)/shard_map/ppermute | solution.py:445

commit v2 on v0

--- a/solution.py
+++ b/solution.py
@@ -92,7 +92,7 @@
     outs, (keys, acc) = refs[:-2], refs[-2:]
     tiles, local_rows, wide = acc.shape
     heads = off_ref.shape[0]
-    group = min(16, heads)
+    group = min(32, heads)
     depth = KDIM + PAD
     per_tile = wide // LANES
     for tile in range(tiles):
@@ -179,7 +179,7 @@
     active_ref, predicted_ref, keys, score = refs[slots:]
     index_heads, rows, seq_total = active_ref.shape
     dims = keys.shape[1]
-    group = min(8, index_heads)
+    group = min(64, index_heads)
     score[...] = jnp.zeros_like(score)
     for place in range(slots):
         keys[lanes_of(place)] = blocks[place][KDIM:]
@@ -259,7 +259,7 @@
     index_heads, rows, _ = active_ref.shape
     dims, columns = tall.shape
     lanes = slice(half * columns, (half + 1) * columns)
-    group = min(8, index_heads)
+    group = min(64, index_heads)
     tall[...] = jnp.zeros_like(tall)
 
     @pl.loop(0, index_heads // group)
@@ -308,7 +308,7 @@
 def query_kernel(factor, gap_ref, even_ref, odd_ref, active_ref, keys_ref, grad_query_ref, grad_weight_ref, sums):
     index_heads, rows, seq_total = active_ref.shape
     dims = keys_ref.shape[1]
-    group = min(8, index_heads)
+    group = min(64, index_heads)
     lane = lax.broadcasted_iota(jnp.int32, (rows, LANES), 1)
     sums[...] = jnp.zeros_like(sums)
 

time: 53 us -> 50.7 us (0.957)
  Pallas kernels: 21.1 us -> 16.6 us
  waiting for transfers between devices: 11.3 us -> 13.5 us
    pallas_call x11, Pallas kernels: 21.1 us -> 16.6 us  [call(): pl.pallas_call(body, out_shape=out_shape, in_specs=specs or [VMEM] * len(...]
    ppermute x6, waiting for transfers between devices: 1.32 us -> 2.97 us  [pass_on(): out.append(lax.ppermute(value, 'head', to))]
    ppermute x11, waiting for transfers between devices: 9.99 us -> 10.6 us  [swap(): lax.ppermute(value, 'seq', [(place, place ^ bits) for place in range(seq_...]
  transfers between devices with their start and end apart: 17 -> 17, of which waited for: 8 -> 10; matrix products, arithmetic and copies ran while one was open for 0% -> 0% of each run, Pallas kernels for 32% -> 27%
where the time goes in v2:
time: 50.7 us; the launch traced here: 50.6 us
  starting transfers between devices  18.1 us (36%)
  Pallas kernels  16.6 us (33%)
  waiting for transfers between devices  13.5 us (27%)
  other arithmetic  1.56 us (3%)
  between operations  0.77 us (2%)
    pallas_call x11, Pallas kernels, call(): pl.pallas_call(body, out_shape=out_shape, in_specs=specs or [VMEM] * len(...  16.6 us
    ppermute x11, waiting for transfers between devices, swap(): lax.ppermute(value, 'seq', [(place, place ^ bits) for place in range(seq_...  10.6 us
    ppermute x6, starting transfers between devices, pass_on(): out.append(lax.ppermute(value, 'head', to))  9.84 us
    ppermute x11, starting transfers between devices, swap(): lax.ppermute(value, 'seq', [(place, place ^ bits) for place in range(seq_...  8.26 us
    ppermute x6, waiting for transfers between devices, pass_on(): out.append(lax.ppermute(value, 'head', to))  2.97 us
  transfers between devices with their start and end apart: 17, of which 10 were waited for; matrix products, arithmetic and copies ran while one was open for 0% of the time, Pallas kernels for 27%

profile of v2, /device:TPU:0, one launch (start us, length us, event | category | flops | bytes accessed | tf_op | source)
XLA Modules:
  0.0 50.6 jit_solution(1433069985984001150)
XLA Ops:
  0.6 0.9 %pad_maximum_fusion.refs_0_ = bf16[704,128]{1,0:T(8,128)(2,1)S(1)} fusion(bf16[128,128]{1,0:T(8,128)(2,1)} %param.12, bf16[576,128]{1,0:T(8,128)(2,1)} %bitcast.2), kind=kLoop, calls=%fused_computation | loop fusion | flops 360448 | bytes 360448 | tf_op jit(solution)/shard_map/concatenate | solution.py:385
  1.6 3.1 %collective-permute-start.4 = (bf16[704,128]{1,0:T(8,128)(2,1)S(1)}, bf16[704,128]{1,0:T(8,128)(2,1)S(1)}, u32[]{:S(2)}, u32[]{:S(2)}) collective-permute-start(bf16[704,128]{1,0:T(8,128)(2,1)S(1)} %pad_maximum_fusion.refs_0_), channel_id=1, source_target_pairs={{0,16},{4,20},{8,24},{12,28},{16,0},{20,4},{24,8},{28,12},{1,17},{... | collective-permute-start | bytes 540680 | tf_op jit(solution)/shard_map/ppermute | solution.py:376
  4.6 1.5 %collective-permute-start.3 = (bf16[704,128]{1,0:T(8,128)(2,1)S(1)}, bf16[704,128]{1,0:T(8,128)(2,1)S(1)}, u32[]{:S(2)}, u32[]{:S(2)}) collective-permute-start(bf16[704,128]{1,0:T(8,128)(2,1)S(1)} %pad_maximum_fusion.refs_0_), channel_id=1, source_target_pairs={{0,8},{4,12},{8,0},{12,4},{16,24},{20,28},{24,16},{28,20},{1,9},{5... | collective-permute-start | bytes 540680 | tf_op jit(solution)/shard_map/ppermute | solution.py:376
  6.1 0.0 collective-permute-start
  6.2 0.0 collective-permute-start.2
  6.2 2.4 %shard_map.94 = (bf16[128,18432]{1,0:T(8,128)(2,1)S(1)}, f32[32,128,128]{2,1,0:T(8,128)S(1)}, f32[64,32,128]{2,1,0:T(8,128)S(1)}, f32[32,128]{1,0:T(8,128)S(1)}) custom-call(bf16[128,18432]{1,0:T(8,128)(2,1)} %query_hbm.1, f32[128,128]{1,0:T(8,128)} %norm_hbm.1, f32[32,64]{1,0:T(8,128)} %weight_hbm.1, s32[1,128]{1,0:T(1,128)} %bitcast.3), custom_call_target="tpu_custom_call" | custom-call | flops 1500000000 | tf_op jit(solution)/shard_map/pallas_call | solution.py:26
  8.6 0.6 %collective-permute-done.4.refs_1_.refs_2_ = bf16[704,128]{1,0:T(8,128)(2,1)S(1)} collective-permute-done((bf16[704,128]{1,0:T(8,128)(2,1)S(1)}, bf16[704,128]{1,0:T(8,128)(2,1)S(1)}, u32[]{:S(2)}, u32[]{:S(2)}) %collective-permute-start.4) | collective-permute-done | bytes 180256 | tf_op jit(solution)/shard_map/ppermute | solution.py:376
  9.2 0.0 collective-permute-start.6
  9.2 2.8 %collective-permute-done.3.refs_0_.refs_1_ = bf16[704,128]{1,0:T(8,128)(2,1)S(1)} collective-permute-done((bf16[704,128]{1,0:T(8,128)(2,1)S(1)}, bf16[704,128]{1,0:T(8,128)(2,1)S(1)}, u32[]{:S(2)}, u32[]{:S(2)}) %collective-permute-start.3) | collective-permute-done | bytes 180256 | tf_op jit(solution)/shard_map/ppermute | solution.py:376
  12.1 0.0 collective-permute-start.5
  12.1 2.2 %collective-permute-done.refs_0_.refs_3_ = bf16[704,128]{1,0:T(8,128)(2,1)S(1)} collective-permute-done((bf16[704,128]{1,0:T(8,128)(2,1)S(1)}, bf16[704,128]{1,0:T(8,128)(2,1)S(1)}, u32[]{:S(2)}, u32[]{:S(2)}) %collective-permute-start) | collective-permute-done | bytes 180256 | tf_op jit(solution)/shard_map/ppermute | solution.py:376
  14.3 0.0 collective-permute-start.1
  14.3 2.0 %shard_map.96.refs_3_ = f32[1,128,256]{2,1,0:T(8,128)S(1)} custom-call(bf16[128,18432]{1,0:T(8,128)(2,1)S(1)} %get-tuple-element.29.query_ref, f32[32,128,128]{2,1,0:T(8,128)S(1)} %get-tuple-element.30.off_ref, bf16[704,128]{1,0:T(8,128)(2,1)S(1)} %collective-permute-done.3.refs_0_.refs_1_, bf16[704,128]{1,0:T(8,128)(2,1)S(1)} %collective-permute-done.4.refs_1_.refs_2_), custom_call_target="tpu_custom_call" | custom-call | flops 1207959552 | tf_op jit(solution)/shard_map/pallas_call | solution.py:26
  16.3 0.0 collective-permute-done.2.refs_1_.refs_4_
  16.4 2.0 %shard_map.95.refs_2_ = f32[1,128,256]{2,1,0:T(8,128)S(1)} custom-call(bf16[128,18432]{1,0:T(8,128)(2,1)S(1)} %get-tuple-element.29.query_ref, f32[32,128,128]{2,1,0:T(8,128)S(1)} %get-tuple-element.30.off_ref, bf16[704,128]{1,0:T(8,128)(2,1)S(1)} %pad_maximum_fusion.refs_0_, bf16[704,128]{1,0:T(8,128)(2,1)S(1)} %collective-permute-done.2.refs_1_.refs_4_), custom_call_target="tpu_custom_call" | custom-call | flops 1207959552 | tf_op jit(solution)/shard_map/pallas_call | solution.py:26
  18.4 0.0 collective-permute-done.6.refs_1_.refs_6_
  18.4 0.0 collective-permute-done.5.refs_0_.refs_5_
  18.4 2.0 %shard_map.97.refs_4_ = f32[1,128,256]{2,1,0:T(8,128)S(1)} custom-call(bf16[128,18432]{1,0:T(8,128)(2,1)S(1)} %get-tuple-element.29.query_ref, f32[32,128,128]{2,1,0:T(8,128)S(1)} %get-tuple-element.30.off_ref, bf16[704,128]{1,0:T(8,128)(2,1)S(1)} %collective-permute-done.5.refs_0_.refs_5_, bf16[704,128]{1,0:T(8,128)(2,1)S(1)} %collective-permute-done.6.refs_1_.refs_6_), custom_call_target="tpu_custom_call" | custom-call | flops 1207959552 | tf_op jit(solution)/shard_map/pallas_call | solution.py:26
  20.5 0.0 copy-start
  20.5 0.0 collective-permute-done.1.refs_1_.refs_7_
  20.5 2.1 %shard_map.98 = (f32[32,1024]{1,0:T(8,128)S(1)}, bf16[32,1024]{1,0:T(8,128)(2,1)S(1)}, bf16[32,1024]{1,0:T(8,128)(2,1)S(1)}, bf16[32,1024]{1,0:T(8,128)(2,1)S(1)}) custom-call(bf16[128,18432]{1,0:T(8,128)(2,1)S(1)} %get-tuple-element.29.query_ref, f32[32,128,128]{2,1,0:T(8,128)S(1)} %get-tuple-element.30.off_ref, ...), custom_call_target="tpu_custom_call" | custom-call | flops 1207959552 | tf_op jit(solution)/shard_map/pallas_call | solution.py:26
  22.6 1.8 %collective-permute-start.7 = (bf16[32,1024]{1,0:T(8,128)(2,1)S(1)}, bf16[32,1024]{1,0:T(8,128)(2,1)S(1)}, u32[]{:S(2)}, u32[]{:S(2)}) collective-permute-start(bf16[32,1024]{1,0:T(8,128)(2,1)S(1)} %get-tuple-element.32), channel_id=1, source_target_pairs={{0,1},{1,2},{2,3},{3,0},{4,5},{5,6},{6,7},{7,4},{8,9},{9,10},{10,1... | collective-permute-start | bytes 196616 | tf_op jit(solution)/shard_map/ppermute | solution.py:382
  24.3 2.6 %collective-permute-start.8 = (bf16[32,1024]{1,0:T(8,128)(2,1)S(1)}, bf16[32,1024]{1,0:T(8,128)(2,1)S(1)}, u32[]{:S(2)}, u32[]{:S(2)}) collective-permute-start(bf16[32,1024]{1,0:T(8,128)(2,1)S(1)} %get-tuple-element.33), channel_id=1, source_target_pairs={{0,2},{1,3},{2,0},{3,1},{4,6},{5,7},{6,4},{7,5},{8,10},{9,11},{10,... | collective-permute-start | bytes 196616 | tf_op jit(solution)/shard_map/ppermute | solution.py:382
  26.9 1.4 %collective-permute-start.9 = (bf16[32,1024]{1,0:T(8,128)(2,1)S(1)}, bf16[32,1024]{1,0:T(8,128)(2,1)S(1)}, u32[]{:S(2)}, u32[]{:S(2)}) collective-permute-start(bf16[32,1024]{1,0:T(8,128)(2,1)S(1)} %get-tuple-element.34), channel_id=1, source_target_pairs={{0,3},{1,0},{2,1},{3,2},{4,7},{5,4},{6,5},{7,6},{8,11},{9,8},{10,9... | collective-permute-start | bytes 196616 | tf_op jit(solution)/shard_map/ppermute | solution.py:382
  28.3 0.0 copy-done
  28.3 1.5 %shard_map.99 = (f32[64,32,1024]{2,1,0:T(8,128)S(1)}, f32[32,1024]{1,0:T(8,128)S(1)}, bf16[1024,128]{1,0:T(8,128)(2,1)S(1)}) custom-call(bf16[32,8192]{1,0:T(8,128)(2,1)S(1)} %copy-done, f32[64,32,128]{2,1,0:T(8,128)S(1)} %get-tuple-element.35.scale_ref.refs_6_.refs_2_, f32[32,128]{1,0:T(8,128)S(1)} %get-tuple-element.36.low_ref, ...), custom_call_target="tpu_custom_call" | custom-call | flops 1610612736 | tf_op jit(solution)/shard_map/pallas_call | solution.py:26
  29.8 0.0 collective-permute-done.7.refs_1_
  29.8 2.3 %collective-permute-done.8.refs_2_ = bf16[32,1024]{1,0:T(8,128)(2,1)S(1)} collective-permute-done((bf16[32,1024]{1,0:T(8,128)(2,1)S(1)}, bf16[32,1024]{1,0:T(8,128)(2,1)S(1)}, u32[]{:S(2)}, u32[]{:S(2)}) %collective-permute-start.8) | collective-permute-done | bytes 65568 | tf_op jit(solution)/shard_map/ppermute | solution.py:382
  32.0 0.2 collective-permute-done.9.refs_3_
  32.3 1.1 %shard_map.100 = (f32[32,1024]{1,0:T(8,128)S(1)}, bf16[2048,512]{1,0:T(8,128)(2,1)S(1)}, f32[512,128]{1,0:T(8,128)S(1)}) custom-call(f32[32,1024]{1,0:T(8,128)S(1)} %get-tuple-element.31.refs_0_, bf16[32,1024]{1,0:T(8,128)(2,1)S(1)} %collective-permute-done.7.refs_1_, bf16[32,1024]{1,0:T(8,128)(2,1)S(1)} %collective-permute-done.8.refs_2_, ...), custom_call_target="tpu_custom_call" | custom-call | flops 1073741824 | tf_op jit(solution)/shard_map/pallas_call | solution.py:26
  33.3 0.1 collective-permute-start.10
  33.4 0.9 %shard_map.101 = (bf16[2048,512]{1,0:T(8,128)(2,1)S(1)}, f32[512,128]{1,0:T(8,128)S(1)}) custom-call(f32[32,1024]{1,0:T(8,128)S(1)} %get-tuple-element.39.refs_0_.gap_ref, f32[64,32,1024]{2,1,0:T(8,128)S(1)} %get-tuple-element.38.refs_5_.refs_1_.active_ref, f32[64,32,128]{2,1,0:T(8,128)S(1)} %get-tuple-element.35.scale_ref.refs_6_.refs_2_, ...), custom_call_target="tpu_custom_call" | custom-call | flops 1073741824 | tf_op jit(solution)/shard_map/pallas_call | solution.py:26
  34.4 0.6 %collective-permute-done.10.come_ref = f32[512,128]{1,0:T(8,128)S(1)} collective-permute-done((f32[512,128]{1,0:T(8,128)S(1)}, f32[512,128]{1,0:T(8,128)S(1)}, u32[]{:S(2)}, u32[]{:S(2)}) %collective-permute-start.10) | collective-permute-done | bytes 262176 | tf_op jit(solution)/shard_map/ppermute | solution.py:376
  35.0 1.6 %collective-permute-start.11 = (bf16[128,128]{1,0:T(8,128)(2,1)S(1)}, bf16[128,128]{1,0:T(8,128)(2,1)S(1)}, u32[]{:S(2)}, u32[]{:S(2)}) collective-permute-start(bf16[128,128]{1,0:T(8,128)(2,1)S(1)} %get-tuple-element.48), channel_id=1, source_target_pairs={{0,8},{4,12},{8,0},{12,4},{16,24},{20,28},{24,16},{28,20},{1,9},{5... | collective-permute-start | bytes 98312 | tf_op jit(solution)/shard_map/ppermute | solution.py:376
  36.5 1.5 %collective-permute-start.12 = (bf16[128,128]{1,0:T(8,128)(2,1)S(1)}, bf16[128,128]{1,0:T(8,128)(2,1)S(1)}, u32[]{:S(2)}, u32[]{:S(2)}) collective-permute-start(bf16[128,128]{1,0:T(8,128)(2,1)S(1)} %get-tuple-element.49), channel_id=1, source_target_pairs={{0,16},{4,20},{8,24},{12,28},{16,0},{20,4},{24,8},{28,12},{1,17},{... | collective-permute-start | bytes 98312 | tf_op jit(solution)/shard_map/ppermute | solution.py:376
  38.1 0.5 collective-permute-start.13
  38.5 0.4 collective-permute-done.11.refs_0_
  38.9 1.5 %collective-permute-done.12.refs_1_ = bf16[128,128]{1,0:T(8,128)(2,1)S(1)} collective-permute-done((bf16[128,128]{1,0:T(8,128)(2,1)S(1)}, bf16[128,128]{1,0:T(8,128)(2,1)S(1)}, u32[]{:S(2)}, u32[]{:S(2)}) %collective-permute-start.12) | collective-permute-done | bytes 32800 | tf_op jit(solution)/shard_map/ppermute | solution.py:376
  40.4 2.4 %collective-permute-done.13.refs_2_ = bf16[128,128]{1,0:T(8,128)(2,1)S(1)} collective-permute-done((bf16[128,128]{1,0:T(8,128)(2,1)S(1)}, bf16[128,128]{1,0:T(8,128)(2,1)S(1)}, u32[]{:S(2)}, u32[]{:S(2)}) %collective-permute-start.13) | collective-permute-done | bytes 32800 | tf_op jit(solution)/shard_map/ppermute | solution.py:376
  42.9 1.7 %collective-permute-start.14 = (f32[32,128]{1,0:T(8,128)S(1)}, f32[32,128]{1,0:T(8,128)S(1)}, u32[]{:S(2)}, u32[]{:S(2)}) collective-permute-start(f32[32,128]{1,0:T(8,128)S(1)} %get-tuple-element.52), channel_id=1, source_target_pairs={{0,1},{1,2},{2,3},{3,0},{4,5},{5,6},{6,7},{7,4},{8,9},{9,10},{10,1... | collective-permute-start | bytes 49160 | tf_op jit(solution)/shard_map/ppermute | solution.py:382
  44.6 1.6 %collective-permute-start.15 = (f32[32,128]{1,0:T(8,128)S(1)}, f32[32,128]{1,0:T(8,128)S(1)}, u32[]{:S(2)}, u32[]{:S(2)}) collective-permute-start(f32[32,128]{1,0:T(8,128)S(1)} %get-tuple-element.53), channel_id=1, source_target_pairs={{0,2},{1,3},{2,0},{3,1},{4,6},{5,7},{6,4},{7,5},{8,10},{9,11},{10,... | collective-permute-start | bytes 49160 | tf_op jit(solution)/shard_map/ppermute | solution.py:382
  46.2 0.8 %collective-permute-start.16 = (f32[32,128]{1,0:T(8,128)S(1)}, f32[32,128]{1,0:T(8,128)S(1)}, u32[]{:S(2)}, u32[]{:S(2)}) collective-permute-start(f32[32,128]{1,0:T(8,128)S(1)} %get-tuple-element.54), channel_id=1, source_target_pairs={{0,3},{1,0},{2,1},{3,2},{4,7},{5,4},{6,5},{7,6},{8,11},{9,8},{10,9... | collective-permute-start | bytes 49160 | tf_op jit(solution)/shard_map/ppermute | solution.py:382
  47.0 2.5 %shard_map.102 = (f32[32,8192]{1,0:T(8,128)}, f32[32,64]{1,0:T(8,128)}) custom-call(f32[32,1024]{1,0:T(8,128)S(1)} %get-tuple-element.39.refs_0_.gap_ref, bf16[2048,512]{1,0:T(8,128)(2,1)S(1)} %get-tuple-element.40.even_ref, bf16[2048,512]{1,0:T(8,128)(2,1)S(1)} %get-tuple-element.41.odd_ref, ...), custom_call_target="tpu_custom_call" | custom-call | flops 1610612736 | tf_op jit(solution)/shard_map/pallas_call | solution.py:26
  49.5 0.0 collective-permute-done.14
  49.5 0.0 collective-permute-done.15
  49.5 0.5 collective-permute-done.16
  50.0 0.6 %add_add_fusion = f32[32,128]{1,0:T(8,128)} fusion(f32[32,128]{1,0:T(8,128)S(1)} %collective-permute-done.16, f32[32,128]{1,0:T(8,128)S(1)} %collective-permute-done.15, f32[32,128]{1,0:T(8,128)S(1)} %get-tuple-element.51, f32[32,128]{1,0:T(8,128)S(1)} %collective-permute-done.14), kind=kLoop, calls=%fused_computation.1 | loop fusion | flops 12288 | bytes 81920 | tf_op jit(solution)/shard_map/add | solution.py:426
  (2 shorter events, 0.1 us)
Async XLA Ops:
  1.6 7.6 %collective-permute-start.4 = (bf16[704,128]{1,0:T(8,128)(2,1)S(1)}, bf16[704,128]{1,0:T(8,128)(2,1)S(1)}, u32[]{:S(2)}, u32[]{:S(2)}) collective-permute-start(bf16[704,128]{1,0:T(8,128)(2,1)S(1)} %pad_maximum_fusion.refs_0_), channel_id=1, source_target_pairs={{0,16},{4,20},{8,24},{12,28},{16,0},{20,4},{24,8},{28,12},{1,17},{... | collective-permute-start | bytes 540680 | tf_op jit(solution)/shard_map/ppermute | solution.py:376
  4.6 7.4 %collective-permute-start.3 = (bf16[704,128]{1,0:T(8,128)(2,1)S(1)}, bf16[704,128]{1,0:T(8,128)(2,1)S(1)}, u32[]{:S(2)}, u32[]{:S(2)}) collective-permute-start(bf16[704,128]{1,0:T(8,128)(2,1)S(1)} %pad_maximum_fusion.refs_0_), channel_id=1, source_target_pairs={{0,8},{4,12},{8,0},{12,4},{16,24},{20,28},{24,16},{28,20},{1,9},{5... | collective-permute-start | bytes 540680 | tf_op jit(solution)/shard_map/ppermute | solution.py:376
  6.1 8.2 %collective-permute-start = (bf16[704,128]{1,0:T(8,128)(2,1)S(1)}, bf16[704,128]{1,0:T(8,128)(2,1)S(1)}, u32[]{:S(2)}, u32[]{:S(2)}) collective-permute-start(bf16[704,128]{1,0:T(8,128)(2,1)S(1)} %pad_maximum_fusion.refs_0_), channel_id=1, source_target_pairs={{0,24},{4,28},{8,16},{12,20},{16,8},{20,12},{24,0},{28,4},{1,25},{... | collective-permute-start | bytes 540680 | tf_op jit(solution)/shard_map/ppermute | solution.py:376
  6.2 10.2 %collective-permute-start.2 = (bf16[704,128]{1,0:T(8,128)(2,1)S(1)}, bf16[704,128]{1,0:T(8,128)(2,1)S(1)}, u32[]{:S(2)}, u32[]{:S(2)}) collective-permute-start(bf16[704,128]{1,0:T(8,128)(2,1)S(1)} %pad_maximum_fusion.refs_0_), channel_id=1, source_target_pairs={{0,4},{4,0},{8,12},{12,8},{16,20},{20,16},{24,28},{28,24},{1,5},{5... | collective-permute-start | bytes 540680 | tf_op jit(solution)/shard_map/ppermute | solution.py:376
  9.2 9.2 %collective-permute-start.6 = (bf16[704,128]{1,0:T(8,128)(2,1)S(1)}, bf16[704,128]{1,0:T(8,128)(2,1)S(1)}, u32[]{:S(2)}, u32[]{:S(2)}) collective-permute-start(bf16[704,128]{1,0:T(8,128)(2,1)S(1)} %collective-permute-done.4.refs_1_.refs_2_), channel_id=1, source_target_pairs={{0,4},{4,0},{8,12},{12,8},{16,20},{20,16},{24,28},{28,24},{1,5},{5... | collective-permute-start | bytes 540680 | tf_op jit(solution)/shard_map/ppermute | solution.py:376
  12.1 6.3 %collective-permute-start.5 = (bf16[704,128]{1,0:T(8,128)(2,1)S(1)}, bf16[704,128]{1,0:T(8,128)(2,1)S(1)}, u32[]{:S(2)}, u32[]{:S(2)}) collective-permute-start(bf16[704,128]{1,0:T(8,128)(2,1)S(1)} %collective-permute-done.3.refs_0_.refs_1_), channel_id=1, source_target_pairs={{0,4},{4,0},{8,12},{12,8},{16,20},{20,16},{24,28},{28,24},{1,5},{5... | collective-permute-start | bytes 540680 | tf_op jit(solution)/shard_map/ppermute | solution.py:376
  14.3 6.2 %collective-permute-start.1 = (bf16[704,128]{1,0:T(8,128)(2,1)S(1)}, bf16[704,128]{1,0:T(8,128)(2,1)S(1)}, u32[]{:S(2)}, u32[]{:S(2)}) collective-permute-start(bf16[704,128]{1,0:T(8,128)(2,1)S(1)} %collective-permute-done.refs_0_.refs_3_), channel_id=1, source_target_pairs={{0,4},{4,0},{8,12},{12,8},{16,20},{20,16},{24,28},{28,24},{1,5},{5... | collective-permute-start | bytes 540680 | tf_op jit(solution)/shard_map/ppermute | solution.py:376
  20.5 7.8 %copy-start = (bf16[32,8192]{1,0:T(8,128)(2,1)S(1)}, bf16[32,8192]{1,0:T(8,128)(2,1)}, u32[]{:S(2)}) copy-start(bf16[32,8192]{1,0:T(8,128)(2,1)} %refs_3_.1) | copy-start | bytes 1572868
  22.6 7.2 %collective-permute-start.7 = (bf16[32,1024]{1,0:T(8,128)(2,1)S(1)}, bf16[32,1024]{1,0:T(8,128)(2,1)S(1)}, u32[]{:S(2)}, u32[]{:S(2)}) collective-permute-start(bf16[32,1024]{1,0:T(8,128)(2,1)S(1)} %get-tuple-element.32), channel_id=1, source_target_pairs={{0,1},{1,2},{2,3},{3,0},{4,5},{5,6},{6,7},{7,4},{8,9},{9,10},{10,1... | collective-permute-start | bytes 196616 | tf_op jit(solution)/shard_map/ppermute | solution.py:382
  24.3 7.7 %collective-permute-start.8 = (bf16[32,1024]{1,0:T(8,128)(2,1)S(1)}, bf16[32,1024]{1,0:T(8,128)(2,1)S(1)}, u32[]{:S(2)}, u32[]{:S(2)}) collective-permute-start(bf16[32,1024]{1,0:T(8,128)(2,1)S(1)} %get-tuple-element.33), channel_id=1, source_target_pairs={{0,2},{1,3},{2,0},{3,1},{4,6},{5,7},{6,4},{7,5},{8,10},{9,11},{10,... | collective-permute-start | bytes 196616 | tf_op jit(solution)/shard_map/ppermute | solution.py:382
  26.9 5.3 %collective-permute-start.9 = (bf16[32,1024]{1,0:T(8,128)(2,1)S(1)}, bf16[32,1024]{1,0:T(8,128)(2,1)S(1)}, u32[]{:S(2)}, u32[]{:S(2)}) collective-permute-start(bf16[32,1024]{1,0:T(8,128)(2,1)S(1)} %get-tuple-element.34), channel_id=1, source_target_pairs={{0,3},{1,0},{2,1},{3,2},{4,7},{5,4},{6,5},{7,6},{8,11},{9,8},{10,9... | collective-permute-start | bytes 196616 | tf_op jit(solution)/shard_map/ppermute | solution.py:382
  33.3 1.6 %collective-permute-start.10 = (f32[512,128]{1,0:T(8,128)S(1)}, f32[512,128]{1,0:T(8,128)S(1)}, u32[]{:S(2)}, u32[]{:S(2)}) collective-permute-start(f32[512,128]{1,0:T(8,128)S(1)} %get-tuple-element.46), channel_id=1, source_target_pairs={{0,4},{4,0},{8,12},{12,8},{16,20},{20,16},{24,28},{28,24},{1,5},{5... | collective-permute-start | bytes 786440 | tf_op jit(solution)/shard_map/ppermute | solution.py:376
  35.0 4.0 %collective-permute-start.11 = (bf16[128,128]{1,0:T(8,128)(2,1)S(1)}, bf16[128,128]{1,0:T(8,128)(2,1)S(1)}, u32[]{:S(2)}, u32[]{:S(2)}) collective-permute-start(bf16[128,128]{1,0:T(8,128)(2,1)S(1)} %get-tuple-element.48), channel_id=1, source_target_pairs={{0,8},{4,12},{8,0},{12,4},{16,24},{20,28},{24,16},{28,20},{1,9},{5... | collective-permute-start | bytes 98312 | tf_op jit(solution)/shard_map/ppermute | solution.py:376
  36.5 3.9 %collective-permute-start.12 = (bf16[128,128]{1,0:T(8,128)(2,1)S(1)}, bf16[128,128]{1,0:T(8,128)(2,1)S(1)}, u32[]{:S(2)}, u32[]{:S(2)}) collective-permute-start(bf16[128,128]{1,0:T(8,128)(2,1)S(1)} %get-tuple-element.49), channel_id=1, source_target_pairs={{0,16},{4,20},{8,24},{12,28},{16,0},{20,4},{24,8},{28,12},{1,17},{... | collective-permute-start | bytes 98312 | tf_op jit(solution)/shard_map/ppermute | solution.py:376
  38.1 4.8 %collective-permute-start.13 = (bf16[128,128]{1,0:T(8,128)(2,1)S(1)}, bf16[128,128]{1,0:T(8,128)(2,1)S(1)}, u32[]{:S(2)}, u32[]{:S(2)}) collective-permute-start(bf16[128,128]{1,0:T(8,128)(2,1)S(1)} %get-tuple-element.50), channel_id=1, source_target_pairs={{0,24},{4,28},{8,16},{12,20},{16,8},{20,12},{24,0},{28,4},{1,25},{... | collective-permute-start | bytes 98312 | tf_op jit(solution)/shard_map/ppermute | solution.py:376
  42.9 6.6 %collective-permute-start.14 = (f32[32,128]{1,0:T(8,128)S(1)}, f32[32,128]{1,0:T(8,128)S(1)}, u32[]{:S(2)}, u32[]{:S(2)}) collective-permute-start(f32[32,128]{1,0:T(8,128)S(1)} %get-tuple-element.52), channel_id=1, source_target_pairs={{0,1},{1,2},{2,3},{3,0},{4,5},{5,6},{6,7},{7,4},{8,9},{9,10},{10,1... | collective-permute-start | bytes 49160 | tf_op jit(solution)/shard_map/ppermute | solution.py:382
  44.6 4.9 %collective-permute-start.15 = (f32[32,128]{1,0:T(8,128)S(1)}, f32[32,128]{1,0:T(8,128)S(1)}, u32[]{:S(2)}, u32[]{:S(2)}) collective-permute-start(f32[32,128]{1,0:T(8,128)S(1)} %get-tuple-element.53), channel_id=1, source_target_pairs={{0,2},{1,3},{2,0},{3,1},{4,6},{5,7},{6,4},{7,5},{8,10},{9,11},{10,... | collective-permute-start | bytes 49160 | tf_op jit(solution)/shard_map/ppermute | solution.py:382
  46.2 3.7 %collective-permute-start.16 = (f32[32,128]{1,0:T(8,128)S(1)}, f32[32,128]{1,0:T(8,128)S(1)}, u32[]{:S(2)}, u32[]{:S(2)}) collective-permute-start(f32[32,128]{1,0:T(8,128)S(1)} %get-tuple-element.54), channel_id=1, source_target_pairs={{0,3},{1,0},{2,1},{3,2},{4,7},{5,4},{6,5},{7,6},{8,11},{9,8},{10,9... | collective-permute-start | bytes 49160 | tf_op jit(solution)/shard_map/ppermute | solution.py:382

commit v3 on v1

--- a/solution.py
+++ b/solution.py
@@ -22,12 +22,12 @@
     return jax.ShapeDtypeStruct(dims, kind)
 
 
-def call(body, out_shape, args, specs=None, scratch=(), flops=0, limit=20):
+def call(body, out_shape, args, specs=None, out_specs=None, scratch=(), flops=0, limit=20):
     return pl.pallas_call(
         body,
         out_shape=out_shape,
         in_specs=specs or [VMEM] * len(args),
-        out_specs=jax.tree.map(lambda _: VMEM, out_shape),
+        out_specs=out_specs or jax.tree.map(lambda _: VMEM, out_shape),
         scratch_shapes=list(scratch),
         compiler_params=pltpu.CompilerParams(vmem_limit_bytes=limit << 20),
         cost_estimate=pl.CostEstimate(flops=flops, bytes_accessed=0, transcendentals=0),
@@ -92,7 +92,7 @@
     outs, (keys, acc) = refs[:-2], refs[-2:]
     tiles, local_rows, wide = acc.shape
     heads = off_ref.shape[0]
-    group = min(16, heads)
+    group = min(32, heads)
     depth = KDIM + PAD
     per_tile = wide // LANES
     for tile in range(tiles):
@@ -130,6 +130,7 @@
         return
     own, sends = outs[0], outs[1:]
     rows = own.shape[0]
+    size = len(sends) + 1
     me = lax.axis_index("head")
     sources = [(ref, tile) for ref in (*prior, acc) for tile in range(ref.shape[0])]
     pieces = [(ref, tile, part) for ref, tile in sources for part in range(per_tile)]
@@ -137,7 +138,7 @@
         lanes = lanes_of(part)
         own[:, lanes_of(place)] = ref[tile, pl.ds(me * rows, rows), lanes]
         for hop, send in enumerate(sends):
-            there = jnp.bitwise_xor(me, hop + 1)
+            there = lax.rem(me + hop + 1, size)
             send[:, lanes_of(place)] = ref[tile, pl.ds(there * rows, rows), lanes].astype(send.dtype)
 
 
@@ -180,7 +181,7 @@
 def score_blocks(blocks, query_ref, scale_ref, active_ref, score, keys):
     index_heads, rows, columns = active_ref.shape
     dims = keys.shape[1]
-    group = min(8, index_heads)
+    group = min(64, index_heads)
     score[...] = jnp.zeros_like(score)
     for place, block in enumerate(blocks):
         keys[lanes_of(place)] = block[KDIM:]
@@ -284,28 +285,31 @@
     )
 
 
-def gap_of(shares, predicted):
-    mine, *others = shares
-    mass = mine[...]
-    for other in others:
-        mass = mass + other[...].astype(jnp.float32)
+def gap_of(shares, peers, predicted):
+    pieces = []
+    for begin in range(0, len(shares), peers):
+        mine, *others = shares[begin : begin + peers]
+        mass = mine[...]
+        for other in others:
+            mass = mass + other[...].astype(jnp.float32)
+        pieces.append(mass)
     seen = predicted >= 0.0
-    mass = jnp.where(seen, mass, 0.0)
+    mass = jnp.where(seen, jnp.concatenate(halved(pieces, 1), axis=1), 0.0)
     target = mass / jnp.sum(mass, axis=1, keepdims=True)
     return jnp.where(seen, predicted - target, 0.0)
 
 
-def key_kernel(peers, half, *refs):
-    shares, refs = refs[:peers], refs[peers:]
-    if peers:
+def key_kernel(count, peers, half, *refs):
+    shares, refs = refs[:count], refs[count:]
+    if count:
         predicted_ref, *actives, scale_ref, query_ref, gap_ref, slopes_ref, out_ref, tall = refs
-        gap_ref[...] = gap_of(shares, predicted_ref[...])
+        gap_ref[...] = gap_of(shares, peers, predicted_ref[...])
     else:
         gap_ref, *actives, scale_ref, query_ref, slopes_ref, out_ref, tall = refs
     index_heads, rows, _ = actives[0].shape
     dims, columns = tall.shape
     lanes = slice(half * columns, (half + 1) * columns)
-    group = min(8, index_heads)
+    group = min(64, index_heads)
     tall[...] = jnp.zeros_like(tall)
 
     @pl.loop(0, index_heads // group)
@@ -330,7 +334,7 @@
         out_ref[lanes_of(place)] = jnp.transpose(tall[:, lanes_of(place)])
 
 
-def key_terms(shares, gap, predicted, actives, scales, index_query, dims, half):
+def key_terms(shares, gap, predicted, actives, scales, index_query, dims, peers, half):
     index_heads, rows, _ = actives[0].shape
     seq_total = sum(active.shape[2] for active in actives)
     columns = seq_total // 2
@@ -344,7 +348,7 @@
     else:
         args = (gap,)
     return call(
-        functools.partial(key_kernel, len(shares), half),
+        functools.partial(key_kernel, len(shares), peers, half),
         out,
         (*args, *actives, scales, index_query),
         scratch=[pltpu.VMEM((dims, columns), jnp.float32)],
@@ -352,27 +356,35 @@
     )
 
 
-def query_kernel(even_ref, odd_ref, keys_ref, grad_query_ref):
-    rows = grad_query_ref.shape[0]
+def query_kernel(pieces, even_ref, odd_ref, keys_ref, grad_query_hbm, grads, sems):
+    rows, columns = grads.shape
     dims = keys_ref.shape[1]
-    index_heads = grad_query_ref.shape[1] // dims
-    group = min(8, index_heads)
-
-    @pl.loop(0, index_heads // group)
-    def _(step):
-        block = pl.ds(pl.multiple_of(step * (group * rows), group * rows), group * rows)
-        slopes = jnp.concatenate([even_ref[block, :], odd_ref[block, :]], axis=1)
+    heads = columns // dims // pieces
+    copies = []
+    for piece in range(pieces):
+        block = slice(piece * heads * rows, (piece + 1) * heads * rows)
+        slopes = jnp.concatenate([even_ref[block], odd_ref[block]], axis=1)
         grad = jnp.dot(slopes, keys_ref[...], preferred_element_type=jnp.float32)
-        for head in range(group):
-            begin = pl.multiple_of((step * group + head) * dims, dims)
-            grad_query_ref[:, pl.ds(begin, dims)] = grad[head * rows : (head + 1) * rows]
+        for head in range(heads):
+            begin = (piece * heads + head) * dims
+            grads[:, begin : begin + dims] = grad[head * rows : (head + 1) * rows]
+        lanes = pl.ds(piece * heads * dims, heads * dims)
+        copy = pltpu.make_async_copy(grads.at[:, lanes], grad_query_hbm.at[:, lanes], sems.at[piece])
+        copy.start()
+        copies.append(copy)
+    for copy in copies:
+        copy.wait()
 
 
 def query_grads(even, odd, keys, rows):
-    return call(
-        query_kernel,
-        shape_of((rows, even.shape[0] // rows * keys.shape[1]), jnp.float32),
+    columns = even.shape[0] // rows * keys.shape[1]
+    pieces = 4
+    return call(
+        functools.partial(query_kernel, pieces),
+        shape_of((rows, columns), jnp.float32),
         (even, odd, keys),
+        out_specs=HBM,
+        scratch=[pltpu.VMEM((rows, columns), jnp.float32), pltpu.SemaphoreType.DMA((pieces,))],
         flops=4 * even.shape[0] * keys.shape[0] * keys.shape[1],
     )
 
@@ -380,7 +392,7 @@
 def weight_kernel(factor, gap_ref, *refs):
     *actives, grad_weight_ref, sums = refs
     index_heads, rows, _ = actives[0].shape
-    group = min(8, index_heads)
+    group = min(64, index_heads)
     lane = lax.broadcasted_iota(jnp.int32, (rows, LANES), 1)
     sums[...] = jnp.zeros_like(sums)
 
@@ -441,7 +453,7 @@
     def pass_on(values):
         out = []
         for hop, value in enumerate(values):
-            to = [(place, place ^ (hop + 1)) for place in range(peers)]
+            to = [(place, (place + hop + 1) % peers) for place in range(peers)]
             out.append(lax.ppermute(value, "head", to))
         return out
 
@@ -457,29 +469,31 @@
     query, offsets, scales, lows = spread(
         lat_query, normalizer, index_weight, lookback, heads, factor
     )
-    prior = []
-    for phase in phases:
-        last = phase is phases[-1]
+    early = sorted((slot for phase in phases[:-1] for slot in phase), key=order.index)
+    late = sorted(phases[-1], key=order.index)
+    prior, shares = [], []
+    for place, phase in enumerate(phases):
+        ready = late if place == 3 else early if place == 2 else []
+        since = [slot for slots in phases[:place] for slot in slots] if place == 2 else []
         mass = attention_mass(
             query,
             offsets,
             [blocks[slot] for slot in phase],
-            prior if last else [],
-            [order.index(slot) for slots in phases for slot in slots] if last else [],
+            prior if since else [],
+            [ready.index(slot) for slot in since + phase] if ready else [],
             rows,
             peers,
         )
-        prior.append(mass)
-    own, *sends = mass
-    shares = [own, *pass_on(sends)]
-    early = sorted((slot for phase in phases[:-1] for slot in phase), key=order.index)
-    late = sorted(phases[-1], key=order.index)
+        if ready:
+            shares += [mass[0], *pass_on(mass[1:])]
+        else:
+            prior.append(mass)
     first, scores, keys = index_scores(index_query, scales, [blocks[slot] for slot in early], dims)
     second, predicted, keys = predictions(
         index_query, scales, lows, scores, keys, [blocks[slot] for slot in late], order, dims
     )
     terms = functools.partial(
-        key_terms, actives=(first, second), scales=scales, index_query=index_query, dims=dims
+        key_terms, actives=(first, second), scales=scales, index_query=index_query, dims=dims, peers=peers
     )
     gap, odd, give = terms(shares, None, predicted, half=1)
     come = swap(give, 1)
@@ -504,7 +518,7 @@
     me = lax.axis_index("head")
     mine_ref[...] = total[pl.ds(me * rows, rows), :]
     for hop, send in enumerate(sends):
-        send[...] = total[pl.ds(jnp.bitwise_xor(me, hop + 1) * rows, rows), :]
+        send[...] = total[pl.ds(lax.rem(me + hop + 1, peers) * rows, rows), :]
 
 
 def gather_terms(own, others, rows, peers):

time: 53.8 us -> 56 us (1.041)
  waiting for transfers between devices: 9.4 us -> 17.9 us
  Pallas kernels: 24.2 us -> 17.8 us
    ppermute x6 -> x9, waiting for transfers between devices: 1.95 us -> 9.27 us  [pass_on(): out.append(lax.ppermute(value, 'head', to))]
    pallas_call x13, Pallas kernels: 24.2 us -> 17.8 us  [call(): pl.pallas_call(body, out_shape=out_shape, in_specs=specs or [VMEM] * len(...]
    ppermute x11, waiting for transfers between devices: 7.45 us -> 8.59 us  [swap(): lax.ppermute(value, 'seq', [(place, place ^ bits) for place in range(seq_...]
    ppermute x6 -> x9, starting transfers between devices: 8.9 us -> 9.13 us  [pass_on(): out.append(lax.ppermute(value, 'head', to))]
  transfers between devices with their start and end apart: 17 -> 20, of which waited for: 6 -> 8; matrix products, arithmetic and copies ran while one was open for 0% -> 0% of each run, Pallas kernels for 37% -> 30%
where the time goes in v3:
time: 56 us; the launch traced here: 55.8 us
  waiting for transfers between devices  17.9 us (32%)
  starting transfers between devices  17.8 us (32%)
  Pallas kernels  17.8 us (32%)
  other arithmetic  1.56 us (3%)
  between operations  0.78 us (1%)
    pallas_call x13, Pallas kernels, call(): pl.pallas_call(body, out_shape=out_shape, in_specs=specs or [VMEM] * len(...  17.8 us
    ppermute x9, waiting for transfers between devices, pass_on(): out.append(lax.ppermute(value, 'head', to))  9.27 us
    ppermute x9, starting transfers between devices, pass_on(): out.append(lax.ppermute(value, 'head', to))  9.13 us
    ppermute x11, starting transfers between devices, swap(): lax.ppermute(value, 'seq', [(place, place ^ bits) for place in range(seq_...  8.71 us
    ppermute x11, waiting for transfers between devices, swap(): lax.ppermute(value, 'seq', [(place, place ^ bits) for place in range(seq_...  8.59 us
  transfers between devices with their start and end apart: 20, of which 8 were waited for; matrix products, arithmetic and copies ran while one was open for 0% of the time, Pallas kernels for 30%

profile of v3, /device:TPU:0, one launch (start us, length us, event | category | flops | bytes accessed | tf_op | source)
XLA Modules:
  0.0 55.8 jit_solution(10484425154515316020)
XLA Ops:
  0.6 0.9 %pad_maximum_fusion.refs_0_ = bf16[704,128]{1,0:T(8,128)(2,1)S(1)} fusion(bf16[128,128]{1,0:T(8,128)(2,1)} %param.12, bf16[576,128]{1,0:T(8,128)(2,1)} %bitcast.2), kind=kLoop, calls=%fused_computation | loop fusion | flops 360448 | bytes 360448 | tf_op jit(solution)/shard_map/concatenate | solution.py:460
  1.6 3.0 %collective-permute-start = (bf16[704,128]{1,0:T(8,128)(2,1)S(1)}, bf16[704,128]{1,0:T(8,128)(2,1)S(1)}, u32[]{:S(2)}, u32[]{:S(2)}) collective-permute-start(bf16[704,128]{1,0:T(8,128)(2,1)S(1)} %pad_maximum_fusion.refs_0_), channel_id=1, source_target_pairs={{0,8},{4,12},{8,0},{12,4},{16,24},{20,28},{24,16},{28,20},{1,9},{5... | collective-permute-start | bytes 540680 | tf_op jit(solution)/shard_map/ppermute | solution.py:451
  4.6 1.5 %collective-permute-start.2 = (bf16[704,128]{1,0:T(8,128)(2,1)S(1)}, bf16[704,128]{1,0:T(8,128)(2,1)S(1)}, u32[]{:S(2)}, u32[]{:S(2)}) collective-permute-start(bf16[704,128]{1,0:T(8,128)(2,1)S(1)} %pad_maximum_fusion.refs_0_), channel_id=1, source_target_pairs={{0,16},{4,20},{8,24},{12,28},{16,0},{20,4},{24,8},{28,12},{1,17},{... | collective-permute-start | bytes 540680 | tf_op jit(solution)/shard_map/ppermute | solution.py:451
  6.1 0.0 collective-permute-start.8
  6.2 0.0 collective-permute-start.4
  6.2 2.4 %shard_map.94 = (bf16[128,18432]{1,0:T(8,128)(2,1)S(1)}, f32[32,128,128]{2,1,0:T(8,128)S(1)}, f32[64,32,128]{2,1,0:T(8,128)S(1)}, f32[32,128]{1,0:T(8,128)S(1)}) custom-call(bf16[128,18432]{1,0:T(8,128)(2,1)} %query_hbm.1, f32[128,128]{1,0:T(8,128)} %norm_hbm.1, f32[32,64]{1,0:T(8,128)} %weight_hbm.1, s32[1,128]{1,0:T(1,128)} %bitcast.3), custom_call_target="tpu_custom_call" | custom-call | flops 1500000000 | tf_op jit(solution)/shard_map/pallas_call | solution.py:26
  8.6 1.4 %collective-permute-done.refs_0_.refs_1_ = bf16[704,128]{1,0:T(8,128)(2,1)S(1)} collective-permute-done((bf16[704,128]{1,0:T(8,128)(2,1)S(1)}, bf16[704,128]{1,0:T(8,128)(2,1)S(1)}, u32[]{:S(2)}, u32[]{:S(2)}) %collective-permute-start) | collective-permute-done | bytes 180256 | tf_op jit(solution)/shard_map/ppermute | solution.py:451
  10.0 0.0 collective-permute-start.1
  10.0 4.5 %collective-permute-done.2.refs_1_.refs_2_ = bf16[704,128]{1,0:T(8,128)(2,1)S(1)} collective-permute-done((bf16[704,128]{1,0:T(8,128)(2,1)S(1)}, bf16[704,128]{1,0:T(8,128)(2,1)S(1)}, u32[]{:S(2)}, u32[]{:S(2)}) %collective-permute-start.2) | collective-permute-done | bytes 180256 | tf_op jit(solution)/shard_map/ppermute | solution.py:451
  14.5 0.0 collective-permute-start.3
  14.5 0.0 collective-permute-done.8.refs_0_
  14.5 0.5 collective-permute-start.9
  15.0 2.0 %shard_map.96.refs_3_ = f32[1,128,256]{2,1,0:T(8,128)S(1)} custom-call(bf16[128,18432]{1,0:T(8,128)(2,1)S(1)} %get-tuple-element.34.query_ref, f32[32,128,128]{2,1,0:T(8,128)S(1)} %get-tuple-element.35.off_ref, bf16[704,128]{1,0:T(8,128)(2,1)S(1)} %collective-permute-done.refs_0_.refs_1_, bf16[704,128]{1,0:T(8,128)(2,1)S(1)} %collective-permute-done.2.refs_1_.refs_2_), custom_call_target="tpu_custom_call" | custom-call | flops 1207959552 | tf_op jit(solution)/shard_map/pallas_call | solution.py:26
  17.0 0.0 collective-permute-done.4.refs_1_.refs_3_
  17.0 2.0 %shard_map.95.refs_2_ = f32[1,128,256]{2,1,0:T(8,128)S(1)} custom-call(bf16[128,18432]{1,0:T(8,128)(2,1)S(1)} %get-tuple-element.34.query_ref, f32[32,128,128]{2,1,0:T(8,128)S(1)} %get-tuple-element.35.off_ref, bf16[704,128]{1,0:T(8,128)(2,1)S(1)} %pad_maximum_fusion.refs_0_, bf16[704,128]{1,0:T(8,128)(2,1)S(1)} %collective-permute-done.4.refs_1_.refs_3_), custom_call_target="tpu_custom_call" | custom-call | flops 1207959552 | tf_op jit(solution)/shard_map/pallas_call | solution.py:26
  19.1 0.0 collective-permute-done.1.refs_0_.refs_4_
  19.1 0.0 collective-permute-done.3.refs_1_.refs_5_
  19.1 2.1 %shard_map.97 = (f32[32,768]{1,0:T(8,128)S(1)}, bf16[32,768]{1,0:T(8,128)(2,1)S(1)}, bf16[32,768]{1,0:T(8,128)(2,1)S(1)}, bf16[32,768]{1,0:T(8,128)(2,1)S(1)}) custom-call(bf16[128,18432]{1,0:T(8,128)(2,1)S(1)} %get-tuple-element.34.query_ref, f32[32,128,128]{2,1,0:T(8,128)S(1)} %get-tuple-element.35.off_ref, ...), custom_call_target="tpu_custom_call" | custom-call | flops 1207959552 | tf_op jit(solution)/shard_map/pallas_call | solution.py:26
  21.2 1.6 %collective-permute-start.5 = (bf16[32,768]{1,0:T(8,128)(2,1)S(1)}, bf16[32,768]{1,0:T(8,128)(2,1)S(1)}, u32[]{:S(2)}, u32[]{:S(2)}) collective-permute-start(bf16[32,768]{1,0:T(8,128)(2,1)S(1)} %get-tuple-element.37), channel_id=1, source_target_pairs={{0,1},{1,2},{2,3},{3,0},{4,5},{5,6},{6,7},{7,4},{8,9},{9,10},{10,1... | collective-permute-start | bytes 147464 | tf_op jit(solution)/shard_map/ppermute | solution.py:457
  22.8 2.6 %collective-permute-start.6 = (bf16[32,768]{1,0:T(8,128)(2,1)S(1)}, bf16[32,768]{1,0:T(8,128)(2,1)S(1)}, u32[]{:S(2)}, u32[]{:S(2)}) collective-permute-start(bf16[32,768]{1,0:T(8,128)(2,1)S(1)} %get-tuple-element.38), channel_id=1, source_target_pairs={{0,2},{1,3},{2,0},{3,1},{4,6},{5,7},{6,4},{7,5},{8,10},{9,11},{10,... | collective-permute-start | bytes 147464 | tf_op jit(solution)/shard_map/ppermute | solution.py:457
  25.4 0.0 copy-start
  25.4 1.4 %collective-permute-start.7 = (bf16[32,768]{1,0:T(8,128)(2,1)S(1)}, bf16[32,768]{1,0:T(8,128)(2,1)S(1)}, u32[]{:S(2)}, u32[]{:S(2)}) collective-permute-start(bf16[32,768]{1,0:T(8,128)(2,1)S(1)} %get-tuple-element.39), channel_id=1, source_target_pairs={{0,3},{1,0},{2,1},{3,2},{4,7},{5,4},{6,5},{7,6},{8,11},{9,8},{10,9... | collective-permute-start | bytes 147464 | tf_op jit(solution)/shard_map/ppermute | solution.py:457
  26.7 0.0 collective-permute-done.9.refs_1_
  26.7 2.0 %shard_map.98 = (f32[32,256]{1,0:T(8,128)S(1)}, bf16[32,256]{1,0:T(8,128)(2,1)S(1)}, bf16[32,256]{1,0:T(8,128)(2,1)S(1)}, bf16[32,256]{1,0:T(8,128)(2,1)S(1)}) custom-call(bf16[128,18432]{1,0:T(8,128)(2,1)S(1)} %get-tuple-element.34.query_ref, f32[32,128,128]{2,1,0:T(8,128)S(1)} %get-tuple-element.35.off_ref, ...), custom_call_target="tpu_custom_call" | custom-call | flops 1207959552 | tf_op jit(solution)/shard_map/pallas_call | solution.py:26
  28.8 0.7 %collective-permute-start.10 = (bf16[32,256]{1,0:T(8,128)(2,1)S(1)}, bf16[32,256]{1,0:T(8,128)(2,1)S(1)}, u32[]{:S(2)}, u32[]{:S(2)}) collective-permute-start(bf16[32,256]{1,0:T(8,128)(2,1)S(1)} %get-tuple-element.41), channel_id=1, source_target_pairs={{0,1},{1,2},{2,3},{3,0},{4,5},{5,6},{6,7},{7,4},{8,9},{9,10},{10,1... | collective-permute-start | bytes 49160 | tf_op jit(solution)/shard_map/ppermute | solution.py:457
  29.5 0.3 collective-permute-start.11
  29.9 0.0 copy-done
  29.9 1.1 %shard_map.99 = (f32[64,32,768]{2,1,0:T(8,128)S(1)}, f32[32,768]{1,0:T(8,128)S(1)}, bf16[768,128]{1,0:T(8,128)(2,1)S(1)}) custom-call(bf16[32,8192]{1,0:T(8,128)(2,1)S(1)} %copy-done, f32[64,32,128]{2,1,0:T(8,128)S(1)} %get-tuple-element.44.scale_ref.refs_11_.refs_3_, bf16[704,128]{1,0:T(8,128)(2,1)S(1)} %pad_maximum_fusion.refs_0_, ...), custom_call_target="tpu_custom_call" | custom-call | flops 1207959552 | tf_op jit(solution)/shard_map/pallas_call | solution.py:26
  30.9 3.4 %collective-permute-done.10.refs_5_ = bf16[32,256]{1,0:T(8,128)(2,1)S(1)} collective-permute-done((bf16[32,256]{1,0:T(8,128)(2,1)S(1)}, bf16[32,256]{1,0:T(8,128)(2,1)S(1)}, u32[]{:S(2)}, u32[]{:S(2)}) %collective-permute-start.10) | collective-permute-done | bytes 16416 | tf_op jit(solution)/shard_map/ppermute | solution.py:457
  34.4 0.0 collective-permute-start.12
  34.4 0.7 %shard_map.100 = (f32[64,32,256]{2,1,0:T(8,128)S(1)}, f32[32,1024]{1,0:T(8,128)S(1)}, bf16[1024,128]{1,0:T(8,128)(2,1)S(1)}) custom-call(bf16[32,8192]{1,0:T(8,128)(2,1)S(1)} %copy-done, f32[64,32,128]{2,1,0:T(8,128)S(1)} %get-tuple-element.44.scale_ref.refs_11_.refs_3_, f32[32,128]{1,0:T(8,128)S(1)} %get-tuple-element.45.low_ref, ...), custom_call_target="tpu_custom_call" | custom-call | flops 536870912 | tf_op jit(solution)/shard_map/pallas_call | solution.py:26
  35.1 0.0 collective-permute-done.11.refs_6_
  35.1 3.0 %collective-permute-done.12.refs_7_ = bf16[32,256]{1,0:T(8,128)(2,1)S(1)} collective-permute-done((bf16[32,256]{1,0:T(8,128)(2,1)S(1)}, bf16[32,256]{1,0:T(8,128)(2,1)S(1)}, u32[]{:S(2)}, u32[]{:S(2)}) %collective-permute-start.12) | collective-permute-done | bytes 16416 | tf_op jit(solution)/shard_map/ppermute | solution.py:457
  38.1 0.0 collective-permute-done.5.refs_1_
  38.1 0.0 collective-permute-done.6.refs_2_
  38.1 0.0 collective-permute-done.7.refs_3_
  38.1 1.1 %shard_map.101 = (f32[32,1024]{1,0:T(8,128)S(1)}, bf16[2048,512]{1,0:T(8,128)(2,1)S(1)}, f32[512,128]{1,0:T(8,128)S(1)}) custom-call(f32[32,768]{1,0:T(8,128)S(1)} %get-tuple-element.36.refs_0_, bf16[32,768]{1,0:T(8,128)(2,1)S(1)} %collective-permute-done.5.refs_1_, bf16[32,768]{1,0:T(8,128)(2,1)S(1)} %collective-permute-done.6.refs_2_, ...), custom_call_target="tpu_custom_call" | custom-call | flops 1073741824 | tf_op jit(solution)/shard_map/pallas_call | solution.py:26
  39.2 0.1 collective-permute-start.13
  39.3 0.9 %shard_map.102 = (bf16[2048,512]{1,0:T(8,128)(2,1)S(1)}, f32[512,128]{1,0:T(8,128)S(1)}) custom-call(f32[32,1024]{1,0:T(8,128)S(1)} %get-tuple-element.51.refs_0_.gap_ref, f32[64,32,768]{2,1,0:T(8,128)S(1)} %get-tuple-element.49.refs_9_.refs_1_.refs_0_, f32[64,32,256]{2,1,0:T(8,128)S(1)} %get-tuple-element.50.refs_10_.refs_2_.refs_1_, ...), custom_call_target="tpu_custom_call" | custom-call | flops 1073741824 | tf_op jit(solution)/shard_map/pallas_call | solution.py:26
  40.2 0.6 %collective-permute-done.13.come_ref = f32[512,128]{1,0:T(8,128)S(1)} collective-permute-done((f32[512,128]{1,0:T(8,128)S(1)}, f32[512,128]{1,0:T(8,128)S(1)}, u32[]{:S(2)}, u32[]{:S(2)}) %collective-permute-start.13) | collective-permute-done | bytes 262176 | tf_op jit(solution)/shard_map/ppermute | solution.py:451
  40.8 0.8 %collective-permute-start.14 = (bf16[128,128]{1,0:T(8,128)(2,1)S(1)}, bf16[128,128]{1,0:T(8,128)(2,1)S(1)}, u32[]{:S(2)}, u32[]{:S(2)}) collective-permute-start(bf16[128,128]{1,0:T(8,128)(2,1)S(1)} %get-tuple-element.58), channel_id=1, source_target_pairs={{0,8},{4,12},{8,0},{12,4},{16,24},{20,28},{24,16},{28,20},{1,9},{5... | collective-permute-start | bytes 98312 | tf_op jit(solution)/shard_map/ppermute | solution.py:451
  41.6 1.3 %collective-permute-start.15 = (bf16[128,128]{1,0:T(8,128)(2,1)S(1)}, bf16[128,128]{1,0:T(8,128)(2,1)S(1)}, u32[]{:S(2)}, u32[]{:S(2)}) collective-permute-start(bf16[128,128]{1,0:T(8,128)(2,1)S(1)} %get-tuple-element.59), channel_id=1, source_target_pairs={{0,16},{4,20},{8,24},{12,28},{16,0},{20,4},{24,8},{28,12},{1,17},{... | collective-permute-start | bytes 98312 | tf_op jit(solution)/shard_map/ppermute | solution.py:451
  43.0 1.4 %collective-permute-start.16 = (bf16[128,128]{1,0:T(8,128)(2,1)S(1)}, bf16[128,128]{1,0:T(8,128)(2,1)S(1)}, u32[]{:S(2)}, u32[]{:S(2)}) collective-permute-start(bf16[128,128]{1,0:T(8,128)(2,1)S(1)} %get-tuple-element.60), channel_id=1, source_target_pairs={{0,24},{4,28},{8,16},{12,20},{16,8},{20,12},{24,0},{28,4},{1,25},{... | collective-permute-start | bytes 98312 | tf_op jit(solution)/shard_map/ppermute | solution.py:451
  44.4 1.2 %shard_map.104 = f32[32,64]{1,0:T(8,128)} custom-call(f32[32,1024]{1,0:T(8,128)S(1)} %get-tuple-element.51.refs_0_.gap_ref, f32[64,32,768]{2,1,0:T(8,128)S(1)} %get-tuple-element.49.refs_9_.refs_1_.refs_0_, f32[64,32,256]{2,1,0:T(8,128)S(1)} %get-tuple-element.50.refs_10_.refs_2_.refs_1_), custom_call_target="tpu_custom_call" | custom-call | flops 1073741824 | tf_op jit(solution)/shard_map/pallas_call | solution.py:26
  45.6 0.0 collective-permute-done.14.refs_0_
  45.7 0.0 collective-permute-done.15.refs_1_
  45.7 2.1 %collective-permute-done.16.refs_2_ = bf16[128,128]{1,0:T(8,128)(2,1)S(1)} collective-permute-done((bf16[128,128]{1,0:T(8,128)(2,1)S(1)}, bf16[128,128]{1,0:T(8,128)(2,1)S(1)}, u32[]{:S(2)}, u32[]{:S(2)}) %collective-permute-start.16) | collective-permute-done | bytes 32800 | tf_op jit(solution)/shard_map/ppermute | solution.py:451
  47.8 1.9 %collective-permute-start.19 = (f32[32,128]{1,0:T(8,128)S(1)}, f32[32,128]{1,0:T(8,128)S(1)}, u32[]{:S(2)}, u32[]{:S(2)}) collective-permute-start(f32[32,128]{1,0:T(8,128)S(1)} %get-tuple-element.64), channel_id=1, source_target_pairs={{0,3},{1,0},{2,1},{3,2},{4,7},{5,4},{6,5},{7,6},{8,11},{9,8},{10,9... | collective-permute-start | bytes 49160 | tf_op jit(solution)/shard_map/ppermute | solution.py:457
  49.7 0.0 collective-permute-start.18
  49.7 0.6 %collective-permute-start.17 = (f32[32,128]{1,0:T(8,128)S(1)}, f32[32,128]{1,0:T(8,128)S(1)}, u32[]{:S(2)}, u32[]{:S(2)}) collective-permute-start(f32[32,128]{1,0:T(8,128)S(1)} %get-tuple-element.62), channel_id=1, source_target_pairs={{0,1},{1,2},{2,3},{3,0},{4,5},{5,6},{6,7},{7,4},{8,9},{9,10},{10,1... | collective-permute-start | bytes 49160 | tf_op jit(solution)/shard_map/ppermute | solution.py:457
  50.3 2.1 %shard_map.103 = f32[32,8192]{1,0:T(8,128)} custom-call(bf16[2048,512]{1,0:T(8,128)(2,1)S(1)} %get-tuple-element.52.even_ref, bf16[2048,512]{1,0:T(8,128)(2,1)S(1)} %get-tuple-element.53.odd_ref, bf16[1024,128]{1,0:T(8,128)(2,1)S(1)} %get-tuple-element.54.keys_ref), custom_call_target="tpu_custom_call" | custom-call | flops 1073741824 | tf_op jit(solution)/shard_map/pallas_call | solution.py:26
  52.4 0.0 collective-permute-done.19
  52.4 1.9 %collective-permute-done.18 = f32[32,128]{1,0:T(8,128)S(1)} collective-permute-done((f32[32,128]{1,0:T(8,128)S(1)}, f32[32,128]{1,0:T(8,128)S(1)}, u32[]{:S(2)}, u32[]{:S(2)}) %collective-permute-start.18) | collective-permute-done | bytes 16416 | tf_op jit(solution)/shard_map/ppermute | solution.py:457
  54.3 0.9 %collective-permute-done.17 = f32[32,128]{1,0:T(8,128)S(1)} collective-permute-done((f32[32,128]{1,0:T(8,128)S(1)}, f32[32,128]{1,0:T(8,128)S(1)}, u32[]{:S(2)}, u32[]{:S(2)}) %collective-permute-start.17) | collective-permute-done | bytes 16416 | tf_op jit(solution)/shard_map/ppermute | solution.py:457
  55.2 0.6 %add_add_fusion = f32[32,128]{1,0:T(8,128)} fusion(f32[32,128]{1,0:T(8,128)S(1)} %collective-permute-done.19, f32[32,128]{1,0:T(8,128)S(1)} %collective-permute-done.18, f32[32,128]{1,0:T(8,128)S(1)} %get-tuple-element.61, f32[32,128]{1,0:T(8,128)S(1)} %collective-permute-done.17), kind=kLoop, calls=%fused_computation.1 | loop fusion | flops 12288 | bytes 81920 | tf_op jit(solution)/shard_map/add | solution.py:507
  (2 shorter events, 0.1 us)
Async XLA Ops:
  1.6 8.4 %collective-permute-start = (bf16[704,128]{1,0:T(8,128)(2,1)S(1)}, bf16[704,128]{1,0:T(8,128)(2,1)S(1)}, u32[]{:S(2)}, u32[]{:S(2)}) collective-permute-start(bf16[704,128]{1,0:T(8,128)(2,1)S(1)} %pad_maximum_fusion.refs_0_), channel_id=1, source_target_pairs={{0,8},{4,12},{8,0},{12,4},{16,24},{20,28},{24,16},{28,20},{1,9},{5... | collective-permute-start | bytes 540680 | tf_op jit(solution)/shard_map/ppermute | solution.py:451
  4.6 9.9 %collective-permute-start.2 = (bf16[704,128]{1,0:T(8,128)(2,1)S(1)}, bf16[704,128]{1,0:T(8,128)(2,1)S(1)}, u32[]{:S(2)}, u32[]{:S(2)}) collective-permute-start(bf16[704,128]{1,0:T(8,128)(2,1)S(1)} %pad_maximum_fusion.refs_0_), channel_id=1, source_target_pairs={{0,16},{4,20},{8,24},{12,28},{16,0},{20,4},{24,8},{28,12},{1,17},{... | collective-permute-start | bytes 540680 | tf_op jit(solution)/shard_map/ppermute | solution.py:451
  6.1 8.4 %collective-permute-start.8 = (bf16[704,128]{1,0:T(8,128)(2,1)S(1)}, bf16[704,128]{1,0:T(8,128)(2,1)S(1)}, u32[]{:S(2)}, u32[]{:S(2)}) collective-permute-start(bf16[704,128]{1,0:T(8,128)(2,1)S(1)} %pad_maximum_fusion.refs_0_), channel_id=1, source_target_pairs={{0,24},{4,28},{8,16},{12,20},{16,8},{20,12},{24,0},{28,4},{1,25},{... | collective-permute-start | bytes 540680 | tf_op jit(solution)/shard_map/ppermute | solution.py:451
  6.2 10.9 %collective-permute-start.4 = (bf16[704,128]{1,0:T(8,128)(2,1)S(1)}, bf16[704,128]{1,0:T(8,128)(2,1)S(1)}, u32[]{:S(2)}, u32[]{:S(2)}) collective-permute-start(bf16[704,128]{1,0:T(8,128)(2,1)S(1)} %pad_maximum_fusion.refs_0_), channel_id=1, source_target_pairs={{0,4},{4,0},{8,12},{12,8},{16,20},{20,16},{24,28},{28,24},{1,5},{5... | collective-permute-start | bytes 540680 | tf_op jit(solution)/shard_map/ppermute | solution.py:451
  10.0 9.1 %collective-permute-start.1 = (bf16[704,128]{1,0:T(8,128)(2,1)S(1)}, bf16[704,128]{1,0:T(8,128)(2,1)S(1)}, u32[]{:S(2)}, u32[]{:S(2)}) collective-permute-start(bf16[704,128]{1,0:T(8,128)(2,1)S(1)} %collective-permute-done.refs_0_.refs_1_), channel_id=1, source_target_pairs={{0,4},{4,0},{8,12},{12,8},{16,20},{20,16},{24,28},{28,24},{1,5},{5... | collective-permute-start | bytes 540680 | tf_op jit(solution)/shard_map/ppermute | solution.py:451
  14.5 4.6 %collective-permute-start.3 = (bf16[704,128]{1,0:T(8,128)(2,1)S(1)}, bf16[704,128]{1,0:T(8,128)(2,1)S(1)}, u32[]{:S(2)}, u32[]{:S(2)}) collective-permute-start(bf16[704,128]{1,0:T(8,128)(2,1)S(1)} %collective-permute-done.2.refs_1_.refs_2_), channel_id=1, source_target_pairs={{0,4},{4,0},{8,12},{12,8},{16,20},{20,16},{24,28},{28,24},{1,5},{5... | collective-permute-start | bytes 540680 | tf_op jit(solution)/shard_map/ppermute | solution.py:451
  14.5 12.3 %collective-permute-start.9 = (bf16[704,128]{1,0:T(8,128)(2,1)S(1)}, bf16[704,128]{1,0:T(8,128)(2,1)S(1)}, u32[]{:S(2)}, u32[]{:S(2)}) collective-permute-start(bf16[704,128]{1,0:T(8,128)(2,1)S(1)} %collective-permute-done.8.refs_0_), channel_id=1, source_target_pairs={{0,4},{4,0},{8,12},{12,8},{16,20},{20,16},{24,28},{28,24},{1,5},{5... | collective-permute-start | bytes 540680 | tf_op jit(solution)/shard_map/ppermute | solution.py:451
  21.2 17.0 %collective-permute-start.5 = (bf16[32,768]{1,0:T(8,128)(2,1)S(1)}, bf16[32,768]{1,0:T(8,128)(2,1)S(1)}, u32[]{:S(2)}, u32[]{:S(2)}) collective-permute-start(bf16[32,768]{1,0:T(8,128)(2,1)S(1)} %get-tuple-element.37), channel_id=1, source_target_pairs={{0,1},{1,2},{2,3},{3,0},{4,5},{5,6},{6,7},{7,4},{8,9},{9,10},{10,1... | collective-permute-start | bytes 147464 | tf_op jit(solution)/shard_map/ppermute | solution.py:457
  22.8 15.3 %collective-permute-start.6 = (bf16[32,768]{1,0:T(8,128)(2,1)S(1)}, bf16[32,768]{1,0:T(8,128)(2,1)S(1)}, u32[]{:S(2)}, u32[]{:S(2)}) collective-permute-start(bf16[32,768]{1,0:T(8,128)(2,1)S(1)} %get-tuple-element.38), channel_id=1, source_target_pairs={{0,2},{1,3},{2,0},{3,1},{4,6},{5,7},{6,4},{7,5},{8,10},{9,11},{10,... | collective-permute-start | bytes 147464 | tf_op jit(solution)/shard_map/ppermute | solution.py:457
  25.4 4.5 %copy-start = (bf16[32,8192]{1,0:T(8,128)(2,1)S(1)}, bf16[32,8192]{1,0:T(8,128)(2,1)}, u32[]{:S(2)}) copy-start(bf16[32,8192]{1,0:T(8,128)(2,1)} %refs_4_.1) | copy-start | bytes 1572868
  25.4 12.7 %collective-permute-start.7 = (bf16[32,768]{1,0:T(8,128)(2,1)S(1)}, bf16[32,768]{1,0:T(8,128)(2,1)S(1)}, u32[]{:S(2)}, u32[]{:S(2)}) collective-permute-start(bf16[32,768]{1,0:T(8,128)(2,1)S(1)} %get-tuple-element.39), channel_id=1, source_target_pairs={{0,3},{1,0},{2,1},{3,2},{4,7},{5,4},{6,5},{7,6},{8,11},{9,8},{10,9... | collective-permute-start | bytes 147464 | tf_op jit(solution)/shard_map/ppermute | solution.py:457
  28.8 5.6 %collective-permute-start.10 = (bf16[32,256]{1,0:T(8,128)(2,1)S(1)}, bf16[32,256]{1,0:T(8,128)(2,1)S(1)}, u32[]{:S(2)}, u32[]{:S(2)}) collective-permute-start(bf16[32,256]{1,0:T(8,128)(2,1)S(1)} %get-tuple-element.41), channel_id=1, source_target_pairs={{0,1},{1,2},{2,3},{3,0},{4,5},{5,6},{6,7},{7,4},{8,9},{9,10},{10,1... | collective-permute-start | bytes 49160 | tf_op jit(solution)/shard_map/ppermute | solution.py:457
  29.5 5.6 %collective-permute-start.11 = (bf16[32,256]{1,0:T(8,128)(2,1)S(1)}, bf16[32,256]{1,0:T(8,128)(2,1)S(1)}, u32[]{:S(2)}, u32[]{:S(2)}) collective-permute-start(bf16[32,256]{1,0:T(8,128)(2,1)S(1)} %get-tuple-element.42), channel_id=1, source_target_pairs={{0,2},{1,3},{2,0},{3,1},{4,6},{5,7},{6,4},{7,5},{8,10},{9,11},{10,... | collective-permute-start | bytes 49160 | tf_op jit(solution)/shard_map/ppermute | solution.py:457
  34.4 3.7 %collective-permute-start.12 = (bf16[32,256]{1,0:T(8,128)(2,1)S(1)}, bf16[32,256]{1,0:T(8,128)(2,1)S(1)}, u32[]{:S(2)}, u32[]{:S(2)}) collective-permute-start(bf16[32,256]{1,0:T(8,128)(2,1)S(1)} %get-tuple-element.43), channel_id=1, source_target_pairs={{0,3},{1,0},{2,1},{3,2},{4,7},{5,4},{6,5},{7,6},{8,11},{9,8},{10,9... | collective-permute-start | bytes 49160 | tf_op jit(solution)/shard_map/ppermute | solution.py:457
  39.2 1.6 %collective-permute-start.13 = (f32[512,128]{1,0:T(8,128)S(1)}, f32[512,128]{1,0:T(8,128)S(1)}, u32[]{:S(2)}, u32[]{:S(2)}) collective-permute-start(f32[512,128]{1,0:T(8,128)S(1)} %get-tuple-element.56), channel_id=1, source_target_pairs={{0,4},{4,0},{8,12},{12,8},{16,20},{20,16},{24,28},{28,24},{1,5},{5... | collective-permute-start | bytes 786440 | tf_op jit(solution)/shard_map/ppermute | solution.py:451
  40.8 4.8 %collective-permute-start.14 = (bf16[128,128]{1,0:T(8,128)(2,1)S(1)}, bf16[128,128]{1,0:T(8,128)(2,1)S(1)}, u32[]{:S(2)}, u32[]{:S(2)}) collective-permute-start(bf16[128,128]{1,0:T(8,128)(2,1)S(1)} %get-tuple-element.58), channel_id=1, source_target_pairs={{0,8},{4,12},{8,0},{12,4},{16,24},{20,28},{24,16},{28,20},{1,9},{5... | collective-permute-start | bytes 98312 | tf_op jit(solution)/shard_map/ppermute | solution.py:451
  41.6 4.0 %collective-permute-start.15 = (bf16[128,128]{1,0:T(8,128)(2,1)S(1)}, bf16[128,128]{1,0:T(8,128)(2,1)S(1)}, u32[]{:S(2)}, u32[]{:S(2)}) collective-permute-start(bf16[128,128]{1,0:T(8,128)(2,1)S(1)} %get-tuple-element.59), channel_id=1, source_target_pairs={{0,16},{4,20},{8,24},{12,28},{16,0},{20,4},{24,8},{28,12},{1,17},{... | collective-permute-start | bytes 98312 | tf_op jit(solution)/shard_map/ppermute | solution.py:451
  43.0 4.8 %collective-permute-start.16 = (bf16[128,128]{1,0:T(8,128)(2,1)S(1)}, bf16[128,128]{1,0:T(8,128)(2,1)S(1)}, u32[]{:S(2)}, u32[]{:S(2)}) collective-permute-start(bf16[128,128]{1,0:T(8,128)(2,1)S(1)} %get-tuple-element.60), channel_id=1, source_target_pairs={{0,24},{4,28},{8,16},{12,20},{16,8},{20,12},{24,0},{28,4},{1,25},{... | collective-permute-start | bytes 98312 | tf_op jit(solution)/shard_map/ppermute | solution.py:451
  47.8 4.6 %collective-permute-start.19 = (f32[32,128]{1,0:T(8,128)S(1)}, f32[32,128]{1,0:T(8,128)S(1)}, u32[]{:S(2)}, u32[]{:S(2)}) collective-permute-start(f32[32,128]{1,0:T(8,128)S(1)} %get-tuple-element.64), channel_id=1, source_target_pairs={{0,3},{1,0},{2,1},{3,2},{4,7},{5,4},{6,5},{7,6},{8,11},{9,8},{10,9... | collective-permute-start | bytes 49160 | tf_op jit(solution)/shard_map/ppermute | solution.py:457
  49.7 4.6 %collective-permute-start.18 = (f32[32,128]{1,0:T(8,128)S(1)}, f32[32,128]{1,0:T(8,128)S(1)}, u32[]{:S(2)}, u32[]{:S(2)}) collective-permute-start(f32[32,128]{1,0:T(8,128)S(1)} %get-tuple-element.63), channel_id=1, source_target_pairs={{0,2},{1,3},{2,0},{3,1},{4,6},{5,7},{6,4},{7,5},{8,10},{9,11},{10,... | collective-permute-start | bytes 49160 | tf_op jit(solution)/shard_map/ppermute | solution.py:457
  49.7 5.5 %collective-permute-start.17 = (f32[32,128]{1,0:T(8,128)S(1)}, f32[32,128]{1,0:T(8,128)S(1)}, u32[]{:S(2)}, u32[]{:S(2)}) collective-permute-start(f32[32,128]{1,0:T(8,128)S(1)} %get-tuple-element.62), channel_id=1, source_target_pairs={{0,1},{1,2},{2,3},{3,0},{4,5},{5,6},{6,7},{7,4},{8,9},{9,10},{10,1... | collective-permute-start | bytes 49160 | tf_op jit(solution)/shard_map/ppermute | solution.py:457

commit v4 on v2

--- a/solution.py
+++ b/solution.py
@@ -349,18 +349,16 @@
     )
 
 
-def fold_kernel(keep_ref, come_ref, own_ref, *sends):
-    total = keep_ref[...] + come_ref[...]
-    rows = own_ref.shape[0]
-    own_ref[...] = total[:rows]
-    for hop, send in enumerate(sends):
-        send[...] = total[(hop + 1) * rows : (hop + 2) * rows].astype(send.dtype)
-
-
-def fold(keep, come, block):
-    count = keep.shape[0] // block
-    piece = (block, keep.shape[1])
-    out = (shape_of(piece, jnp.float32),) + (shape_of(piece, jnp.bfloat16),) * (count - 1)
+def fold_kernel(keep_ref, come_ref, out_ref):
+    place = lax.axis_index("seq") // 2
+    for chip in range(out_ref.shape[0] // LANES):
+        begin = pl.multiple_of(jnp.bitwise_xor(place, chip) * LANES, LANES)
+        total = keep_ref[lanes_of(chip)] + come_ref[lanes_of(chip)]
+        out_ref[pl.ds(begin, LANES), :] = total.astype(out_ref.dtype)
+
+
+def fold(keep, come):
+    out = shape_of(keep.shape, jnp.bfloat16)
     return call(fold_kernel, out, (keep, come), flops=10_000_000)
 
 
@@ -388,7 +386,7 @@
         blocks[bits] = swap(mine, bits)
     for bits in range(0, seq_count, 2):
         blocks[bits + 1] = swap(blocks[bits], 1)
-    phases = [[0, 1], [2, 4], [3, 5], list(range(6, seq_count))]
+    phases = [[0, 1], [2, 3], [*range(4, seq_count, 2)], [*range(5, seq_count, 2)]]
     order = [*range(0, seq_count, 2), *range(1, seq_count, 2)]
 
     query, offsets, scales, lows = spread(
@@ -418,37 +416,16 @@
     gap, odd, give = terms(shares, None, predicted, half=1)
     come = swap(give, 1)
     even, keep = terms([], gap, None, half=0)
-    own, *sends = fold(keep, come, LANES)
-    others = [swap(send, 2 * (hop + 1)) for hop, send in enumerate(sends)]
+    members = [
+        [seq * peers + head for seq in range(core, seq_count, 2) for head in range(peers)]
+        for core in range(2)
+    ]
+    arrived = lax.all_to_all(
+        fold(keep, come), ("seq", "head"), 0, 0, tiled=True, axis_index_groups=members
+    )
     grad_query, grad_weight = query_grads(gap, even, odd, active, keys, factor)
-    own, *sends = gather_terms(own, others, rows, peers)
-    others = pass_on(sends)
-    grad_key = functools.reduce(jnp.add, others, own)
+    grad_key = jnp.sum(arrived.reshape(-1, rows, dims).astype(jnp.float32), axis=0)
     return grad_query, grad_weight, grad_key
-
-
-def gather_kernel(peers, own_ref, *refs):
-    others, (mine_ref, *sends), total = refs[: len(refs) - peers - 1], refs[-peers - 1 : -1], refs[-1]
-    value = own_ref[...]
-    for other in others:
-        value = value + other[...].astype(jnp.float32)
-    total[...] = value
-    rows = mine_ref.shape[0]
-    me = lax.axis_index("head")
-    mine_ref[...] = total[pl.ds(me * rows, rows), :]
-    for hop, send in enumerate(sends):
-        send[...] = total[pl.ds(lax.rem(me + hop + 1, peers) * rows, rows), :]
-
-
-def gather_terms(own, others, rows, peers):
-    piece = shape_of((rows, own.shape[1]), jnp.float32)
-    return call(
-        functools.partial(gather_kernel, peers),
-        (piece,) * peers,
-        (own, *others),
-        scratch=[pltpu.VMEM(own.shape, jnp.float32)],
-        flops=10_000_000,
-    )
 
 
 def solution(mesh):

time: 50.7 us -> 52 us (1.026)
  local copies, waits for them, and re-layouts: 0.01 us -> 6.36 us
  waiting for transfers between devices: 13.5 us -> 10.5 us
  starting transfers between devices: 18.1 us -> 15.3 us
  Pallas kernels: 16.6 us -> 17.2 us
    unnamed x2 -> x10, local copies, waits for them, and re-layouts: 0.01 us -> 6.36 us
    all_to_all x0 -> x1, starting transfers between devices: none -> 5.03 us  [per_device(): lax.all_to_all(fold(keep, come), ('seq', 'head'), 0, 0, tiled=True, axis_...]
    ppermute x6 -> x3, starting transfers between devices: 9.84 us -> 5.58 us  [pass_on(): out.append(lax.ppermute(value, 'head', to))]
    ppermute x11 -> x8, starting transfers between devices: 8.26 us -> 4.65 us  [swap(): lax.ppermute(value, 'seq', [(place, place ^ bits) for place in range(seq_...]
    ppermute x11 -> x8, waiting for transfers between devices: 10.6 us -> 7.09 us  [swap(): lax.ppermute(value, 'seq', [(place, place ^ bits) for place in range(seq_...]
    all_to_all x0 -> x1, waiting for transfers between devices: none -> 0.88 us  [per_device(): lax.all_to_all(fold(keep, come), ('seq', 'head'), 0, 0, tiled=True, axis_...]
    reduce_sum x0 -> x1, other arithmetic: none -> 0.63 us  [per_device(): jnp.sum(arrived.reshape(-1, rows, dims).astype(jnp.float32), axis=0)]
    pallas_call x11 -> x10, Pallas kernels: 16.6 us -> 17.2 us  [call(): pl.pallas_call(body, out_shape=out_shape, in_specs=specs or [VMEM] * len(...]
  transfers between devices with their start and end apart: 17 -> 12, of which waited for: 10 -> 6; matrix products, arithmetic and copies ran while one was open for 0% -> 0% of each run, Pallas kernels for 27% -> 26%
where the time goes in v4:
time: 52 us; the launch traced here: 51.7 us
  Pallas kernels  17.2 us (33%)
  starting transfers between devices  15.3 us (29%)
  waiting for transfers between devices  10.5 us (20%)
  local copies, waits for them, and re-layouts  6.36 us (12%)
  other arithmetic  1.57 us (3%)
  between operations  0.8 us (2%)
    pallas_call x10, Pallas kernels, call(): pl.pallas_call(body, out_shape=out_shape, in_specs=specs or [VMEM] * len(...  17.2 us
    ppermute x8, waiting for transfers between devices, swap(): lax.ppermute(value, 'seq', [(place, place ^ bits) for place in range(seq_...  7.09 us
    unnamed x10, local copies, waits for them, and re-layouts  6.36 us
    ppermute x3, starting transfers between devices, pass_on(): out.append(lax.ppermute(value, 'head', to))  5.58 us
    all_to_all x1, starting transfers between devices, per_device(): lax.all_to_all(fold(keep, come), ('seq', 'head'), 0, 0, tiled=True, axis_...  5.03 us
    ppermute x8, starting transfers between devices, swap(): lax.ppermute(value, 'seq', [(place, place ^ bits) for place in range(seq_...  4.65 us
    ppermute x3, waiting for transfers between devices, pass_on(): out.append(lax.ppermute(value, 'head', to))  2.48 us
  transfers between devices with their start and end apart: 12, of which 6 were waited for; matrix products, arithmetic and copies ran while one was open for 0% of the time, Pallas kernels for 26%

profile of v4, /device:TPU:0, one launch (start us, length us, event | category | flops | bytes accessed | tf_op | source)
XLA Modules:
  0.0 51.7 jit_solution(5709818960409384678)
XLA Ops:
  0.6 0.9 %pad_maximum_fusion.refs_0_ = bf16[704,128]{1,0:T(8,128)(2,1)S(1)} fusion(bf16[128,128]{1,0:T(8,128)(2,1)} %param.12, bf16[576,128]{1,0:T(8,128)(2,1)} %bitcast.3), kind=kLoop, calls=%fused_computation.1 | loop fusion | flops 360448 | bytes 360448 | tf_op jit(solution)/shard_map/concatenate | solution.py:383
  1.6 3.0 %collective-permute-start.5 = (bf16[704,128]{1,0:T(8,128)(2,1)S(1)}, bf16[704,128]{1,0:T(8,128)(2,1)S(1)}, u32[]{:S(2)}, u32[]{:S(2)}) collective-permute-start(bf16[704,128]{1,0:T(8,128)(2,1)S(1)} %pad_maximum_fusion.refs_0_), channel_id=1, source_target_pairs={{0,8},{4,12},{8,0},{12,4},{16,24},{20,28},{24,16},{28,20},{1,9},{5... | collective-permute-start | bytes 540680 | tf_op jit(solution)/shard_map/ppermute | solution.py:374
  4.6 1.5 %collective-permute-start.2 = (bf16[704,128]{1,0:T(8,128)(2,1)S(1)}, bf16[704,128]{1,0:T(8,128)(2,1)S(1)}, u32[]{:S(2)}, u32[]{:S(2)}) collective-permute-start(bf16[704,128]{1,0:T(8,128)(2,1)S(1)} %pad_maximum_fusion.refs_0_), channel_id=1, source_target_pairs={{0,24},{4,28},{8,16},{12,20},{16,8},{20,12},{24,0},{28,4},{1,25},{... | collective-permute-start | bytes 540680 | tf_op jit(solution)/shard_map/ppermute | solution.py:374
  6.1 0.1 collective-permute-start
  6.2 0.0 collective-permute-start.4
  6.2 2.4 %shard_map.94 = (bf16[128,18432]{1,0:T(8,128)(2,1)S(1)}, f32[32,128,128]{2,1,0:T(8,128)S(1)}, f32[64,32,128]{2,1,0:T(8,128)S(1)}, f32[32,128]{1,0:T(8,128)S(1)}) custom-call(bf16[128,18432]{1,0:T(8,128)(2,1)} %query_hbm.1, f32[128,128]{1,0:T(8,128)} %norm_hbm.1, f32[32,64]{1,0:T(8,128)} %weight_hbm.1, s32[1,128]{1,0:T(1,128)} %bitcast.4), custom_call_target="tpu_custom_call" | custom-call | flops 1500000000 | tf_op jit(solution)/shard_map/pallas_call | solution.py:26
  8.6 1.4 %collective-permute-done.5.refs_0_.refs_1_ = bf16[704,128]{1,0:T(8,128)(2,1)S(1)} collective-permute-done((bf16[704,128]{1,0:T(8,128)(2,1)S(1)}, bf16[704,128]{1,0:T(8,128)(2,1)S(1)}, u32[]{:S(2)}, u32[]{:S(2)}) %collective-permute-start.5) | collective-permute-done | bytes 180256 | tf_op jit(solution)/shard_map/ppermute | solution.py:374
  10.0 0.0 collective-permute-start.6
  10.0 4.3 %collective-permute-done.2.refs_1_.refs_3_ = bf16[704,128]{1,0:T(8,128)(2,1)S(1)} collective-permute-done((bf16[704,128]{1,0:T(8,128)(2,1)S(1)}, bf16[704,128]{1,0:T(8,128)(2,1)S(1)}, u32[]{:S(2)}, u32[]{:S(2)}) %collective-permute-start.2) | collective-permute-done | bytes 180256 | tf_op jit(solution)/shard_map/ppermute | solution.py:374
  14.3 0.0 collective-permute-start.3
  14.3 1.4 %collective-permute-done.refs_0_.refs_2_ = bf16[704,128]{1,0:T(8,128)(2,1)S(1)} collective-permute-done((bf16[704,128]{1,0:T(8,128)(2,1)S(1)}, bf16[704,128]{1,0:T(8,128)(2,1)S(1)}, u32[]{:S(2)}, u32[]{:S(2)}) %collective-permute-start) | collective-permute-done | bytes 180256 | tf_op jit(solution)/shard_map/ppermute | solution.py:374
  15.7 0.0 collective-permute-start.1
  15.7 2.0 %shard_map.97.refs_4_ = f32[1,128,256]{2,1,0:T(8,128)S(1)} custom-call(bf16[128,18432]{1,0:T(8,128)(2,1)S(1)} %get-tuple-element.21.query_ref, f32[32,128,128]{2,1,0:T(8,128)S(1)} %get-tuple-element.22.off_ref, bf16[704,128]{1,0:T(8,128)(2,1)S(1)} %collective-permute-done.refs_0_.refs_2_, bf16[704,128]{1,0:T(8,128)(2,1)S(1)} %collective-permute-done.2.refs_1_.refs_3_), custom_call_target="tpu_custom_call" | custom-call | flops 1207959552 | tf_op jit(solution)/shard_map/pallas_call | solution.py:26
  17.7 0.0 collective-permute-done.4.refs_1_.refs_4_
  17.7 2.0 %shard_map.95.refs_2_ = f32[1,128,256]{2,1,0:T(8,128)S(1)} custom-call(bf16[128,18432]{1,0:T(8,128)(2,1)S(1)} %get-tuple-element.21.query_ref, f32[32,128,128]{2,1,0:T(8,128)S(1)} %get-tuple-element.22.off_ref, bf16[704,128]{1,0:T(8,128)(2,1)S(1)} %pad_maximum_fusion.refs_0_, bf16[704,128]{1,0:T(8,128)(2,1)S(1)} %collective-permute-done.4.refs_1_.refs_4_), custom_call_target="tpu_custom_call" | custom-call | flops 1207959552 | tf_op jit(solution)/shard_map/pallas_call | solution.py:26
  19.8 0.0 collective-permute-done.6.refs_1_.refs_5_
  19.8 2.0 %shard_map.96.refs_3_ = f32[1,128,256]{2,1,0:T(8,128)S(1)} custom-call(bf16[128,18432]{1,0:T(8,128)(2,1)S(1)} %get-tuple-element.21.query_ref, f32[32,128,128]{2,1,0:T(8,128)S(1)} %get-tuple-element.22.off_ref, bf16[704,128]{1,0:T(8,128)(2,1)S(1)} %collective-permute-done.5.refs_0_.refs_1_, bf16[704,128]{1,0:T(8,128)(2,1)S(1)} %collective-permute-done.6.refs_1_.refs_5_), custom_call_target="tpu_custom_call" | custom-call | flops 1207959552 | tf_op jit(solution)/shard_map/pallas_call | solution.py:26
  21.8 0.0 copy-start.4
  21.8 0.0 collective-permute-done.3.refs_1_.refs_7_
  21.9 0.0 collective-permute-done.1.refs_0_.refs_6_
  21.9 2.1 %shard_map.98 = (f32[32,1024]{1,0:T(8,128)S(1)}, bf16[32,1024]{1,0:T(8,128)(2,1)S(1)}, bf16[32,1024]{1,0:T(8,128)(2,1)S(1)}, bf16[32,1024]{1,0:T(8,128)(2,1)S(1)}) custom-call(bf16[128,18432]{1,0:T(8,128)(2,1)S(1)} %get-tuple-element.21.query_ref, f32[32,128,128]{2,1,0:T(8,128)S(1)} %get-tuple-element.22.off_ref, ...), custom_call_target="tpu_custom_call" | custom-call | flops 1207959552 | tf_op jit(solution)/shard_map/pallas_call | solution.py:26
  23.9 1.6 %collective-permute-start.7 = (bf16[32,1024]{1,0:T(8,128)(2,1)S(1)}, bf16[32,1024]{1,0:T(8,128)(2,1)S(1)}, u32[]{:S(2)}, u32[]{:S(2)}) collective-permute-start(bf16[32,1024]{1,0:T(8,128)(2,1)S(1)} %get-tuple-element.24), channel_id=1, source_target_pairs={{0,1},{1,2},{2,3},{3,0},{4,5},{5,6},{6,7},{7,4},{8,9},{9,10},{10,1... | collective-permute-start | bytes 196616 | tf_op jit(solution)/shard_map/ppermute | solution.py:380
  25.6 2.6 %collective-permute-start.8 = (bf16[32,1024]{1,0:T(8,128)(2,1)S(1)}, bf16[32,1024]{1,0:T(8,128)(2,1)S(1)}, u32[]{:S(2)}, u32[]{:S(2)}) collective-permute-start(bf16[32,1024]{1,0:T(8,128)(2,1)S(1)} %get-tuple-element.25), channel_id=1, source_target_pairs={{0,2},{1,3},{2,0},{3,1},{4,6},{5,7},{6,4},{7,5},{8,10},{9,11},{10,... | collective-permute-start | bytes 196616 | tf_op jit(solution)/shard_map/ppermute | solution.py:380
  28.2 1.3 %collective-permute-start.9 = (bf16[32,1024]{1,0:T(8,128)(2,1)S(1)}, bf16[32,1024]{1,0:T(8,128)(2,1)S(1)}, u32[]{:S(2)}, u32[]{:S(2)}) collective-permute-start(bf16[32,1024]{1,0:T(8,128)(2,1)S(1)} %get-tuple-element.26), channel_id=1, source_target_pairs={{0,3},{1,0},{2,1},{3,2},{4,7},{5,4},{6,5},{7,6},{8,11},{9,8},{10,9... | collective-permute-start | bytes 196616 | tf_op jit(solution)/shard_map/ppermute | solution.py:380
  29.5 0.0 copy-done.4
  29.5 1.5 %shard_map.99 = (f32[64,32,1024]{2,1,0:T(8,128)S(1)}, f32[32,1024]{1,0:T(8,128)S(1)}, bf16[1024,128]{1,0:T(8,128)(2,1)S(1)}) custom-call(bf16[32,8192]{1,0:T(8,128)(2,1)S(1)} %copy-done.4, f32[64,32,128]{2,1,0:T(8,128)S(1)} %get-tuple-element.27.scale_ref.refs_6_.refs_2_, f32[32,128]{1,0:T(8,128)S(1)} %get-tuple-element.28.low_ref, ...), custom_call_target="tpu_custom_call" | custom-call | flops 1610612736 | tf_op jit(solution)/shard_map/pallas_call | solution.py:26
  31.0 0.0 copy-start
  31.0 0.0 collective-permute-done.7.refs_1_
  31.0 2.2 %collective-permute-done.8.refs_2_ = bf16[32,1024]{1,0:T(8,128)(2,1)S(1)} collective-permute-done((bf16[32,1024]{1,0:T(8,128)(2,1)S(1)}, bf16[32,1024]{1,0:T(8,128)(2,1)S(1)}, u32[]{:S(2)}, u32[]{:S(2)}) %collective-permute-start.8) | collective-permute-done | bytes 65568 | tf_op jit(solution)/shard_map/ppermute | solution.py:380
  33.3 0.2 collective-permute-done.9.refs_3_
  33.5 1.1 %shard_map.100 = (f32[32,1024]{1,0:T(8,128)S(1)}, bf16[2048,512]{1,0:T(8,128)(2,1)S(1)}, f32[512,128]{1,0:T(8,128)S(1)}) custom-call(f32[32,1024]{1,0:T(8,128)S(1)} %get-tuple-element.23.refs_0_, bf16[32,1024]{1,0:T(8,128)(2,1)S(1)} %collective-permute-done.7.refs_1_, bf16[32,1024]{1,0:T(8,128)(2,1)S(1)} %collective-permute-done.8.refs_2_, ...), custom_call_target="tpu_custom_call" | custom-call | flops 1073741824 | tf_op jit(solution)/shard_map/pallas_call | solution.py:26
  34.6 0.1 collective-permute-start.10
  34.7 0.0 copy-done
  34.7 0.9 %shard_map.101 = (bf16[2048,512]{1,0:T(8,128)(2,1)S(1)}, f32[512,128]{1,0:T(8,128)S(1)}) custom-call(f32[32,1024]{1,0:T(8,128)S(1)} %get-tuple-element.31.refs_0_.gap_ref, f32[64,32,1024]{2,1,0:T(8,128)S(1)} %get-tuple-element.30.refs_5_.refs_1_.active_ref, f32[64,32,128]{2,1,0:T(8,128)S(1)} %get-tuple-element.27.scale_ref.refs_6_.refs_2_, ...), custom_call_target="tpu_custom_call" | custom-call | flops 1073741824 | tf_op jit(solution)/shard_map/pallas_call | solution.py:26
  35.6 0.0 copy-start.2
  35.6 1.4 %copy-done.2 = bf16[2048,512]{1,0:T(8,128)(2,1)} copy-done((bf16[2048,512]{1,0:T(8,128)(2,1)}, bf16[2048,512]{1,0:T(8,128)(2,1)S(1)}, u32[]{:S(2)}) %copy-start.2) | copy-done | bytes 2097176
  37.0 0.0 collective-permute-done.10.come_ref
  37.0 0.7 %shard_map.103 = bf16[512,128]{1,0:T(8,128)(2,1)} custom-call(f32[512,128]{1,0:T(8,128)S(1)} %get-tuple-element.37.keep_ref, f32[512,128]{1,0:T(8,128)S(1)} %collective-permute-done.10.come_ref), custom_call_target="tpu_custom_call" | custom-call | flops 10000000 | tf_op jit(solution)/shard_map/pallas_call | solution.py:26
  37.7 5.0 %all-to-all-start = ((bf16[16,32,128]{2,1,0:T(8,128)(2,1)}), bf16[16,32,128]{2,1,0:T(8,128)(2,1)S(1)}, u32[]{:S(2)}, u32[]{:S(2)}) async-start(bf16[16,32,128]{2,1,0:T(8,128)(2,1)} %bitcast.2), calls=%async_computation | async-start | bytes 262144 | tf_op jit(solution)/shard_map/all_to_all | solution.py:423
  42.7 0.0 copy-start.1
  42.7 3.4 %copy-done.1 = f32[64,32,1024]{2,1,0:T(8,128)S(1)} copy-done((f32[64,32,1024]{2,1,0:T(8,128)S(1)}, f32[64,32,1024]{2,1,0:T(8,128)}, u32[]{:S(2)}) %copy-start.1) | copy-done | bytes 8388632
  46.1 0.0 copy-start.3
  46.1 1.6 %copy-done.3 = bf16[2048,512]{1,0:T(8,128)(2,1)S(1)} copy-done((bf16[2048,512]{1,0:T(8,128)(2,1)S(1)}, bf16[2048,512]{1,0:T(8,128)(2,1)}, u32[]{:S(2)}) %copy-start.3) | copy-done | bytes 2097176
  47.7 2.5 %shard_map.102 = (f32[32,8192]{1,0:T(8,128)}, f32[32,64]{1,0:T(8,128)}) custom-call(f32[32,1024]{1,0:T(8,128)S(1)} %get-tuple-element.31.refs_0_.gap_ref, bf16[2048,512]{1,0:T(8,128)(2,1)S(1)} %copy-done.3, bf16[2048,512]{1,0:T(8,128)(2,1)S(1)} %get-tuple-element.33.odd_ref, f32[64,32,1024]{2,1,0:T(8,128)S(1)} %copy-done.1, ...), custom_call_target="tpu_custom_call" | custom-call | flops 1610612736 | tf_op jit(solution)/shard_map/pallas_call | solution.py:26
  50.2 0.9 %all-to-all-done = bf16[16,32,128]{2,1,0:T(8,128)(2,1)S(1)} async-done(((bf16[16,32,128]{2,1,0:T(8,128)(2,1)}), bf16[16,32,128]{2,1,0:T(8,128)(2,1)S(1)}, u32[]{:S(2)}, u32[]{:S(2)}) %all-to-all-start) | async-done | bytes 131104 | tf_op jit(solution)/shard_map/all_to_all | solution.py:423
  51.0 0.6 %convert_reduce_fusion = f32[32,128]{1,0:T(8,128)} fusion(bf16[16,32,128]{2,1,0:T(8,128)(2,1)S(1)} %all-to-all-done), kind=kLoop, calls=%fused_computation | loop fusion | flops 126976 | bytes 147456 | tf_op jit(solution)/shard_map/reduce_sum | solution.py:427
Async XLA Ops:
  1.6 8.4 %collective-permute-start.5 = (bf16[704,128]{1,0:T(8,128)(2,1)S(1)}, bf16[704,128]{1,0:T(8,128)(2,1)S(1)}, u32[]{:S(2)}, u32[]{:S(2)}) collective-permute-start(bf16[704,128]{1,0:T(8,128)(2,1)S(1)} %pad_maximum_fusion.refs_0_), channel_id=1, source_target_pairs={{0,8},{4,12},{8,0},{12,4},{16,24},{20,28},{24,16},{28,20},{1,9},{5... | collective-permute-start | bytes 540680 | tf_op jit(solution)/shard_map/ppermute | solution.py:374
  4.6 9.7 %collective-permute-start.2 = (bf16[704,128]{1,0:T(8,128)(2,1)S(1)}, bf16[704,128]{1,0:T(8,128)(2,1)S(1)}, u32[]{:S(2)}, u32[]{:S(2)}) collective-permute-start(bf16[704,128]{1,0:T(8,128)(2,1)S(1)} %pad_maximum_fusion.refs_0_), channel_id=1, source_target_pairs={{0,24},{4,28},{8,16},{12,20},{16,8},{20,12},{24,0},{28,4},{1,25},{... | collective-permute-start | bytes 540680 | tf_op jit(solution)/shard_map/ppermute | solution.py:374
  6.1 9.6 %collective-permute-start = (bf16[704,128]{1,0:T(8,128)(2,1)S(1)}, bf16[704,128]{1,0:T(8,128)(2,1)S(1)}, u32[]{:S(2)}, u32[]{:S(2)}) collective-permute-start(bf16[704,128]{1,0:T(8,128)(2,1)S(1)} %pad_maximum_fusion.refs_0_), channel_id=1, source_target_pairs={{0,16},{4,20},{8,24},{12,28},{16,0},{20,4},{24,8},{28,12},{1,17},{... | collective-permute-start | bytes 540680 | tf_op jit(solution)/shard_map/ppermute | solution.py:374
  6.2 11.6 %collective-permute-start.4 = (bf16[704,128]{1,0:T(8,128)(2,1)S(1)}, bf16[704,128]{1,0:T(8,128)(2,1)S(1)}, u32[]{:S(2)}, u32[]{:S(2)}) collective-permute-start(bf16[704,128]{1,0:T(8,128)(2,1)S(1)} %pad_maximum_fusion.refs_0_), channel_id=1, source_target_pairs={{0,4},{4,0},{8,12},{12,8},{16,20},{20,16},{24,28},{28,24},{1,5},{5... | collective-permute-start | bytes 540680 | tf_op jit(solution)/shard_map/ppermute | solution.py:374
  10.0 9.8 %collective-permute-start.6 = (bf16[704,128]{1,0:T(8,128)(2,1)S(1)}, bf16[704,128]{1,0:T(8,128)(2,1)S(1)}, u32[]{:S(2)}, u32[]{:S(2)}) collective-permute-start(bf16[704,128]{1,0:T(8,128)(2,1)S(1)} %collective-permute-done.5.refs_0_.refs_1_), channel_id=1, source_target_pairs={{0,4},{4,0},{8,12},{12,8},{16,20},{20,16},{24,28},{28,24},{1,5},{5... | collective-permute-start | bytes 540680 | tf_op jit(solution)/shard_map/ppermute | solution.py:374
  14.3 7.5 %collective-permute-start.3 = (bf16[704,128]{1,0:T(8,128)(2,1)S(1)}, bf16[704,128]{1,0:T(8,128)(2,1)S(1)}, u32[]{:S(2)}, u32[]{:S(2)}) collective-permute-start(bf16[704,128]{1,0:T(8,128)(2,1)S(1)} %collective-permute-done.2.refs_1_.refs_3_), channel_id=1, source_target_pairs={{0,4},{4,0},{8,12},{12,8},{16,20},{20,16},{24,28},{28,24},{1,5},{5... | collective-permute-start | bytes 540680 | tf_op jit(solution)/shard_map/ppermute | solution.py:374
  15.7 6.2 %collective-permute-start.1 = (bf16[704,128]{1,0:T(8,128)(2,1)S(1)}, bf16[704,128]{1,0:T(8,128)(2,1)S(1)}, u32[]{:S(2)}, u32[]{:S(2)}) collective-permute-start(bf16[704,128]{1,0:T(8,128)(2,1)S(1)} %collective-permute-done.refs_0_.refs_2_), channel_id=1, source_target_pairs={{0,4},{4,0},{8,12},{12,8},{16,20},{20,16},{24,28},{28,24},{1,5},{5... | collective-permute-start | bytes 540680 | tf_op jit(solution)/shard_map/ppermute | solution.py:374
  21.8 7.7 %copy-start.4 = (bf16[32,8192]{1,0:T(8,128)(2,1)S(1)}, bf16[32,8192]{1,0:T(8,128)(2,1)}, u32[]{:S(2)}) copy-start(bf16[32,8192]{1,0:T(8,128)(2,1)} %refs_3_.1) | copy-start | bytes 1572868
  23.9 7.1 %collective-permute-start.7 = (bf16[32,1024]{1,0:T(8,128)(2,1)S(1)}, bf16[32,1024]{1,0:T(8,128)(2,1)S(1)}, u32[]{:S(2)}, u32[]{:S(2)}) collective-permute-start(bf16[32,1024]{1,0:T(8,128)(2,1)S(1)} %get-tuple-element.24), channel_id=1, source_target_pairs={{0,1},{1,2},{2,3},{3,0},{4,5},{5,6},{6,7},{7,4},{8,9},{9,10},{10,1... | collective-permute-start | bytes 196616 | tf_op jit(solution)/shard_map/ppermute | solution.py:380
  25.6 7.7 %collective-permute-start.8 = (bf16[32,1024]{1,0:T(8,128)(2,1)S(1)}, bf16[32,1024]{1,0:T(8,128)(2,1)S(1)}, u32[]{:S(2)}, u32[]{:S(2)}) collective-permute-start(bf16[32,1024]{1,0:T(8,128)(2,1)S(1)} %get-tuple-element.25), channel_id=1, source_target_pairs={{0,2},{1,3},{2,0},{3,1},{4,6},{5,7},{6,4},{7,5},{8,10},{9,11},{10,... | collective-permute-start | bytes 196616 | tf_op jit(solution)/shard_map/ppermute | solution.py:380
  28.2 5.3 %collective-permute-start.9 = (bf16[32,1024]{1,0:T(8,128)(2,1)S(1)}, bf16[32,1024]{1,0:T(8,128)(2,1)S(1)}, u32[]{:S(2)}, u32[]{:S(2)}) collective-permute-start(bf16[32,1024]{1,0:T(8,128)(2,1)S(1)} %get-tuple-element.26), channel_id=1, source_target_pairs={{0,3},{1,0},{2,1},{3,2},{4,7},{5,4},{6,5},{7,6},{8,11},{9,8},{10,9... | collective-permute-start | bytes 196616 | tf_op jit(solution)/shard_map/ppermute | solution.py:380
  31.0 3.7 %copy-start = (f32[64,32,1024]{2,1,0:T(8,128)}, f32[64,32,1024]{2,1,0:T(8,128)S(1)}, u32[]{:S(2)}) copy-start(f32[64,32,1024]{2,1,0:T(8,128)S(1)} %get-tuple-element.30.refs_5_.refs_1_.active_ref) | copy-start | bytes 25165828
  34.6 2.4 %collective-permute-start.10 = (f32[512,128]{1,0:T(8,128)S(1)}, f32[512,128]{1,0:T(8,128)S(1)}, u32[]{:S(2)}, u32[]{:S(2)}) collective-permute-start(f32[512,128]{1,0:T(8,128)S(1)} %get-tuple-element.38), channel_id=1, source_target_pairs={{0,4},{4,0},{8,12},{12,8},{16,20},{20,16},{24,28},{28,24},{1,5},{5... | collective-permute-start | bytes 786440 | tf_op jit(solution)/shard_map/ppermute | solution.py:374
  35.6 1.4 %copy-start.2 = (bf16[2048,512]{1,0:T(8,128)(2,1)}, bf16[2048,512]{1,0:T(8,128)(2,1)S(1)}, u32[]{:S(2)}) copy-start(bf16[2048,512]{1,0:T(8,128)(2,1)S(1)} %get-tuple-element.32.even_ref) | copy-start | bytes 6291460
  37.7 13.3 %all-to-all-start = ((bf16[16,32,128]{2,1,0:T(8,128)(2,1)}), bf16[16,32,128]{2,1,0:T(8,128)(2,1)S(1)}, u32[]{:S(2)}, u32[]{:S(2)}) async-start(bf16[16,32,128]{2,1,0:T(8,128)(2,1)} %bitcast.2), calls=%async_computation | async-start | bytes 262144 | tf_op jit(solution)/shard_map/all_to_all | solution.py:423
  42.7 3.4 %copy-start.1 = (f32[64,32,1024]{2,1,0:T(8,128)S(1)}, f32[64,32,1024]{2,1,0:T(8,128)}, u32[]{:S(2)}) copy-start(f32[64,32,1024]{2,1,0:T(8,128)} %copy-done) | copy-start | bytes 25165828
  46.1 1.6 %copy-start.3 = (bf16[2048,512]{1,0:T(8,128)(2,1)S(1)}, bf16[2048,512]{1,0:T(8,128)(2,1)}, u32[]{:S(2)}) copy-start(bf16[2048,512]{1,0:T(8,128)(2,1)} %copy-done.2) | copy-start | bytes 6291460

commit v5 on v4

--- a/solution.py
+++ b/solution.py
@@ -14,6 +14,7 @@
 WIDE = 2 * LANES
 PAD = LANES - KDIM % LANES
 LOG2E = 1.0 / math.log(2.0)
+QUERY_COPIES = 8
 HBM = pl.BlockSpec(memory_space=pltpu.HBM)
 VMEM = pl.BlockSpec(memory_space=pltpu.VMEM)
 
@@ -22,12 +23,12 @@
     return jax.ShapeDtypeStruct(dims, kind)
 
 
-def call(body, out_shape, args, specs=None, scratch=(), flops=0, limit=20):
+def call(body, out_shape, args, specs=None, out_specs=None, scratch=(), flops=0, limit=20):
     return pl.pallas_call(
         body,
         out_shape=out_shape,
         in_specs=specs or [VMEM] * len(args),
-        out_specs=jax.tree.map(lambda _: VMEM, out_shape),
+        out_specs=out_specs or jax.tree.map(lambda _: VMEM, out_shape),
         scratch_shapes=list(scratch),
         compiler_params=pltpu.CompilerParams(vmem_limit_bytes=limit << 20),
         cost_estimate=pl.CostEstimate(flops=flops, bytes_accessed=0, transcendentals=0),
@@ -40,7 +41,11 @@
 
 def spread_kernel(factor, query_hbm, norm_hbm, weight_hbm, look_hbm, *refs):
     query_ref, off_ref, scale_ref, low_ref, norm, weight, look, tall, sems = refs
-    pairs = ((norm_hbm, norm), (weight_hbm, weight), (look_hbm, look), (query_hbm, query_ref))
+    pairs = [(norm_hbm, norm), (weight_hbm, weight), (look_hbm, look)]
+    chunk = query_ref.shape[0] // QUERY_COPIES
+    for part in range(QUERY_COPIES):
+        block = pl.ds(part * chunk, chunk)
+        pairs.append((query_hbm.at[block], query_ref.at[block]))
     copies = [pltpu.make_async_copy(*pair, sems.at[place]) for place, pair in enumerate(pairs)]
     for copy in copies:
         copy.start()
@@ -61,7 +66,8 @@
         jnp.broadcast_to(look[...].astype(jnp.float32), (LANES, local_rows))
     )
     low_ref[...] = tall[pl.ds(me * rows, rows), :]
-    copies[3].wait()
+    for copy in copies[3:]:
+        copy.wait()
 
 
 def spread(lat_query, normalizer, weight, lookback, heads, factor):
@@ -75,7 +81,7 @@
         shape_of((rows, LANES), jnp.float32),
     )
     scratch = [pltpu.VMEM(value.shape, value.dtype) for value in (normalizer, weight, look)]
-    scratch += [pltpu.VMEM((local_rows, LANES), jnp.float32), pltpu.SemaphoreType.DMA((4,))]
+    scratch += [pltpu.VMEM((local_rows, LANES), jnp.float32), pltpu.SemaphoreType.DMA((3 + QUERY_COPIES,))]
     return call(
         functools.partial(spread_kernel, factor),
         out,
@@ -130,7 +136,6 @@
         return
     own, sends = outs[0], outs[1:]
     rows = own.shape[0]
-    size = len(sends) + 1
     me = lax.axis_index("head")
     sources = [(ref, tile) for ref in (*prior, acc) for tile in range(ref.shape[0])]
     pieces = [(ref, tile, part) for ref, tile in sources for part in range(per_tile)]
@@ -138,7 +143,7 @@
         lanes = lanes_of(part)
         own[:, lanes_of(place)] = ref[tile, pl.ds(me * rows, rows), lanes]
         for hop, send in enumerate(sends):
-            there = lax.rem(me + hop + 1, size)
+            there = lax.rem(me + hop + 1, lax.axis_size("head"))
             send[:, lanes_of(place)] = ref[tile, pl.ds(there * rows, rows), lanes].astype(send.dtype)
 
 
@@ -252,10 +257,10 @@
 def key_kernel(peers, half, *refs):
     shares, refs = refs[:peers], refs[peers:]
     if peers:
-        predicted_ref, active_ref, scale_ref, query_ref, gap_ref, slopes_ref, out_ref, tall = refs
+        predicted_ref, active_ref, scale_ref, query_ref, gap_ref, out_ref, tall = refs
         gap_ref[...] = gap_of(shares, predicted_ref[...])
     else:
-        gap_ref, active_ref, scale_ref, query_ref, slopes_ref, out_ref, tall = refs
+        gap_ref, active_ref, scale_ref, query_ref, out_ref, tall = refs
     index_heads, rows, _ = active_ref.shape
     dims, columns = tall.shape
     lanes = slice(half * columns, (half + 1) * columns)
@@ -272,8 +277,6 @@
             slope = jnp.where(active_ref[place, :, lanes] > 0.0, scaled, 0.0)
             slopes.append(slope if rows % 16 else slope.astype(jnp.bfloat16))
         slopes = jnp.concatenate(slopes, axis=0).astype(jnp.bfloat16)
-        block = pl.ds(pl.multiple_of(step * (group * rows), group * rows), group * rows)
-        slopes_ref[block, :] = slopes
         begin = pl.multiple_of(step * (group * dims), LANES)
         stacked = stack_heads(query_ref[:, pl.ds(begin, group * dims)], group, dims)
         tall[...] += lax.dot_general(
@@ -287,10 +290,7 @@
 def key_terms(shares, gap, predicted, active, scales, index_query, dims, half):
     index_heads, rows, seq_total = active.shape
     columns = seq_total // 2
-    out = (
-        shape_of((index_heads * rows, columns), jnp.bfloat16),
-        shape_of((columns, dims), jnp.float32),
-    )
+    out = (shape_of((columns, dims), jnp.float32),)
     if shares:
         out = (shape_of((rows, seq_total), jnp.float32), *out)
         args = (*shares, predicted)
@@ -305,47 +305,82 @@
     )
 
 
-def query_kernel(factor, gap_ref, even_ref, odd_ref, active_ref, keys_ref, grad_query_ref, grad_weight_ref, sums):
-    index_heads, rows, seq_total = active_ref.shape
-    dims = keys_ref.shape[1]
-    group = min(64, index_heads)
+def query_kernel(pieces, factor, query_hbm, keys_hbm, gap_hbm, weight_hbm, *refs):
+    grad_query_hbm, grad_weight_ref, query, keys, gap, weight, slopes, grads, scales, sems = refs
+    pairs = ((query_hbm, query), (keys_hbm, keys), (weight_hbm, weight), (gap_hbm, gap))
+    copies = [pltpu.make_async_copy(*pair, sems.at[place]) for place, pair in enumerate(pairs)]
+    for copy in copies:
+        copy.start()
+    for copy in copies:
+        copy.wait()
+    rows, index_heads = weight.shape
+    seq_total, dims = keys.shape
+    heads = index_heads // pieces
     lane = lax.broadcasted_iota(jnp.int32, (rows, LANES), 1)
-    sums[...] = jnp.zeros_like(sums)
-
-    @pl.loop(0, index_heads // group)
-    def _(step):
-        gap = gap_ref[...]
-        total = sums[...]
-        for head in range(group):
-            product = active_ref[step * group + head] * gap
-            partial = functools.reduce(
-                jnp.add, [product[:, lanes_of(place)] for place in range(seq_total // LANES)]
+    sums = jnp.zeros((rows, LANES), jnp.float32)
+    weights = weight[...] * factor
+    for head in range(index_heads):
+        scales[head] = jnp.broadcast_to(weights[:, head : head + 1], (rows, LANES))
+    copies = []
+    for piece in range(pieces):
+        lanes = slice(piece * heads * dims, (piece + 1) * heads * dims)
+        stacked = stack_heads(query[:, lanes], heads, dims)
+        partial = [jnp.zeros((rows, LANES), jnp.float32)] * heads
+        for begin in range(0, seq_total, WIDE):
+            inner = lax.dot_general(
+                stacked,
+                keys[begin : begin + WIDE],
+                (((1,), (1,)), ((), ())),
+                preferred_element_type=jnp.float32,
             )
-            partial = jnp.sum(partial, axis=1, keepdims=True)
-            total = jnp.where(lane == step * group + head, partial, total)
-        sums[...] = total
-        block = pl.ds(pl.multiple_of(step * (group * rows), group * rows), group * rows)
-        slopes = jnp.concatenate([even_ref[block, :], odd_ref[block, :]], axis=1)
-        grad = jnp.dot(slopes, keys_ref[...], preferred_element_type=jnp.float32)
-        for head in range(group):
-            begin = pl.multiple_of((step * group + head) * dims, dims)
-            grad_query_ref[:, pl.ds(begin, dims)] = grad[head * rows : (head + 1) * rows]
-
+            part = gap[:, begin : begin + WIDE]
+            for head in range(heads):
+                place = piece * heads + head
+                active = jnp.maximum(inner[head * rows : (head + 1) * rows], 0.0)
+                product = active * part
+                partial[head] = partial[head] + (product[:, :LANES] + product[:, LANES:])
+                scaled = part * jnp.concatenate([scales[place]] * 2, axis=1)
+                slope = jnp.where(active > 0.0, scaled, 0.0)
+                slopes[head * rows : (head + 1) * rows, begin : begin + WIDE] = slope.astype(slopes.dtype)
+        grad = jnp.dot(slopes[...].astype(keys.dtype), keys[...], preferred_element_type=jnp.float32)
+        for head in range(heads):
+            begin = (piece * heads + head) * dims
+            grads[:, begin : begin + dims] = grad[head * rows : (head + 1) * rows]
+            total = jnp.sum(partial[head], axis=1, keepdims=True)
+            sums = jnp.where(lane == piece * heads + head, total, sums)
+        lanes = pl.ds(piece * heads * dims, heads * dims)
+        copy = pltpu.make_async_copy(grads.at[:, lanes], grad_query_hbm.at[:, lanes], sems.at[4 + piece])
+        copy.start()
+        copies.append(copy)
     grad_weight_ref[...] = sums[:, :index_heads] * factor
-
-
-def query_grads(gap, even, odd, active, keys, factor):
-    index_heads, rows, seq_total = active.shape
-    dims = keys.shape[1]
+    for copy in copies:
+        copy.wait()
+
+
+def query_grads(index_query, keys, gap, weight, factor):
+    rows, index_heads = weight.shape
+    seq_total, dims = keys.shape
+    pieces = 2
+    args = (index_query, keys, gap, weight)
+    kind = jnp.float32 if rows % 16 else jnp.bfloat16
+    scratch = [pltpu.VMEM(value.shape, value.dtype) for value in args]
+    scratch += [
+        pltpu.VMEM((index_heads // pieces * rows, seq_total), kind),
+        pltpu.VMEM((rows, index_heads * dims), jnp.float32),
+        pltpu.VMEM((index_heads, rows, LANES), jnp.float32),
+        pltpu.SemaphoreType.DMA((4 + pieces,)),
+    ]
     return call(
-        functools.partial(query_kernel, factor),
+        functools.partial(query_kernel, pieces, factor),
         (
             shape_of((rows, index_heads * dims), jnp.float32),
             shape_of((rows, index_heads), jnp.float32),
         ),
-        (gap, even, odd, active, keys),
-        scratch=[pltpu.VMEM((rows, LANES), jnp.float32)],
-        flops=6 * rows * index_heads * seq_total * dims,
+        tuple(pltpu.with_memory_space_constraint(value, pltpu.HBM) for value in args),
+        specs=[HBM] * 4,
+        out_specs=(HBM, VMEM),
+        scratch=scratch,
+        flops=8 * rows * index_heads * seq_total * dims,
     )
 
 
@@ -373,10 +408,10 @@
     def swap(value, bits):
         return lax.ppermute(value, "seq", [(place, place ^ bits) for place in range(seq_count)])
 
-    def pass_on(values):
+    def pass_on(values, pair):
         out = []
         for hop, value in enumerate(values):
-            to = [(place, (place + hop + 1) % peers) for place in range(peers)]
+            to = [(place, pair(place, hop + 1)) for place in range(peers)]
             out.append(lax.ppermute(value, "head", to))
         return out
 
@@ -386,7 +421,7 @@
         blocks[bits] = swap(mine, bits)
     for bits in range(0, seq_count, 2):
         blocks[bits + 1] = swap(blocks[bits], 1)
-    phases = [[0, 1], [2, 3], [*range(4, seq_count, 2)], [*range(5, seq_count, 2)]]
+    phases = [[0, 1], [2, 4], [3, 5], [*range(6, seq_count)]]
     order = [*range(0, seq_count, 2), *range(1, seq_count, 2)]
 
     query, offsets, scales, lows = spread(
@@ -406,16 +441,16 @@
         )
         prior.append(mass)
     own, *sends = mass
-    shares = [own, *pass_on(sends)]
+    shares = [own, *pass_on(sends, lambda place, hop: (place + hop) % peers)]
     active, predicted, keys = index_scores(
         index_query, scales, lows, [blocks[slot] for slot in order], order, dims
     )
     terms = functools.partial(
         key_terms, active=active, scales=scales, index_query=index_query, dims=dims
     )
-    gap, odd, give = terms(shares, None, predicted, half=1)
+    gap, give = terms(shares, None, predicted, half=1)
     come = swap(give, 1)
-    even, keep = terms([], gap, None, half=0)
+    (keep,) = terms([], gap, None, half=0)
     members = [
         [seq * peers + head for seq in range(core, seq_count, 2) for head in range(peers)]
         for core in range(2)
@@ -423,7 +458,7 @@
     arrived = lax.all_to_all(
         fold(keep, come), ("seq", "head"), 0, 0, tiled=True, axis_index_groups=members
     )
-    grad_query, grad_weight = query_grads(gap, even, odd, active, keys, factor)
+    grad_query, grad_weight = query_grads(index_query, keys, gap, index_weight, factor)
     grad_key = jnp.sum(arrived.reshape(-1, rows, dims).astype(jnp.float32), axis=0)
     return grad_query, grad_weight, grad_key
 

time: 52 us -> 49.9 us (0.960)
  local copies, waits for them, and re-layouts: 6.36 us -> 0.71 us
  Pallas kernels: 17.2 us -> 19.4 us
  starting transfers between devices: 15.3 us -> 16.3 us
    unnamed x10 -> x6, local copies, waits for them, and re-layouts: 6.36 us -> 0.71 us
    pallas_call x10, Pallas kernels: 17.2 us -> 19.4 us  [call(): pl.pallas_call(body, out_shape=out_shape, in_specs=specs or [VMEM] * len(...]
    all_to_all x1, waiting for transfers between devices: 0.88 us -> 3.08 us  [per_device(): lax.all_to_all(fold(keep, come), ('seq', 'head'), 0, 0, tiled=True, axis_...]
    ppermute x3, waiting for transfers between devices: 2.48 us -> 1.39 us  [pass_on(): out.append(lax.ppermute(value, 'head', to))]
    ppermute x8, waiting for transfers between devices: 7.09 us -> 6.38 us  [swap(): lax.ppermute(value, 'seq', [(place, place ^ bits) for place in range(seq_...]
    all_to_all x1, starting transfers between devices: 5.03 us -> 5.61 us  [per_device(): lax.all_to_all(fold(keep, come), ('seq', 'head'), 0, 0, tiled=True, axis_...]
  transfers between devices with their start and end apart: 12 -> 12, of which waited for: 6 -> 7; matrix products, arithmetic and copies ran while one was open for 0% -> 0% of each run, Pallas kernels for 26% -> 32%
where the time goes in v5:
time: 49.9 us; the launch traced here: 49.7 us
  Pallas kernels  19.4 us (39%)
  starting transfers between devices  16.3 us (33%)
  waiting for transfers between devices  10.9 us (22%)
  other arithmetic  1.57 us (3%)
  between operations  0.79 us (2%)
  local copies, waits for them, and re-layouts  0.71 us (1%)
    pallas_call x10, Pallas kernels, call(): pl.pallas_call(body, out_shape=out_shape, in_specs=specs or [VMEM] * len(...  19.4 us
    ppermute x8, waiting for transfers between devices, swap(): lax.ppermute(value, 'seq', [(place, place ^ bits) for place in range(seq_...  6.38 us
    ppermute x3, starting transfers between devices, pass_on(): out.append(lax.ppermute(value, 'head', to))  5.75 us
    all_to_all x1, starting transfers between devices, per_device(): lax.all_to_all(fold(keep, come), ('seq', 'head'), 0, 0, tiled=True, axis_...  5.61 us
    ppermute x8, starting transfers between devices, swap(): lax.ppermute(value, 'seq', [(place, place ^ bits) for place in range(seq_...  4.94 us
    all_to_all x1, waiting for transfers between devices, per_device(): lax.all_to_all(fold(keep, come), ('seq', 'head'), 0, 0, tiled=True, axis_...  3.08 us
    ppermute x3, waiting for transfers between devices, pass_on(): out.append(lax.ppermute(value, 'head', to))  1.39 us
  transfers between devices with their start and end apart: 12, of which 7 were waited for; matrix products, arithmetic and copies ran while one was open for 0% of the time, Pallas kernels for 32%

profile of v5, /device:TPU:0, one launch (start us, length us, event | category | flops | bytes accessed | tf_op | source)
XLA Modules:
  0.0 49.7 jit_solution(11886023152814513441)
XLA Ops:
  0.6 0.9 %pad_maximum_fusion.refs_0_ = bf16[704,128]{1,0:T(8,128)(2,1)S(1)} fusion(bf16[128,128]{1,0:T(8,128)(2,1)} %param.12, bf16[576,128]{1,0:T(8,128)(2,1)} %bitcast.3), kind=kLoop, calls=%fused_computation.1 | loop fusion | flops 360448 | bytes 360448 | tf_op jit(solution)/shard_map/concatenate | solution.py:418
  1.6 4.0 %collective-permute-start.2 = (bf16[704,128]{1,0:T(8,128)(2,1)S(1)}, bf16[704,128]{1,0:T(8,128)(2,1)S(1)}, u32[]{:S(2)}, u32[]{:S(2)}) collective-permute-start(bf16[704,128]{1,0:T(8,128)(2,1)S(1)} %pad_maximum_fusion.refs_0_), channel_id=1, source_target_pairs={{0,24},{4,28},{8,16},{12,20},{16,8},{20,12},{24,0},{28,4},{1,25},{... | collective-permute-start | bytes 540680 | tf_op jit(solution)/shard_map/ppermute | solution.py:409
  5.6 0.5 %collective-permute-start.1 = (bf16[704,128]{1,0:T(8,128)(2,1)S(1)}, bf16[704,128]{1,0:T(8,128)(2,1)S(1)}, u32[]{:S(2)}, u32[]{:S(2)}) collective-permute-start(bf16[704,128]{1,0:T(8,128)(2,1)S(1)} %pad_maximum_fusion.refs_0_), channel_id=1, source_target_pairs={{0,16},{4,20},{8,24},{12,28},{16,0},{20,4},{24,8},{28,12},{1,17},{... | collective-permute-start | bytes 540680 | tf_op jit(solution)/shard_map/ppermute | solution.py:409
  6.1 0.1 collective-permute-start
  6.2 0.0 collective-permute-start.3
  6.2 2.5 %shard_map.94 = (bf16[128,18432]{1,0:T(8,128)(2,1)S(1)}, f32[32,128,128]{2,1,0:T(8,128)S(1)}, f32[64,32,128]{2,1,0:T(8,128)S(1)}, f32[32,128]{1,0:T(8,128)S(1)}) custom-call(bf16[128,18432]{1,0:T(8,128)(2,1)} %query_hbm.2, f32[128,128]{1,0:T(8,128)} %norm_hbm.1, f32[32,64]{1,0:T(8,128)} %weight_hbm.3, s32[1,128]{1,0:T(1,128)} %bitcast.4), custom_call_target="tpu_custom_call" | custom-call | flops 1500000000 | tf_op jit(solution)/shard_map/pallas_call | solution.py:27
  8.7 2.3 %collective-permute-done.2.refs_3_.refs_0_ = bf16[704,128]{1,0:T(8,128)(2,1)S(1)} collective-permute-done((bf16[704,128]{1,0:T(8,128)(2,1)S(1)}, bf16[704,128]{1,0:T(8,128)(2,1)S(1)}, u32[]{:S(2)}, u32[]{:S(2)}) %collective-permute-start.2) | collective-permute-done | bytes 180256 | tf_op jit(solution)/shard_map/ppermute | solution.py:409
  11.0 0.0 collective-permute-start.6
  11.0 3.0 %collective-permute-done.1.refs_2_.refs_1_ = bf16[704,128]{1,0:T(8,128)(2,1)S(1)} collective-permute-done((bf16[704,128]{1,0:T(8,128)(2,1)S(1)}, bf16[704,128]{1,0:T(8,128)(2,1)S(1)}, u32[]{:S(2)}, u32[]{:S(2)}) %collective-permute-start.1) | collective-permute-done | bytes 180256 | tf_op jit(solution)/shard_map/ppermute | solution.py:409
  14.0 0.0 collective-permute-start.5
  14.0 0.3 collective-permute-done.refs_1_.refs_0_
  14.3 0.2 collective-permute-start.4
  14.5 2.0 %shard_map.97.refs_3_ = f32[1,128,256]{2,1,0:T(8,128)S(1)} custom-call(bf16[128,18432]{1,0:T(8,128)(2,1)S(1)} %get-tuple-element.21.query_ref, f32[32,128,128]{2,1,0:T(8,128)S(1)} %get-tuple-element.22.off_ref, bf16[704,128]{1,0:T(8,128)(2,1)S(1)} %collective-permute-done.refs_1_.refs_0_, bf16[704,128]{1,0:T(8,128)(2,1)S(1)} %collective-permute-done.1.refs_2_.refs_1_), custom_call_target="tpu_custom_call" | custom-call | flops 1207959552 | tf_op jit(solution)/shard_map/pallas_call | solution.py:27
  16.5 0.0 collective-permute-done.3.refs_4_.refs_1_
  16.5 2.0 %shard_map.96.refs_2_ = f32[1,128,256]{2,1,0:T(8,128)S(1)} custom-call(bf16[128,18432]{1,0:T(8,128)(2,1)S(1)} %get-tuple-element.21.query_ref, f32[32,128,128]{2,1,0:T(8,128)S(1)} %get-tuple-element.22.off_ref, bf16[704,128]{1,0:T(8,128)(2,1)S(1)} %pad_maximum_fusion.refs_0_, bf16[704,128]{1,0:T(8,128)(2,1)S(1)} %collective-permute-done.3.refs_4_.refs_1_), custom_call_target="tpu_custom_call" | custom-call | flops 1207959552 | tf_op jit(solution)/shard_map/pallas_call | solution.py:27
  18.6 0.0 collective-permute-done.5.refs_6_.refs_1_
  18.6 0.0 collective-permute-done.4.refs_5_.refs_0_
  18.6 2.0 %shard_map.98.refs_4_ = f32[1,128,256]{2,1,0:T(8,128)S(1)} custom-call(bf16[128,18432]{1,0:T(8,128)(2,1)S(1)} %get-tuple-element.21.query_ref, f32[32,128,128]{2,1,0:T(8,128)S(1)} %get-tuple-element.22.off_ref, bf16[704,128]{1,0:T(8,128)(2,1)S(1)} %collective-permute-done.4.refs_5_.refs_0_, bf16[704,128]{1,0:T(8,128)(2,1)S(1)} %collective-permute-done.5.refs_6_.refs_1_), custom_call_target="tpu_custom_call" | custom-call | flops 1207959552 | tf_op jit(solution)/shard_map/pallas_call | solution.py:27
  20.6 0.0 copy-start
  20.7 0.0 collective-permute-done.6.refs_7_.refs_1_
  20.7 2.1 %shard_map.99 = (f32[32,1024]{1,0:T(8,128)S(1)}, bf16[32,1024]{1,0:T(8,128)(2,1)S(1)}, bf16[32,1024]{1,0:T(8,128)(2,1)S(1)}, bf16[32,1024]{1,0:T(8,128)(2,1)S(1)}) custom-call(bf16[128,18432]{1,0:T(8,128)(2,1)S(1)} %get-tuple-element.21.query_ref, f32[32,128,128]{2,1,0:T(8,128)S(1)} %get-tuple-element.22.off_ref, ...), custom_call_target="tpu_custom_call" | custom-call | flops 1207959552 | tf_op jit(solution)/shard_map/pallas_call | solution.py:27
  22.7 1.8 %collective-permute-start.7 = (bf16[32,1024]{1,0:T(8,128)(2,1)S(1)}, bf16[32,1024]{1,0:T(8,128)(2,1)S(1)}, u32[]{:S(2)}, u32[]{:S(2)}) collective-permute-start(bf16[32,1024]{1,0:T(8,128)(2,1)S(1)} %get-tuple-element.24), channel_id=1, source_target_pairs={{0,1},{1,2},{2,3},{3,0},{4,5},{5,6},{6,7},{7,4},{8,9},{9,10},{10,1... | collective-permute-start | bytes 196616 | tf_op jit(solution)/shard_map/ppermute | solution.py:415
  24.6 2.6 %collective-permute-start.8 = (bf16[32,1024]{1,0:T(8,128)(2,1)S(1)}, bf16[32,1024]{1,0:T(8,128)(2,1)S(1)}, u32[]{:S(2)}, u32[]{:S(2)}) collective-permute-start(bf16[32,1024]{1,0:T(8,128)(2,1)S(1)} %get-tuple-element.25), channel_id=1, source_target_pairs={{0,2},{1,3},{2,0},{3,1},{4,6},{5,7},{6,4},{7,5},{8,10},{9,11},{10,... | collective-permute-start | bytes 196616 | tf_op jit(solution)/shard_map/ppermute | solution.py:415
  27.1 1.3 %collective-permute-start.9 = (bf16[32,1024]{1,0:T(8,128)(2,1)S(1)}, bf16[32,1024]{1,0:T(8,128)(2,1)S(1)}, u32[]{:S(2)}, u32[]{:S(2)}) collective-permute-start(bf16[32,1024]{1,0:T(8,128)(2,1)S(1)} %get-tuple-element.26), channel_id=1, source_target_pairs={{0,3},{1,0},{2,1},{3,2},{4,7},{5,4},{6,5},{7,6},{8,11},{9,8},{10,9... | collective-permute-start | bytes 196616 | tf_op jit(solution)/shard_map/ppermute | solution.py:415
  28.5 0.0 copy-done
  28.5 1.5 %shard_map.95 = (f32[64,32,1024]{2,1,0:T(8,128)S(1)}, f32[32,1024]{1,0:T(8,128)S(1)}, bf16[1024,128]{1,0:T(8,128)(2,1)S(1)}) custom-call(bf16[32,8192]{1,0:T(8,128)(2,1)S(1)} %copy-done, f32[64,32,128]{2,1,0:T(8,128)S(1)} %get-tuple-element.18.scale_ref.refs_6_.refs_2_, f32[32,128]{1,0:T(8,128)S(1)} %get-tuple-element.19.low_ref, ...), custom_call_target="tpu_custom_call" | custom-call | flops 1610612736 | tf_op jit(solution)/shard_map/pallas_call | solution.py:27
  30.0 0.0 copy-start.2
  30.0 0.7 %copy-done.2 = bf16[1024,128]{1,0:T(8,128)(2,1)} copy-done((bf16[1024,128]{1,0:T(8,128)(2,1)}, bf16[1024,128]{1,0:T(8,128)(2,1)S(1)}, u32[]{:S(2)}) %copy-start.2) | copy-done | bytes 262168
  30.7 0.0 collective-permute-done.7.refs_1_
  30.7 1.2 %collective-permute-done.8.refs_2_ = bf16[32,1024]{1,0:T(8,128)(2,1)S(1)} collective-permute-done((bf16[32,1024]{1,0:T(8,128)(2,1)S(1)}, bf16[32,1024]{1,0:T(8,128)(2,1)S(1)}, u32[]{:S(2)}, u32[]{:S(2)}) %collective-permute-start.8) | collective-permute-done | bytes 65568 | tf_op jit(solution)/shard_map/ppermute | solution.py:415
  31.8 0.2 collective-permute-done.9.refs_3_
  32.1 0.9 %shard_map.100 = (f32[32,1024]{1,0:T(8,128)S(1)}, f32[512,128]{1,0:T(8,128)S(1)}) custom-call(f32[32,1024]{1,0:T(8,128)S(1)} %get-tuple-element.23.refs_0_, bf16[32,1024]{1,0:T(8,128)(2,1)S(1)} %collective-permute-done.7.refs_1_, bf16[32,1024]{1,0:T(8,128)(2,1)S(1)} %collective-permute-done.8.refs_2_, bf16[32,1024]{1,0:T(8,128)(2,1)S(1)} %collective-permute-done.9.refs_3_, ...), custom_call_target="tpu_custom_call" | custom-call | flops 1073741824 | tf_op jit(solution)/shard_map/pallas_call | solution.py:27
  33.0 0.0 copy-start.1
  33.0 0.1 collective-permute-start.10
  33.1 0.7 %shard_map.102.keep_ref = f32[512,128]{1,0:T(8,128)S(1)} custom-call(f32[32,1024]{1,0:T(8,128)S(1)} %get-tuple-element.29.gap_hbm.refs_0_, f32[64,32,1024]{2,1,0:T(8,128)S(1)} %get-tuple-element.28.refs_5_.refs_1_, f32[64,32,128]{2,1,0:T(8,128)S(1)} %get-tuple-element.18.scale_ref.refs_6_.refs_2_, bf16[32,8192]{1,0:T(8,128)(2,1)S(1)} %copy-done), custom_call_target="tpu_custom_call" | custom-call | flops 1073741824 | tf_op jit(solution)/shard_map/pallas_call | solution.py:27
  33.7 0.0 copy-done.1
  33.8 0.8 %collective-permute-done.10.come_ref = f32[512,128]{1,0:T(8,128)S(1)} collective-permute-done((f32[512,128]{1,0:T(8,128)S(1)}, f32[512,128]{1,0:T(8,128)S(1)}, u32[]{:S(2)}, u32[]{:S(2)}) %collective-permute-start.10) | collective-permute-done | bytes 262176 | tf_op jit(solution)/shard_map/ppermute | solution.py:409
  34.6 0.7 %shard_map.103 = bf16[512,128]{1,0:T(8,128)(2,1)} custom-call(f32[512,128]{1,0:T(8,128)S(1)} %shard_map.102.keep_ref, f32[512,128]{1,0:T(8,128)S(1)} %collective-permute-done.10.come_ref), custom_call_target="tpu_custom_call" | custom-call | flops 10000000 | tf_op jit(solution)/shard_map/pallas_call | solution.py:27
  35.2 5.6 %all-to-all-start = ((bf16[16,32,128]{2,1,0:T(8,128)(2,1)}), bf16[16,32,128]{2,1,0:T(8,128)(2,1)S(1)}, u32[]{:S(2)}, u32[]{:S(2)}) async-start(bf16[16,32,128]{2,1,0:T(8,128)(2,1)} %bitcast.2), calls=%async_computation | async-start | bytes 262144 | tf_op jit(solution)/shard_map/all_to_all | solution.py:458
  40.9 5.1 %shard_map.101 = (f32[32,8192]{1,0:T(8,128)}, f32[32,64]{1,0:T(8,128)}) custom-call(bf16[32,8192]{1,0:T(8,128)(2,1)} %refs_3_.1, bf16[1024,128]{1,0:T(8,128)(2,1)} %copy-done.2, f32[32,1024]{1,0:T(8,128)} %copy-done.1, f32[32,64]{1,0:T(8,128)} %weight_hbm.3), custom_call_target="tpu_custom_call" | custom-call | flops 2147483648 | tf_op jit(solution)/shard_map/pallas_call | solution.py:27
  46.0 3.1 %all-to-all-done = bf16[16,32,128]{2,1,0:T(8,128)(2,1)S(1)} async-done(((bf16[16,32,128]{2,1,0:T(8,128)(2,1)}), bf16[16,32,128]{2,1,0:T(8,128)(2,1)S(1)}, u32[]{:S(2)}, u32[]{:S(2)}) %all-to-all-start) | async-done | bytes 131104 | tf_op jit(solution)/shard_map/all_to_all | solution.py:458
  49.0 0.6 %convert_reduce_fusion = f32[32,128]{1,0:T(8,128)} fusion(bf16[16,32,128]{2,1,0:T(8,128)(2,1)S(1)} %all-to-all-done), kind=kLoop, calls=%fused_computation | loop fusion | flops 126976 | bytes 147456 | tf_op jit(solution)/shard_map/reduce_sum | solution.py:462
Async XLA Ops:
  1.6 9.4 %collective-permute-start.2 = (bf16[704,128]{1,0:T(8,128)(2,1)S(1)}, bf16[704,128]{1,0:T(8,128)(2,1)S(1)}, u32[]{:S(2)}, u32[]{:S(2)}) collective-permute-start(bf16[704,128]{1,0:T(8,128)(2,1)S(1)} %pad_maximum_fusion.refs_0_), channel_id=1, source_target_pairs={{0,24},{4,28},{8,16},{12,20},{16,8},{20,12},{24,0},{28,4},{1,25},{... | collective-permute-start | bytes 540680 | tf_op jit(solution)/shard_map/ppermute | solution.py:409
  5.6 8.4 %collective-permute-start.1 = (bf16[704,128]{1,0:T(8,128)(2,1)S(1)}, bf16[704,128]{1,0:T(8,128)(2,1)S(1)}, u32[]{:S(2)}, u32[]{:S(2)}) collective-permute-start(bf16[704,128]{1,0:T(8,128)(2,1)S(1)} %pad_maximum_fusion.refs_0_), channel_id=1, source_target_pairs={{0,16},{4,20},{8,24},{12,28},{16,0},{20,4},{24,8},{28,12},{1,17},{... | collective-permute-start | bytes 540680 | tf_op jit(solution)/shard_map/ppermute | solution.py:409
  6.1 8.2 %collective-permute-start = (bf16[704,128]{1,0:T(8,128)(2,1)S(1)}, bf16[704,128]{1,0:T(8,128)(2,1)S(1)}, u32[]{:S(2)}, u32[]{:S(2)}) collective-permute-start(bf16[704,128]{1,0:T(8,128)(2,1)S(1)} %pad_maximum_fusion.refs_0_), channel_id=1, source_target_pairs={{0,8},{4,12},{8,0},{12,4},{16,24},{20,28},{24,16},{28,20},{1,9},{5... | collective-permute-start | bytes 540680 | tf_op jit(solution)/shard_map/ppermute | solution.py:409
  6.2 10.3 %collective-permute-start.3 = (bf16[704,128]{1,0:T(8,128)(2,1)S(1)}, bf16[704,128]{1,0:T(8,128)(2,1)S(1)}, u32[]{:S(2)}, u32[]{:S(2)}) collective-permute-start(bf16[704,128]{1,0:T(8,128)(2,1)S(1)} %pad_maximum_fusion.refs_0_), channel_id=1, source_target_pairs={{0,4},{4,0},{8,12},{12,8},{16,20},{20,16},{24,28},{28,24},{1,5},{5... | collective-permute-start | bytes 540680 | tf_op jit(solution)/shard_map/ppermute | solution.py:409
  11.0 9.7 %collective-permute-start.6 = (bf16[704,128]{1,0:T(8,128)(2,1)S(1)}, bf16[704,128]{1,0:T(8,128)(2,1)S(1)}, u32[]{:S(2)}, u32[]{:S(2)}) collective-permute-start(bf16[704,128]{1,0:T(8,128)(2,1)S(1)} %collective-permute-done.2.refs_3_.refs_0_), channel_id=1, source_target_pairs={{0,4},{4,0},{8,12},{12,8},{16,20},{20,16},{24,28},{28,24},{1,5},{5... | collective-permute-start | bytes 540680 | tf_op jit(solution)/shard_map/ppermute | solution.py:409
  14.0 4.6 %collective-permute-start.5 = (bf16[704,128]{1,0:T(8,128)(2,1)S(1)}, bf16[704,128]{1,0:T(8,128)(2,1)S(1)}, u32[]{:S(2)}, u32[]{:S(2)}) collective-permute-start(bf16[704,128]{1,0:T(8,128)(2,1)S(1)} %collective-permute-done.1.refs_2_.refs_1_), channel_id=1, source_target_pairs={{0,4},{4,0},{8,12},{12,8},{16,20},{20,16},{24,28},{28,24},{1,5},{5... | collective-permute-start | bytes 540680 | tf_op jit(solution)/shard_map/ppermute | solution.py:409
  14.3 4.3 %collective-permute-start.4 = (bf16[704,128]{1,0:T(8,128)(2,1)S(1)}, bf16[704,128]{1,0:T(8,128)(2,1)S(1)}, u32[]{:S(2)}, u32[]{:S(2)}) collective-permute-start(bf16[704,128]{1,0:T(8,128)(2,1)S(1)} %collective-permute-done.refs_1_.refs_0_), channel_id=1, source_target_pairs={{0,4},{4,0},{8,12},{12,8},{16,20},{20,16},{24,28},{28,24},{1,5},{5... | collective-permute-start | bytes 540680 | tf_op jit(solution)/shard_map/ppermute | solution.py:409
  20.6 7.9 %copy-start = (bf16[32,8192]{1,0:T(8,128)(2,1)S(1)}, bf16[32,8192]{1,0:T(8,128)(2,1)}, u32[]{:S(2)}) copy-start(bf16[32,8192]{1,0:T(8,128)(2,1)} %refs_3_.1) | copy-start | bytes 1572868
  22.7 8.0 %collective-permute-start.7 = (bf16[32,1024]{1,0:T(8,128)(2,1)S(1)}, bf16[32,1024]{1,0:T(8,128)(2,1)S(1)}, u32[]{:S(2)}, u32[]{:S(2)}) collective-permute-start(bf16[32,1024]{1,0:T(8,128)(2,1)S(1)} %get-tuple-element.24), channel_id=1, source_target_pairs={{0,1},{1,2},{2,3},{3,0},{4,5},{5,6},{6,7},{7,4},{8,9},{9,10},{10,1... | collective-permute-start | bytes 196616 | tf_op jit(solution)/shard_map/ppermute | solution.py:415
  24.6 7.3 %collective-permute-start.8 = (bf16[32,1024]{1,0:T(8,128)(2,1)S(1)}, bf16[32,1024]{1,0:T(8,128)(2,1)S(1)}, u32[]{:S(2)}, u32[]{:S(2)}) collective-permute-start(bf16[32,1024]{1,0:T(8,128)(2,1)S(1)} %get-tuple-element.25), channel_id=1, source_target_pairs={{0,2},{1,3},{2,0},{3,1},{4,6},{5,7},{6,4},{7,5},{8,10},{9,11},{10,... | collective-permute-start | bytes 196616 | tf_op jit(solution)/shard_map/ppermute | solution.py:415
  27.1 4.9 %collective-permute-start.9 = (bf16[32,1024]{1,0:T(8,128)(2,1)S(1)}, bf16[32,1024]{1,0:T(8,128)(2,1)S(1)}, u32[]{:S(2)}, u32[]{:S(2)}) collective-permute-start(bf16[32,1024]{1,0:T(8,128)(2,1)S(1)} %get-tuple-element.26), channel_id=1, source_target_pairs={{0,3},{1,0},{2,1},{3,2},{4,7},{5,4},{6,5},{7,6},{8,11},{9,8},{10,9... | collective-permute-start | bytes 196616 | tf_op jit(solution)/shard_map/ppermute | solution.py:415
  30.0 0.7 %copy-start.2 = (bf16[1024,128]{1,0:T(8,128)(2,1)}, bf16[1024,128]{1,0:T(8,128)(2,1)S(1)}, u32[]{:S(2)}) copy-start(bf16[1024,128]{1,0:T(8,128)(2,1)S(1)} %get-tuple-element.20.keys_hbm) | copy-start | bytes 786436
  33.0 0.8 %copy-start.1 = (f32[32,1024]{1,0:T(8,128)}, f32[32,1024]{1,0:T(8,128)S(1)}, u32[]{:S(2)}) copy-start(f32[32,1024]{1,0:T(8,128)S(1)} %get-tuple-element.29.gap_hbm.refs_0_) | copy-start | bytes 393220
  33.0 1.6 %collective-permute-start.10 = (f32[512,128]{1,0:T(8,128)S(1)}, f32[512,128]{1,0:T(8,128)S(1)}, u32[]{:S(2)}, u32[]{:S(2)}) collective-permute-start(f32[512,128]{1,0:T(8,128)S(1)} %get-tuple-element.32), channel_id=1, source_target_pairs={{0,4},{4,0},{8,12},{12,8},{16,20},{20,16},{24,28},{28,24},{1,5},{5... | collective-permute-start | bytes 786440 | tf_op jit(solution)/shard_map/ppermute | solution.py:409
  35.2 13.8 %all-to-all-start = ((bf16[16,32,128]{2,1,0:T(8,128)(2,1)}), bf16[16,32,128]{2,1,0:T(8,128)(2,1)S(1)}, u32[]{:S(2)}, u32[]{:S(2)}) async-start(bf16[16,32,128]{2,1,0:T(8,128)(2,1)} %bitcast.2), calls=%async_computation | async-start | bytes 262144 | tf_op jit(solution)/shard_map/all_to_all | solution.py:458

commit v6 on v5

--- a/solution.py
+++ b/solution.py
@@ -98,7 +98,7 @@
     outs, (keys, acc) = refs[:-2], refs[-2:]
     tiles, local_rows, wide = acc.shape
     heads = off_ref.shape[0]
-    group = min(32, heads)
+    group = min(8, heads)
     depth = KDIM + PAD
     per_tile = wide // LANES
     for tile in range(tiles):
@@ -106,30 +106,25 @@
         keys[tile, PAD + KDIM :] = jnp.zeros((PAD, wide), keys.dtype)
         for part in range(per_tile):
             keys[tile, PAD : PAD + KDIM, lanes_of(part)] = blocks[tile * per_tile + part][:KDIM]
-    acc[...] = jnp.zeros_like(acc)
     scale = KDIM ** (-0.5) * LOG2E
 
-    @pl.loop(0, heads // group)
-    def _(step):
-        @pl.loop(0, tiles)
-        def _(tile):
-            total = acc[tile]
+    for tile in range(tiles):
+        total = jnp.zeros((local_rows, wide), jnp.float32)
+        for step in range(heads // group):
             for odd in range(2):
-                picked = []
-                for head in range(odd, group, 2):
-                    begin = step * (group * KDIM) + (head * KDIM - (PAD if odd else 0))
-                    picked.append(query_ref[:, pl.ds(pl.multiple_of(begin, LANES), depth)])
+                mine = [step * group + head for head in range(odd, group, 2)]
+                starts = [head * KDIM - (PAD if odd else 0) for head in mine]
                 first = 0 if odd else PAD
                 scores = jnp.dot(
-                    jnp.concatenate(picked, axis=0),
+                    jnp.concatenate([query_ref[:, at : at + depth] for at in starts], axis=0),
                     keys[tile, first : first + depth],
                     preferred_element_type=jnp.float32,
                 )
-                for place, head in enumerate(range(odd, group, 2)):
-                    offset = jnp.concatenate([off_ref[step * group + head]] * per_tile, axis=1)
+                for place, head in enumerate(mine):
+                    offset = jnp.concatenate([off_ref[head]] * per_tile, axis=1)
                     part = scores[place * local_rows : (place + 1) * local_rows]
                     total = total + jnp.exp2(part * scale - offset)
-            acc[tile] = total
+        acc[tile] = total
 
     if not places:
         outs[0][...] = acc[...]
@@ -284,13 +279,13 @@
         )
 
     for place in range(columns // LANES):
-        out_ref[lanes_of(place)] = jnp.transpose(tall[:, lanes_of(place)])
+        out_ref[lanes_of(place)] = jnp.transpose(tall[:, lanes_of(place)]).astype(out_ref.dtype)
 
 
 def key_terms(shares, gap, predicted, active, scales, index_query, dims, half):
     index_heads, rows, seq_total = active.shape
     columns = seq_total // 2
-    out = (shape_of((columns, dims), jnp.float32),)
+    out = (shape_of((columns, dims), jnp.bfloat16 if half else jnp.float32),)
     if shares:
         out = (shape_of((rows, seq_total), jnp.float32), *out)
         args = (*shares, predicted)
@@ -388,7 +383,7 @@
     place = lax.axis_index("seq") // 2
     for chip in range(out_ref.shape[0] // LANES):
         begin = pl.multiple_of(jnp.bitwise_xor(place, chip) * LANES, LANES)
-        total = keep_ref[lanes_of(chip)] + come_ref[lanes_of(chip)]
+        total = keep_ref[lanes_of(chip)] + come_ref[lanes_of(chip)].astype(jnp.float32)
         out_ref[pl.ds(begin, LANES), :] = total.astype(out_ref.dtype)
 
 

time: 49.9 us -> 48.9 us (0.980)
  local copies, waits for them, and re-layouts: 0.71 us -> 0.01 us
  Pallas kernels: 19.4 us -> 18.7 us
  waiting for transfers between devices: 10.9 us -> 11.4 us
    pallas_call x10, Pallas kernels: 19.4 us -> 18.7 us  [call(): pl.pallas_call(body, out_shape=out_shape, in_specs=specs or [VMEM] * len(...]
    unnamed x6, local copies, waits for them, and re-layouts: 0.71 us -> 0.01 us
    ppermute x3, waiting for transfers between devices: 1.39 us -> 2.08 us  [pass_on(): out.append(lax.ppermute(value, 'head', to))]
where the time goes in v6:
time: 48.9 us; the launch traced here: 48.6 us
  Pallas kernels  18.7 us (38%)
  starting transfers between devices  16.1 us (33%)
  waiting for transfers between devices  11.4 us (23%)
  other arithmetic  1.57 us (3%)
  between operations  0.81 us (2%)
    pallas_call x10, Pallas kernels, call(): pl.pallas_call(body, out_shape=out_shape, in_specs=specs or [VMEM] * len(...  18.7 us
    ppermute x8, waiting for transfers between devices, swap(): lax.ppermute(value, 'seq', [(place, place ^ bits) for place in range(seq_...  6.2 us
    ppermute x3, starting transfers between devices, pass_on(): out.append(lax.ppermute(value, 'head', to))  5.76 us
    all_to_all x1, starting transfers between devices, per_device(): lax.all_to_all(fold(keep, come), ('seq', 'head'), 0, 0, tiled=True, axis_...  5.44 us
    ppermute x8, starting transfers between devices, swap(): lax.ppermute(value, 'seq', [(place, place ^ bits) for place in range(seq_...  4.94 us
    all_to_all x1, waiting for transfers between devices, per_device(): lax.all_to_all(fold(keep, come), ('seq', 'head'), 0, 0, tiled=True, axis_...  3.09 us
    ppermute x3, waiting for transfers between devices, pass_on(): out.append(lax.ppermute(value, 'head', to))  2.08 us
  transfers between devices with their start and end apart: 12, of which 7 were waited for; matrix products, arithmetic and copies ran while one was open for 0% of the time, Pallas kernels for 32%

profile of v6, /device:TPU:0, one launch (start us, length us, event | category | flops | bytes accessed | tf_op | source)
XLA Modules:
  0.0 48.6 jit_solution(10018590872396799722)
XLA Ops:
  0.6 0.9 %pad_maximum_fusion.refs_0_ = bf16[704,128]{1,0:T(8,128)(2,1)S(1)} fusion(bf16[128,128]{1,0:T(8,128)(2,1)} %param.12, bf16[576,128]{1,0:T(8,128)(2,1)} %bitcast.3), kind=kLoop, calls=%fused_computation.1 | loop fusion | flops 360448 | bytes 360448 | tf_op jit(solution)/shard_map/concatenate | solution.py:413
  1.6 4.0 %collective-permute-start.2 = (bf16[704,128]{1,0:T(8,128)(2,1)S(1)}, bf16[704,128]{1,0:T(8,128)(2,1)S(1)}, u32[]{:S(2)}, u32[]{:S(2)}) collective-permute-start(bf16[704,128]{1,0:T(8,128)(2,1)S(1)} %pad_maximum_fusion.refs_0_), channel_id=1, source_target_pairs={{0,24},{4,28},{8,16},{12,20},{16,8},{20,12},{24,0},{28,4},{1,25},{... | collective-permute-start | bytes 540680 | tf_op jit(solution)/shard_map/ppermute | solution.py:404
  5.6 0.5 %collective-permute-start.1 = (bf16[704,128]{1,0:T(8,128)(2,1)S(1)}, bf16[704,128]{1,0:T(8,128)(2,1)S(1)}, u32[]{:S(2)}, u32[]{:S(2)}) collective-permute-start(bf16[704,128]{1,0:T(8,128)(2,1)S(1)} %pad_maximum_fusion.refs_0_), channel_id=1, source_target_pairs={{0,16},{4,20},{8,24},{12,28},{16,0},{20,4},{24,8},{28,12},{1,17},{... | collective-permute-start | bytes 540680 | tf_op jit(solution)/shard_map/ppermute | solution.py:404
  6.1 0.1 collective-permute-start
  6.2 0.0 collective-permute-start.3
  6.2 2.5 %shard_map.94 = (bf16[128,18432]{1,0:T(8,128)(2,1)S(1)}, f32[32,128,128]{2,1,0:T(8,128)S(1)}, f32[64,32,128]{2,1,0:T(8,128)S(1)}, f32[32,128]{1,0:T(8,128)S(1)}) custom-call(bf16[128,18432]{1,0:T(8,128)(2,1)} %query_hbm.2, f32[128,128]{1,0:T(8,128)} %norm_hbm.1, f32[32,64]{1,0:T(8,128)} %weight_hbm.3, s32[1,128]{1,0:T(1,128)} %bitcast.4), custom_call_target="tpu_custom_call" | custom-call | flops 1500000000 | tf_op jit(solution)/shard_map/pallas_call | solution.py:27
  8.7 2.3 %collective-permute-done.2.refs_3_.refs_0_ = bf16[704,128]{1,0:T(8,128)(2,1)S(1)} collective-permute-done((bf16[704,128]{1,0:T(8,128)(2,1)S(1)}, bf16[704,128]{1,0:T(8,128)(2,1)S(1)}, u32[]{:S(2)}, u32[]{:S(2)}) %collective-permute-start.2) | collective-permute-done | bytes 180256 | tf_op jit(solution)/shard_map/ppermute | solution.py:404
  11.0 0.0 collective-permute-start.6
  11.0 3.0 %collective-permute-done.1.refs_2_.refs_1_ = bf16[704,128]{1,0:T(8,128)(2,1)S(1)} collective-permute-done((bf16[704,128]{1,0:T(8,128)(2,1)S(1)}, bf16[704,128]{1,0:T(8,128)(2,1)S(1)}, u32[]{:S(2)}, u32[]{:S(2)}) %collective-permute-start.1) | collective-permute-done | bytes 180256 | tf_op jit(solution)/shard_map/ppermute | solution.py:404
  14.0 0.0 collective-permute-start.5
  14.0 0.3 collective-permute-done.refs_1_.refs_0_
  14.3 0.2 collective-permute-start.4
  14.5 1.9 %shard_map.97.refs_3_ = f32[1,128,256]{2,1,0:T(8,128)S(1)} custom-call(bf16[128,18432]{1,0:T(8,128)(2,1)S(1)} %get-tuple-element.21.query_ref, f32[32,128,128]{2,1,0:T(8,128)S(1)} %get-tuple-element.22.off_ref, bf16[704,128]{1,0:T(8,128)(2,1)S(1)} %collective-permute-done.refs_1_.refs_0_, bf16[704,128]{1,0:T(8,128)(2,1)S(1)} %collective-permute-done.1.refs_2_.refs_1_), custom_call_target="tpu_custom_call" | custom-call | flops 1207959552 | tf_op jit(solution)/shard_map/pallas_call | solution.py:27
  16.4 0.0 collective-permute-done.3.refs_4_.refs_1_
  16.4 1.9 %shard_map.96.refs_2_ = f32[1,128,256]{2,1,0:T(8,128)S(1)} custom-call(bf16[128,18432]{1,0:T(8,128)(2,1)S(1)} %get-tuple-element.21.query_ref, f32[32,128,128]{2,1,0:T(8,128)S(1)} %get-tuple-element.22.off_ref, bf16[704,128]{1,0:T(8,128)(2,1)S(1)} %pad_maximum_fusion.refs_0_, bf16[704,128]{1,0:T(8,128)(2,1)S(1)} %collective-permute-done.3.refs_4_.refs_1_), custom_call_target="tpu_custom_call" | custom-call | flops 1207959552 | tf_op jit(solution)/shard_map/pallas_call | solution.py:27
  18.2 0.0 collective-permute-done.5.refs_6_.refs_1_
  18.3 0.0 collective-permute-done.4.refs_5_.refs_0_
  18.3 1.9 %shard_map.98.refs_4_ = f32[1,128,256]{2,1,0:T(8,128)S(1)} custom-call(bf16[128,18432]{1,0:T(8,128)(2,1)S(1)} %get-tuple-element.21.query_ref, f32[32,128,128]{2,1,0:T(8,128)S(1)} %get-tuple-element.22.off_ref, bf16[704,128]{1,0:T(8,128)(2,1)S(1)} %collective-permute-done.4.refs_5_.refs_0_, bf16[704,128]{1,0:T(8,128)(2,1)S(1)} %collective-permute-done.5.refs_6_.refs_1_), custom_call_target="tpu_custom_call" | custom-call | flops 1207959552 | tf_op jit(solution)/shard_map/pallas_call | solution.py:27
  20.1 0.0 copy-start
  20.1 0.0 collective-permute-done.6.refs_7_.refs_1_
  20.2 1.9 %shard_map.99 = (f32[32,1024]{1,0:T(8,128)S(1)}, bf16[32,1024]{1,0:T(8,128)(2,1)S(1)}, bf16[32,1024]{1,0:T(8,128)(2,1)S(1)}, bf16[32,1024]{1,0:T(8,128)(2,1)S(1)}) custom-call(bf16[128,18432]{1,0:T(8,128)(2,1)S(1)} %get-tuple-element.21.query_ref, f32[32,128,128]{2,1,0:T(8,128)S(1)} %get-tuple-element.22.off_ref, ...), custom_call_target="tpu_custom_call" | custom-call | flops 1207959552 | tf_op jit(solution)/shard_map/pallas_call | solution.py:27
  22.1 1.8 %collective-permute-start.7 = (bf16[32,1024]{1,0:T(8,128)(2,1)S(1)}, bf16[32,1024]{1,0:T(8,128)(2,1)S(1)}, u32[]{:S(2)}, u32[]{:S(2)}) collective-permute-start(bf16[32,1024]{1,0:T(8,128)(2,1)S(1)} %get-tuple-element.24), channel_id=1, source_target_pairs={{0,1},{1,2},{2,3},{3,0},{4,5},{5,6},{6,7},{7,4},{8,9},{9,10},{10,1... | collective-permute-start | bytes 196616 | tf_op jit(solution)/shard_map/ppermute | solution.py:410
  23.9 2.6 %collective-permute-start.8 = (bf16[32,1024]{1,0:T(8,128)(2,1)S(1)}, bf16[32,1024]{1,0:T(8,128)(2,1)S(1)}, u32[]{:S(2)}, u32[]{:S(2)}) collective-permute-start(bf16[32,1024]{1,0:T(8,128)(2,1)S(1)} %get-tuple-element.25), channel_id=1, source_target_pairs={{0,2},{1,3},{2,0},{3,1},{4,6},{5,7},{6,4},{7,5},{8,10},{9,11},{10,... | collective-permute-start | bytes 196616 | tf_op jit(solution)/shard_map/ppermute | solution.py:410
  26.5 1.3 %collective-permute-start.9 = (bf16[32,1024]{1,0:T(8,128)(2,1)S(1)}, bf16[32,1024]{1,0:T(8,128)(2,1)S(1)}, u32[]{:S(2)}, u32[]{:S(2)}) collective-permute-start(bf16[32,1024]{1,0:T(8,128)(2,1)S(1)} %get-tuple-element.26), channel_id=1, source_target_pairs={{0,3},{1,0},{2,1},{3,2},{4,7},{5,4},{6,5},{7,6},{8,11},{9,8},{10,9... | collective-permute-start | bytes 196616 | tf_op jit(solution)/shard_map/ppermute | solution.py:410
  27.8 0.0 copy-done
  27.8 1.5 %shard_map.95 = (f32[64,32,1024]{2,1,0:T(8,128)S(1)}, f32[32,1024]{1,0:T(8,128)S(1)}, bf16[1024,128]{1,0:T(8,128)(2,1)S(1)}) custom-call(bf16[32,8192]{1,0:T(8,128)(2,1)S(1)} %copy-done, f32[64,32,128]{2,1,0:T(8,128)S(1)} %get-tuple-element.18.scale_ref.refs_6_.refs_2_, f32[32,128]{1,0:T(8,128)S(1)} %get-tuple-element.19.low_ref, ...), custom_call_target="tpu_custom_call" | custom-call | flops 1610612736 | tf_op jit(solution)/shard_map/pallas_call | solution.py:27
  29.3 0.0 copy-start.2
  29.3 0.0 collective-permute-done.7.refs_1_
  29.3 1.8 %collective-permute-done.8.refs_2_ = bf16[32,1024]{1,0:T(8,128)(2,1)S(1)} collective-permute-done((bf16[32,1024]{1,0:T(8,128)(2,1)S(1)}, bf16[32,1024]{1,0:T(8,128)(2,1)S(1)}, u32[]{:S(2)}, u32[]{:S(2)}) %collective-permute-start.8) | collective-permute-done | bytes 65568 | tf_op jit(solution)/shard_map/ppermute | solution.py:410
  31.2 0.2 collective-permute-done.9.refs_3_
  31.4 0.8 %shard_map.100 = (f32[32,1024]{1,0:T(8,128)S(1)}, bf16[512,128]{1,0:T(8,128)(2,1)S(1)}) custom-call(f32[32,1024]{1,0:T(8,128)S(1)} %get-tuple-element.23.refs_0_, bf16[32,1024]{1,0:T(8,128)(2,1)S(1)} %collective-permute-done.7.refs_1_, bf16[32,1024]{1,0:T(8,128)(2,1)S(1)} %collective-permute-done.8.refs_2_, ...), custom_call_target="tpu_custom_call" | custom-call | flops 1073741824 | tf_op jit(solution)/shard_map/pallas_call | solution.py:27
  32.3 0.0 copy-done.2
  32.3 0.0 copy-start.1
  32.3 0.1 collective-permute-start.10
  32.4 0.7 %shard_map.102.keep_ref = f32[512,128]{1,0:T(8,128)S(1)} custom-call(f32[32,1024]{1,0:T(8,128)S(1)} %get-tuple-element.29.gap_hbm.refs_0_, f32[64,32,1024]{2,1,0:T(8,128)S(1)} %get-tuple-element.28.refs_5_.refs_1_, f32[64,32,128]{2,1,0:T(8,128)S(1)} %get-tuple-element.18.scale_ref.refs_6_.refs_2_, bf16[32,8192]{1,0:T(8,128)(2,1)S(1)} %copy-done), custom_call_target="tpu_custom_call" | custom-call | flops 1073741824 | tf_op jit(solution)/shard_map/pallas_call | solution.py:27
  33.1 0.0 copy-done.1
  33.1 0.6 %collective-permute-done.10.come_ref = bf16[512,128]{1,0:T(8,128)(2,1)S(1)} collective-permute-done((bf16[512,128]{1,0:T(8,128)(2,1)S(1)}, bf16[512,128]{1,0:T(8,128)(2,1)S(1)}, u32[]{:S(2)}, u32[]{:S(2)}) %collective-permute-start.10) | collective-permute-done | bytes 131104 | tf_op jit(solution)/shard_map/ppermute | solution.py:404
  33.7 0.7 %shard_map.103 = bf16[512,128]{1,0:T(8,128)(2,1)} custom-call(f32[512,128]{1,0:T(8,128)S(1)} %shard_map.102.keep_ref, bf16[512,128]{1,0:T(8,128)(2,1)S(1)} %collective-permute-done.10.come_ref), custom_call_target="tpu_custom_call" | custom-call | flops 10000000 | tf_op jit(solution)/shard_map/pallas_call | solution.py:27
  34.4 5.4 %all-to-all-start = ((bf16[16,32,128]{2,1,0:T(8,128)(2,1)}), bf16[16,32,128]{2,1,0:T(8,128)(2,1)S(1)}, u32[]{:S(2)}, u32[]{:S(2)}) async-start(bf16[16,32,128]{2,1,0:T(8,128)(2,1)} %bitcast.2), calls=%async_computation | async-start | bytes 262144 | tf_op jit(solution)/shard_map/all_to_all | solution.py:453
  39.8 5.1 %shard_map.101 = (f32[32,8192]{1,0:T(8,128)}, f32[32,64]{1,0:T(8,128)}) custom-call(bf16[32,8192]{1,0:T(8,128)(2,1)} %refs_3_.1, bf16[1024,128]{1,0:T(8,128)(2,1)} %copy-done.2, f32[32,1024]{1,0:T(8,128)} %copy-done.1, f32[32,64]{1,0:T(8,128)} %weight_hbm.3), custom_call_target="tpu_custom_call" | custom-call | flops 2147483648 | tf_op jit(solution)/shard_map/pallas_call | solution.py:27
  44.9 3.1 %all-to-all-done = bf16[16,32,128]{2,1,0:T(8,128)(2,1)S(1)} async-done(((bf16[16,32,128]{2,1,0:T(8,128)(2,1)}), bf16[16,32,128]{2,1,0:T(8,128)(2,1)S(1)}, u32[]{:S(2)}, u32[]{:S(2)}) %all-to-all-start) | async-done | bytes 131104 | tf_op jit(solution)/shard_map/all_to_all | solution.py:453
  48.0 0.6 %convert_reduce_fusion = f32[32,128]{1,0:T(8,128)} fusion(bf16[16,32,128]{2,1,0:T(8,128)(2,1)S(1)} %all-to-all-done), kind=kLoop, calls=%fused_computation | loop fusion | flops 126976 | bytes 147456 | tf_op jit(solution)/shard_map/reduce_sum | solution.py:457
Async XLA Ops:
  1.6 9.4 %collective-permute-start.2 = (bf16[704,128]{1,0:T(8,128)(2,1)S(1)}, bf16[704,128]{1,0:T(8,128)(2,1)S(1)}, u32[]{:S(2)}, u32[]{:S(2)}) collective-permute-start(bf16[704,128]{1,0:T(8,128)(2,1)S(1)} %pad_maximum_fusion.refs_0_), channel_id=1, source_target_pairs={{0,24},{4,28},{8,16},{12,20},{16,8},{20,12},{24,0},{28,4},{1,25},{... | collective-permute-start | bytes 540680 | tf_op jit(solution)/shard_map/ppermute | solution.py:404
  5.6 8.4 %collective-permute-start.1 = (bf16[704,128]{1,0:T(8,128)(2,1)S(1)}, bf16[704,128]{1,0:T(8,128)(2,1)S(1)}, u32[]{:S(2)}, u32[]{:S(2)}) collective-permute-start(bf16[704,128]{1,0:T(8,128)(2,1)S(1)} %pad_maximum_fusion.refs_0_), channel_id=1, source_target_pairs={{0,16},{4,20},{8,24},{12,28},{16,0},{20,4},{24,8},{28,12},{1,17},{... | collective-permute-start | bytes 540680 | tf_op jit(solution)/shard_map/ppermute | solution.py:404
  6.1 8.2 %collective-permute-start = (bf16[704,128]{1,0:T(8,128)(2,1)S(1)}, bf16[704,128]{1,0:T(8,128)(2,1)S(1)}, u32[]{:S(2)}, u32[]{:S(2)}) collective-permute-start(bf16[704,128]{1,0:T(8,128)(2,1)S(1)} %pad_maximum_fusion.refs_0_), channel_id=1, source_target_pairs={{0,8},{4,12},{8,0},{12,4},{16,24},{20,28},{24,16},{28,20},{1,9},{5... | collective-permute-start | bytes 540680 | tf_op jit(solution)/shard_map/ppermute | solution.py:404
  6.2 10.2 %collective-permute-start.3 = (bf16[704,128]{1,0:T(8,128)(2,1)S(1)}, bf16[704,128]{1,0:T(8,128)(2,1)S(1)}, u32[]{:S(2)}, u32[]{:S(2)}) collective-permute-start(bf16[704,128]{1,0:T(8,128)(2,1)S(1)} %pad_maximum_fusion.refs_0_), channel_id=1, source_target_pairs={{0,4},{4,0},{8,12},{12,8},{16,20},{20,16},{24,28},{28,24},{1,5},{5... | collective-permute-start | bytes 540680 | tf_op jit(solution)/shard_map/ppermute | solution.py:404
  11.0 9.2 %collective-permute-start.6 = (bf16[704,128]{1,0:T(8,128)(2,1)S(1)}, bf16[704,128]{1,0:T(8,128)(2,1)S(1)}, u32[]{:S(2)}, u32[]{:S(2)}) collective-permute-start(bf16[704,128]{1,0:T(8,128)(2,1)S(1)} %collective-permute-done.2.refs_3_.refs_0_), channel_id=1, source_target_pairs={{0,4},{4,0},{8,12},{12,8},{16,20},{20,16},{24,28},{28,24},{1,5},{5... | collective-permute-start | bytes 540680 | tf_op jit(solution)/shard_map/ppermute | solution.py:404
  14.0 4.3 %collective-permute-start.5 = (bf16[704,128]{1,0:T(8,128)(2,1)S(1)}, bf16[704,128]{1,0:T(8,128)(2,1)S(1)}, u32[]{:S(2)}, u32[]{:S(2)}) collective-permute-start(bf16[704,128]{1,0:T(8,128)(2,1)S(1)} %collective-permute-done.1.refs_2_.refs_1_), channel_id=1, source_target_pairs={{0,4},{4,0},{8,12},{12,8},{16,20},{20,16},{24,28},{28,24},{1,5},{5... | collective-permute-start | bytes 540680 | tf_op jit(solution)/shard_map/ppermute | solution.py:404
  14.3 4.0 %collective-permute-start.4 = (bf16[704,128]{1,0:T(8,128)(2,1)S(1)}, bf16[704,128]{1,0:T(8,128)(2,1)S(1)}, u32[]{:S(2)}, u32[]{:S(2)}) collective-permute-start(bf16[704,128]{1,0:T(8,128)(2,1)S(1)} %collective-permute-done.refs_1_.refs_0_), channel_id=1, source_target_pairs={{0,4},{4,0},{8,12},{12,8},{16,20},{20,16},{24,28},{28,24},{1,5},{5... | collective-permute-start | bytes 540680 | tf_op jit(solution)/shard_map/ppermute | solution.py:404
  20.1 7.7 %copy-start = (bf16[32,8192]{1,0:T(8,128)(2,1)S(1)}, bf16[32,8192]{1,0:T(8,128)(2,1)}, u32[]{:S(2)}) copy-start(bf16[32,8192]{1,0:T(8,128)(2,1)} %refs_3_.1) | copy-start | bytes 1572868
  22.1 7.3 %collective-permute-start.7 = (bf16[32,1024]{1,0:T(8,128)(2,1)S(1)}, bf16[32,1024]{1,0:T(8,128)(2,1)S(1)}, u32[]{:S(2)}, u32[]{:S(2)}) collective-permute-start(bf16[32,1024]{1,0:T(8,128)(2,1)S(1)} %get-tuple-element.24), channel_id=1, source_target_pairs={{0,1},{1,2},{2,3},{3,0},{4,5},{5,6},{6,7},{7,4},{8,9},{9,10},{10,1... | collective-permute-start | bytes 196616 | tf_op jit(solution)/shard_map/ppermute | solution.py:410
  23.9 7.3 %collective-permute-start.8 = (bf16[32,1024]{1,0:T(8,128)(2,1)S(1)}, bf16[32,1024]{1,0:T(8,128)(2,1)S(1)}, u32[]{:S(2)}, u32[]{:S(2)}) collective-permute-start(bf16[32,1024]{1,0:T(8,128)(2,1)S(1)} %get-tuple-element.25), channel_id=1, source_target_pairs={{0,2},{1,3},{2,0},{3,1},{4,6},{5,7},{6,4},{7,5},{8,10},{9,11},{10,... | collective-permute-start | bytes 196616 | tf_op jit(solution)/shard_map/ppermute | solution.py:410
  26.5 4.9 %collective-permute-start.9 = (bf16[32,1024]{1,0:T(8,128)(2,1)S(1)}, bf16[32,1024]{1,0:T(8,128)(2,1)S(1)}, u32[]{:S(2)}, u32[]{:S(2)}) collective-permute-start(bf16[32,1024]{1,0:T(8,128)(2,1)S(1)} %get-tuple-element.26), channel_id=1, source_target_pairs={{0,3},{1,0},{2,1},{3,2},{4,7},{5,4},{6,5},{7,6},{8,11},{9,8},{10,9... | collective-permute-start | bytes 196616 | tf_op jit(solution)/shard_map/ppermute | solution.py:410
  29.3 3.0 %copy-start.2 = (bf16[1024,128]{1,0:T(8,128)(2,1)}, bf16[1024,128]{1,0:T(8,128)(2,1)S(1)}, u32[]{:S(2)}) copy-start(bf16[1024,128]{1,0:T(8,128)(2,1)S(1)} %get-tuple-element.20.keys_hbm) | copy-start | bytes 786436
  32.3 0.8 %copy-start.1 = (f32[32,1024]{1,0:T(8,128)}, f32[32,1024]{1,0:T(8,128)S(1)}, u32[]{:S(2)}) copy-start(f32[32,1024]{1,0:T(8,128)S(1)} %get-tuple-element.29.gap_hbm.refs_0_) | copy-start | bytes 393220
  32.3 1.4 %collective-permute-start.10 = (bf16[512,128]{1,0:T(8,128)(2,1)S(1)}, bf16[512,128]{1,0:T(8,128)(2,1)S(1)}, u32[]{:S(2)}, u32[]{:S(2)}) collective-permute-start(bf16[512,128]{1,0:T(8,128)(2,1)S(1)} %get-tuple-element.32), channel_id=1, source_target_pairs={{0,4},{4,0},{8,12},{12,8},{16,20},{20,16},{24,28},{28,24},{1,5},{5... | collective-permute-start | bytes 393224 | tf_op jit(solution)/shard_map/ppermute | solution.py:404
  34.4 13.6 %all-to-all-start = ((bf16[16,32,128]{2,1,0:T(8,128)(2,1)}), bf16[16,32,128]{2,1,0:T(8,128)(2,1)S(1)}, u32[]{:S(2)}, u32[]{:S(2)}) async-start(bf16[16,32,128]{2,1,0:T(8,128)(2,1)} %bitcast.2), calls=%async_computation | async-start | bytes 262144 | tf_op jit(solution)/shard_map/all_to_all | solution.py:453
